TPU v7x, 32 devices: a whole 2x2x4 slice. The times are simulated.
32 devices in a mesh: shard: 4 (over z), replica: 8 (over y, x, core).
Axes of the slice: x: 2, y: 2, z: 4, core: 2. Of those that a mesh axis runs over, the one named last changes fastest.
Arguments:
- block_in: bfloat16 [4096, 2048], P(('shard', 'replica')), may hold values from -6 to 6
- positions: int32 [4096], P(('shard', 'replica')), may hold values from 0 to 127, as said below
- out_grad: bfloat16 [4096, 2048], P(('shard', 'replica')), may hold values from -6 to 6
- w_qkv: bfloat16 [2048, 6144], P('shard'), may hold values from -0.125 to 0.125
- b_qkv: bfloat16 [6144], P('shard'), may hold values from -4.75 to 4.75
- w_out: bfloat16 [2048, 2048], P('shard'), may hold values from -0.25 to 0.25
- b_out: bfloat16 [2048], P('shard'), may hold values from -3 to 3
- w_up: bfloat16 [2048, 8192], P('shard'), may hold values from -0.125 to 0.125
- b_up: bfloat16 [8192], P('shard'), may hold values from -3 to 3
- w_down: bfloat16 [8192, 2048], P('shard'), may hold values from -0.0625 to 0.0625
- b_down: bfloat16 [2048], P('shard'), may hold values from -3 to 3
- first_gain: bfloat16 [2048], P('shard'), may hold values from 0.5 to 1.5
- first_shift: bfloat16 [2048], P('shard'), may hold values from -3 to 3
- second_gain: bfloat16 [2048], P('shard'), may hold values from 0.5 to 1.5
- second_shift: bfloat16 [2048], P('shard'), may hold values from -3 to 3
Outputs:
- block_out: bfloat16 [4096, 2048], P(('shard', 'replica'))
- in_grad: bfloat16 [4096, 2048], P(('shard', 'replica'))
- grad_w_qkv: float32 [2048, 6144], P('shard')
- grad_b_qkv: float32 [6144], P('shard')
- grad_w_out: float32 [2048, 2048], P('shard')
- grad_b_out: float32 [2048], P('shard')
- grad_w_up: float32 [2048, 8192], P('shard')
- grad_b_up: float32 [8192], P('shard')
- grad_w_down: float32 [8192, 2048], P('shard')
- grad_b_down: float32 [2048], P('shard')
- grad_first_gain: float32 [2048], P('shard')
- grad_first_shift: float32 [2048], P('shard')
- grad_second_gain: float32 [2048], P('shard')
- grad_second_shift: float32 [2048], P('shard')
Inputs may be any that keep to these rules, and one draw needn't show every extreme that they name: `positions`: each device's 128 tokens hold whole sequences: a position is 0 at a sequence's start and at each device's first token and otherwise one more than the position before; some device holds one sequence of 128 tokens.
All inputs are finite; a program needn't handle non-finite values.
Results may differ from a plain program's by a relative error of at most 0.006.
The roundings to bfloat16 on the way count: a program that leaves them out, or rounds other values in their place, can miss the bound.
Values may be sent and summed in bfloat16 or wider, within the bound.
A program may use at most 384 MiB of HBM per device.

v0:
```python
import jax
import jax.numpy as jnp
import numpy as np
from jax import lax
from jax.experimental import pallas as pl
from jax.experimental.pallas import tpu as pltpu
from jax.sharding import PartitionSpec as P

H = 8
HD = 256
ROT = 64

epsilon = 1e-05


F32 = jnp.float32
BF16 = jnp.bfloat16
MESH = pl.DeviceIdType.MESH


def rotary_freqs():
    freqs = 10000.0 ** (-(np.arange(ROT // 2) * (2.0 / ROT)))
    return np.concatenate([freqs, freqs, np.zeros(128 - ROT)]).astype(np.float32).reshape(1, 128)


def dot(left, right, left_dim, right_dim):
    return lax.dot_general(
        left, right, (((left_dim,), (right_dim,)), ((), ())), preferred_element_type=F32
    )


def widen(value):
    rows, width = value.shape
    n = min(rows, max(8, 2**20 // width))

    def kernel(in_ref, out_ref):
        out_ref[...] = in_ref[...].astype(F32)

    spec = pl.BlockSpec((n, width), lambda i: (i, 0))
    return pl.pallas_call(
        kernel,
        grid=(rows // n,),
        in_specs=[spec],
        out_specs=spec,
        out_shape=jax.ShapeDtypeStruct(value.shape, F32),
        cost_estimate=pl.CostEstimate(flops=0, bytes_accessed=6 * rows * width, transcendentals=0),
        name="widen",
    )(value)


def place(pieces, rows, result):
    n, width = pieces[0].shape
    count = len(pieces)

    def kernel(rows_ref, *refs):
        sources, target = refs[:count], refs[count + 1]
        low, wide, come, go = refs[count + 2 :]
        for i in range(count):
            pltpu.make_async_copy(sources[i], low.at[i], come.at[i]).start()
        copies = []
        for i in range(count):
            pltpu.make_async_copy(sources[i], low.at[i], come.at[i]).wait()
            wide[i] = low[i].astype(F32)
            at = pl.multiple_of(rows_ref[i], n)
            copies.append(pltpu.make_async_copy(wide.at[i], target.at[pl.ds(at, n), :], go.at[i]))
            copies[-1].start()
        for copy in copies:
            copy.wait()

    any_spec = pl.BlockSpec(memory_space=pl.ANY)
    return pl.pallas_call(
        kernel,
        in_specs=[pl.BlockSpec(memory_space=pltpu.SMEM)] + [any_spec] * (count + 1),
        out_specs=any_spec,
        out_shape=jax.ShapeDtypeStruct(result.shape, F32),
        scratch_shapes=[
            pltpu.VMEM((count, n, width), BF16),
            pltpu.VMEM((count, n, width), F32),
            pltpu.SemaphoreType.DMA((count,)),
            pltpu.SemaphoreType.DMA((count,)),
        ],
        input_output_aliases={count + 1: 0},
        cost_estimate=pl.CostEstimate(flops=0, bytes_accessed=6 * count * n * width, transcendentals=0),
        name="place",
    )(rows, *pieces, result)


def unwritten(shape, dtype):
    return pl.pallas_call(
        lambda out_ref: None,
        out_shape=jax.ShapeDtypeStruct(shape, dtype),
        out_specs=pl.BlockSpec(memory_space=pl.ANY),
    )()


def bits_of(mask):
    return [1 << i for i in range(mask.bit_length()) if mask >> i & 1]


def layer(block_in, out_grad, small, freqs, w_up, w_qkv, w_down, w_out, S, TP, DP):
    T, D = block_in.shape
    rows, FS = w_up.shape[0], w_down.shape[0]
    NT, ND = 2 ** len(TP), 2 ** len(DP)
    FD, AD = FS // NT, w_out.shape[0] // NT
    heads = AD // HD
    scale = HD ** (-0.5)
    part = rows // ND
    third = w_qkv.shape[1] // 3
    tile = NT * T
    per = third * 3 // S // 128
    rest = D // S // 128
    base_out = 3 * third // 128
    base_up = base_out + D // 128
    base_norm = base_up + FS * S // 128
    count = base_norm + 4 * D // 128
    widths = [D, D, AD, FD, 3 * AD, FD, D, D]

    def kernel(
        small_ref, grad_ref, in_ref, up_ref, qkv_ref, down_ref, out_ref, freqs_ref,
        first_hbm, second_hbm, attended_hbm, activated_hbm, mixed_hbm, hidden_hbm, branch_hbm, inner_hbm, grad_hbm,
        small_all, sums_ref, bias_sum_ref,
        first_v, second_v, attended_v, activated_v, mixed_v, hidden_v, branch_v, inner_v,
        grad_all, in_all, up_all, qkv_all, down_all, out_all,
        wide_small, norms_ref, bias_ref, bias_up_ref, sum_qkv_ref, sum_up_ref, sum_norm_ref, sum_grad_ref,
        small_send, small_recv, line_send, line_recv, tp_send, tp_recv, z_send, z_recv, dp_send, dp_recv, local, leave,
    ):
        s = lax.axis_index("shard")
        r = lax.axis_index("replica")
        t = sum(((r // bit) % 2 * 2**i for i, bit in enumerate(TP)), jnp.int32(0))
        d = sum(((r // bit) % 2 * 2**i for i, bit in enumerate(DP)), jnp.int32(0))
        place = s * NT + t

        def flipped(value, mask):
            return sum((bit * (1 - 2 * ((value // bit) % 2)) for bit in bits_of(mask)), value)

        def other(k, m):
            mask = sum(bit for i, bit in enumerate(TP) if m >> i & 1)
            return {"shard": lax.rem(s + k, S), "replica": flipped(r, mask)}

        def mate(m):
            return {"replica": flipped(r, sum(bit for i, bit in enumerate(DP) if m >> i & 1))}

        group = [(k, m) for k in range(S) for m in range(NT) if k or m]
        plane = range(1, ND)
        gathered = (grad_all, in_all)
        mine = (grad_ref, in_ref)

        def columns(ref, at, n):
            return ref.at[:, pl.ds(pl.multiple_of(at, n), n)]

        here = pl.ds(pl.multiple_of(s * rows, rows), rows)
        copies = [
            pltpu.make_async_copy(small_ref, small_all.at[t, s], local.at[0]),
            pltpu.make_async_copy(grad_ref, grad_all.at[t, s], local.at[1]),
            pltpu.make_async_copy(in_ref, in_all.at[t, s], local.at[2]),
            pltpu.make_async_copy(columns(up_ref, place * FD, FD), up_all.at[here, :], local.at[3]),
            pltpu.make_async_copy(down_ref.at[pl.ds(pl.multiple_of(t * FD, FD), FD), :], down_all, local.at[4]),
            pltpu.make_async_copy(out_ref.at[pl.ds(pl.multiple_of(t * AD, AD), AD), :], out_all, local.at[5]),
        ]
        for j in range(3):
            source = columns(qkv_ref, j * third + place * AD, AD)
            copies.append(
                pltpu.make_async_copy(source, qkv_all.at[here, j * AD : (j + 1) * AD], local.at[6 + j])
            )
        for copy in copies:
            copy.start()

        barrier = pltpu.get_barrier_semaphore()
        for k, m in group:
            pl.semaphore_signal(barrier, inc=1, device_id=other(k, m), device_id_type=MESH)
        for m in plane:
            pl.semaphore_signal(barrier, inc=1, device_id=mate(m), device_id_type=MESH)
        pl.semaphore_wait(barrier, len(group) + len(plane))

        def small_copy(k, m):
            return pltpu.make_async_remote_copy(
                src_ref=small_ref, dst_ref=small_all.at[t, s], send_sem=small_send.at[k, m],
                recv_sem=small_recv.at[k, m], device_id=other(k, m), device_id_type=MESH,
            )

        def line(i, j, way, source):
            return pltpu.make_async_remote_copy(
                src_ref=source, dst_ref=gathered[i].at[t, j], send_sem=line_send.at[i, j, way],
                recv_sem=line_recv.at[i, j], device_id={"shard": s + 2 * way - 1}, device_id_type=MESH,
            )

        def across(i, j, m, source):
            slot = gathered[i].at[t, j]
            return pltpu.make_async_remote_copy(
                src_ref=slot if source is None else source, dst_ref=slot, send_sem=tp_send.at[i, j, m],
                recv_sem=tp_recv.at[i, j, m], device_id=other(0, m), device_id_type=MESH,
            )

        def z_copies(w, k, sending):
            to = lax.rem(s + k, S)
            at = (s if sending else lax.rem(s + S - k, S)) * rows + d * part
            at = pl.ds(pl.multiple_of(at, part), part)
            source_rows = pl.ds(pl.multiple_of(d * part, part), part)
            out = []
            for j in range(1 if w == 0 else 3):
                if w == 0:
                    source = up_ref.at[source_rows, pl.ds(pl.multiple_of((to * NT + t) * FD, FD), FD)]
                    target = up_all.at[at, :]
                else:
                    col = pl.multiple_of(j * third + (to * NT + t) * AD, AD)
                    source = qkv_ref.at[source_rows, pl.ds(col, AD)]
                    target = qkv_all.at[at, j * AD : (j + 1) * AD]
                out.append(
                    pltpu.make_async_remote_copy(
                        src_ref=source, dst_ref=target, send_sem=z_send.at[k, w + j], recv_sem=z_recv.at[k, w + j],
                        device_id={"shard": to}, device_id_type=MESH,
                    )
                )
            return out

        def shared(w, k, m):
            at = pl.multiple_of(lax.rem(s + S - k, S) * rows + d * part, part)
            slot = (up_all, qkv_all)[w].at[pl.ds(at, part), :]
            return pltpu.make_async_remote_copy(
                src_ref=slot, dst_ref=slot, send_sem=dp_send.at[w, k, m], recv_sem=dp_recv.at[w, k, m],
                device_id=mate(m), device_id_type=MESH,
            )

        for k, m in group:
            small_copy(k, m).start()
        for w in range(2):
            for k in range(1, S):
                for copy in z_copies(w, k, True):
                    copy.start()
        for i in range(2):

            @pl.when(s + 1 < S)
            def _():
                line(i, s, 1, mine[i]).start()

            @pl.when(s > 0)
            def _():
                line(i, s, 0, mine[i]).start()

            for m in range(1, NT):
                across(i, s, m, mine[i]).start()

        for ref in (sum_qkv_ref, sum_up_ref, sum_norm_ref, sum_grad_ref):
            ref[...] = jnp.zeros_like(ref)
        for w in range(2):
            for k in range(1, S):
                for copy in z_copies(w, k, False):
                    copy.wait_recv()
                for m in plane:
                    shared(w, k, m).start()
        for k, m in group:
            small_copy(k, m).wait_recv()
        for copy in copies:
            copy.wait()

        wide_small[...] = small_all[0].astype(F32)
        for v in range(4):
            for j in range(S):
                for i in range(rest):
                    at = (j * rest + i) * 128
                    row = per + (2 + v) * rest + i
                    norms_ref[v : v + 1, at : at + 128] = wide_small[j, row : row + 1, :]
        for j in range(S):
            for i in range(rest):
                at = (j * rest + i) * 128
                row = per + i
                bias_sum_ref[0:1, at : at + 128] = (
                    wide_small[j, row : row + 1, :] + wide_small[j, row + rest : row + rest + 1, :]
                )
        for v in range(3):
            for i in range(AD // 128):
                flat = v * (third // 128) + place * (AD // 128) + i
                at = v * AD + i * 128
                bias_ref[0:1, at : at + 128] = wide_small[flat // per, pl.ds(flat % per, 1), :]
        for i in range(FD // 128):
            row = per + 6 * rest + t * (FD // 128) + i
            bias_up_ref[0:1, i * 128 : (i + 1) * 128] = wide_small[s, pl.ds(row, 1), :]

        def from_line(i, j, way):
            line(i, j, way, gathered[i].at[t, j]).wait_recv()

            @pl.when((s + 1 < S) if way else (s > 0))
            def _():
                line(i, j, way, gathered[i].at[t, j]).start()

            for m in range(1, NT):
                across(i, j, m, None).start()

        def advance(k):
            for i in range(2):

                @pl.when(s - k >= 0)
                def _():
                    from_line(i, s - k, 1)

                @pl.when(s + k < S)
                def _():
                    from_line(i, s + k, 0)

        least = jnp.where(s < S - 1 - s, s, S - 1 - s)

        def block_at(i):
            both = jnp.where(i % 2 == 1, s - (i + 1) // 2, s + i // 2)
            one = jnp.where(s < S - 1 - s, i, S - 1 - i)
            return jnp.where(i <= 2 * least, both, one)

        row = lax.broadcasted_iota(jnp.int32, (T, T), 0)
        col = lax.broadcasted_iota(jnp.int32, (T, T), 1)
        away = (row - col).astype(F32)
        lane = lax.broadcasted_iota(jnp.int32, (T, 128), 1)

        def turn(value, table, sign):
            straight, ahead, back = table
            low = value[:, :128]
            low = low * straight + sign * (
                pltpu.roll(low, 128 - ROT // 2, 1) * ahead + pltpu.roll(low, ROT // 2, 1) * back
            )
            return jnp.concatenate([low, value[:, 128:]], axis=1)

        leaving = (
            (first_v, first_hbm), (second_v, second_hbm), (attended_v, attended_hbm), (activated_v, activated_hbm),
            (mixed_v, mixed_hbm), (hidden_v, hidden_hbm), (branch_v, branch_hbm), (inner_v, inner_hbm),
            (grad_all, grad_hbm),
        )

        def depart(v, u, j):
            source, target = leaving[v]
            return pltpu.make_async_copy(source.at[u, j], target.at[u, j], leave.at[v, u, j])

        def compute(i, carry):
            j = block_at(i)

            @pl.when(i == 0)
            def _():
                advance(1)
                for k in range(1, S):
                    for m in plane:
                        shared(0, k, m).wait_recv()

            @pl.when(i >= 2)
            def _():
                advance(i)

            for m in range(1, NT):
                for v in range(2):
                    across(v, j, m, None).wait_recv()

            def join(ref):
                return jnp.concatenate([ref[u, j] for u in range(NT)], axis=0)

            def put(v, value):
                for u in range(NT):
                    leaving[v][0][u, j] = value[u * T : (u + 1) * T]

            gain_1, shift_1, gain_2, shift_2 = [norms_ref[v : v + 1, :] for v in range(4)]
            wide = join(in_all).astype(F32)
            offsets = wide - jnp.mean(wide, axis=-1, keepdims=True)
            inverse = lax.rsqrt(jnp.mean(offsets * offsets, axis=-1, keepdims=True) + epsilon)
            normed = offsets * inverse
            first = (normed * gain_1 + shift_1).astype(BF16)
            second = (normed * gain_2 + shift_2).astype(BF16)
            put(0, first)
            put(1, second)
            grad = join(grad_all)
            sum_grad_ref[...] += jnp.sum(grad.astype(F32), axis=0, keepdims=True)

            pre = dot(second, up_all[...], 1, 0) + bias_up_ref[...]
            bell = 0.5 * (1.0 + lax.erf(pre * 0.7071067811865476))
            activated = (pre * bell).astype(BF16)
            put(3, activated)
            slope = bell + pre * jnp.exp(-0.5 * pre * pre) * 0.3989422804014327
            hidden_grad = dot(grad, down_all[...], 1, 1) * slope
            sum_up_ref[...] += jnp.sum(hidden_grad, axis=0, keepdims=True)
            hidden_low = hidden_grad.astype(BF16)
            put(5, hidden_low)

            @pl.when(i == 0)
            def _():
                for k in range(1, S):
                    for m in plane:
                        shared(1, k, m).wait_recv()

            mixed = dot(first, qkv_all[...], 1, 0) + bias_ref[...]
            attended_grad = dot(grad, out_all[...], 1, 1).astype(BF16)
            attended_parts, mixed_parts = [], []
            for u in range(NT):
                flat = small_all[u, j, -1:, :].astype(F32)
                position = jnp.sum(jnp.where(row == col, flat, 0.0), axis=1, keepdims=True)
                angle = position * freqs_ref[...]
                sine = jnp.sin(angle)
                table = (
                    jnp.cos(angle),
                    jnp.where(lane < ROT // 2, -sine, 0.0),
                    jnp.where((lane >= ROT // 2) & (lane < ROT), sine, 0.0),
                )
                allowed = (away >= 0) & (away <= position)
                at_rows = slice(u * T, (u + 1) * T)
                outs, q_grads, k_grads, v_grads = [], [], [], []
                for h in range(heads):
                    at = slice(h * HD, (h + 1) * HD)
                    ag = attended_grad[at_rows, at]
                    q = turn(mixed[at_rows, at], table, 1.0).astype(BF16)
                    k = turn(mixed[at_rows, AD + h * HD : AD + (h + 1) * HD], table, 1.0).astype(BF16)
                    v = mixed[at_rows, 2 * AD + h * HD : 2 * AD + (h + 1) * HD].astype(BF16)
                    scores = jnp.where(allowed, dot(q, k, 1, 1) * scale, -1e30)
                    peak = jnp.max(scores, axis=-1, keepdims=True)
                    logsum = peak + jnp.log(jnp.sum(jnp.exp(scores - peak), axis=-1, keepdims=True))
                    probs = jnp.exp(scores - logsum)
                    low = probs.astype(BF16)
                    outs.append(dot(low, v, 1, 0).astype(BF16))
                    dprobs = dot(ag, v, 1, 1)
                    total = jnp.sum(probs * dprobs, axis=-1, keepdims=True)
                    dscores = (probs * (dprobs - total) * scale).astype(BF16)
                    q_grads.append(turn(dot(dscores, k, 1, 0), table, -1.0))
                    k_grads.append(turn(dot(dscores, q, 0, 0), table, -1.0))
                    v_grads.append(dot(low, ag, 0, 0))
                attended_parts.append(jnp.concatenate(outs, axis=1))
                mixed_parts.append(jnp.concatenate(q_grads + k_grads + v_grads, axis=1))
            attended = jnp.concatenate(attended_parts, axis=0)
            put(2, attended)
            mixed_grad = jnp.concatenate(mixed_parts, axis=0)
            sum_qkv_ref[...] += jnp.sum(mixed_grad, axis=0, keepdims=True)
            mixed_low = mixed_grad.astype(BF16)
            put(4, mixed_low)

            branch = dot(attended, out_all[...], 1, 0) + dot(activated, down_all[...], 1, 0)
            put(6, branch.astype(BF16))
            first_grad = dot(mixed_low, qkv_all[...], 1, 1)
            second_grad = dot(hidden_low, up_all[...], 1, 1)
            sum_norm_ref[0:1, :] += jnp.sum(first_grad * normed, axis=0, keepdims=True)
            sum_norm_ref[1:2, :] += jnp.sum(first_grad, axis=0, keepdims=True)
            sum_norm_ref[2:3, :] += jnp.sum(second_grad * normed, axis=0, keepdims=True)
            sum_norm_ref[3:4, :] += jnp.sum(second_grad, axis=0, keepdims=True)
            put(7, (first_grad * gain_1 + second_grad * gain_2).astype(BF16))
            for v in range(len(leaving)):
                for u in range(NT):
                    depart(v, u, j).start()
            return carry

        lax.fori_loop(0, S, compute, 0)

        sums_ref[...] = jnp.zeros_like(sums_ref)
        n = AD // 128
        for v in range(3):
            for i in range(n):
                at = v * AD + i * 128
                sums_ref[pl.ds(v * (third // 128) + place * n + i, 1), :] = sum_qkv_ref[:, at : at + 128]
        for i in range(FD // 128):
            sums_ref[pl.ds(base_up + place * (FD // 128) + i, 1), :] = sum_up_ref[:, i * 128 : (i + 1) * 128]
        for i in range(D // 128):
            at = slice(i * 128, (i + 1) * 128)
            sums_ref[base_out + i : base_out + i + 1, :] = sum_grad_ref[:, at] * (1.0 / (S * NT))
            for v in range(4):
                at_row = base_norm + v * (D // 128) + i
                sums_ref[at_row : at_row + 1, :] = sum_norm_ref[v : v + 1, at]

        for i in range(2):
            for j in range(S):

                @pl.when((s + 1 < S) & (j <= s))
                def _():
                    line(i, j, 1, gathered[i].at[t, j]).wait_send()

                @pl.when((s > 0) & (j >= s))
                def _():
                    line(i, j, 0, gathered[i].at[t, j]).wait_send()

                for m in range(1, NT):
                    across(i, j, m, None).wait_send()
        for k, m in group:
            small_copy(k, m).wait_send()
        for w in range(2):
            for k in range(1, S):
                for copy in z_copies(w, k, True):
                    copy.wait_send()
                for m in plane:
                    shared(w, k, m).wait_send()
        for v in range(len(leaving)):
            for u in range(NT):
                for j in range(S):
                    depart(v, u, j).wait()

    any_spec = pl.BlockSpec(memory_space=pl.ANY)
    vmem_spec = pl.BlockSpec(memory_space=pltpu.VMEM)
    outs = [jax.ShapeDtypeStruct((NT, S, T, w), BF16) for w in widths + [D]]
    outs += [jax.ShapeDtypeStruct((NT, S) + small.shape, BF16), jax.ShapeDtypeStruct((count, 128), F32)]
    outs += [jax.ShapeDtypeStruct((1, D), F32)]
    flops = 2 * S * tile * D * (2 * 3 * AD + 2 * FD + 2 * FD + 2 * AD)
    return pl.pallas_call(
        kernel,
        out_shape=outs,
        in_specs=[any_spec] * 7 + [vmem_spec],
        out_specs=[any_spec] * 9 + [vmem_spec] * 3,
        scratch_shapes=[pltpu.VMEM((NT, S, T, w), BF16) for w in widths]
        + [
            pltpu.VMEM((NT, S, T, D), BF16),
            pltpu.VMEM((NT, S, T, D), BF16),
            pltpu.VMEM((D, FD), BF16),
            pltpu.VMEM((D, 3 * AD), BF16),
            pltpu.VMEM((FD, D), BF16),
            pltpu.VMEM((AD, D), BF16),
            pltpu.VMEM((S,) + small.shape, F32),
            pltpu.VMEM((4, D), F32),
            pltpu.VMEM((1, 3 * AD), F32),
            pltpu.VMEM((1, FD), F32),
            pltpu.VMEM((1, 3 * AD), F32),
            pltpu.VMEM((1, FD), F32),
            pltpu.VMEM((4, D), F32),
            pltpu.VMEM((1, D), F32),
            pltpu.SemaphoreType.DMA((S, NT)),
            pltpu.SemaphoreType.DMA((S, NT)),
            pltpu.SemaphoreType.DMA((2, S, 2)),
            pltpu.SemaphoreType.DMA((2, S)),
            pltpu.SemaphoreType.DMA((2, S, NT)),
            pltpu.SemaphoreType.DMA((2, S, NT)),
            pltpu.SemaphoreType.DMA((S, 4)),
            pltpu.SemaphoreType.DMA((S, 4)),
            pltpu.SemaphoreType.DMA((2, S, ND)),
            pltpu.SemaphoreType.DMA((2, S, ND)),
            pltpu.SemaphoreType.DMA((9,)),
            pltpu.SemaphoreType.DMA((9, NT, S)),
        ],
        compiler_params=pltpu.CompilerParams(
            collective_id=0, has_side_effects=True, vmem_limit_bytes=67043328
        ),
        cost_estimate=pl.CostEstimate(flops=flops, bytes_accessed=80 * 2**20, transcendentals=S * tile * FD * 2),
        name="layer",
    )(small, out_grad, block_in, w_up, w_qkv, w_down, w_out, freqs)


def grads(
    first, second, attended, activated, mixed, hidden, grad, branch, inner, sums, block_in, out_grad, bias, S, R, TP, DP
):
    N, D = grad.shape
    T = block_in.shape[0]
    NT, ND, steps = 2 ** len(TP), 2 ** len(DP), len(DP)
    lefts = (second, first, activated, attended)
    rights = (hidden, mixed, grad, grad)
    pieces = []
    for left, right, lead, mid in zip(lefts, rights, (S, S, 1, 1), (NT, NT, 1, 1)):
        pieces.append((lead, mid, left.shape[1] // (lead * ND * mid * 2), right.shape[1]))
    ways = []
    for way in (DP, DP[::-1]):
        ways.append([(bit, 1 << DP.index(bit)) for bit in way])

    def masks(bits):
        out = [0]
        for _, bit in bits:
            out += [v | bit for v in out]
        return sorted(out)

    slots = []
    for way in ways:
        table = {}
        for j in range(steps):
            for u in masks(way[j + 1 :]):
                table[j, u] = len(table)
        slots.append(table)

    def kernel(
        second_hbm, first_hbm, activated_hbm, attended_hbm, hidden_hbm, mixed_hbm, grad_hbm, branch_hbm, inner_hbm, sums_hbm,
        block_hbm, out_hbm, bias_ref,
        whole_up, whole_down, whole_out, own_qkv_0, own_qkv_1, block_out, in_grad, sums_out,
        own_up, own_down, own_out, block_v, out_v, near, near_came, far_came, held, held_came,
        second_v, first_v, activated_v, attended_v, hidden_v, mixed_v, grad_v,
        part_up, part_qkv, part_down, part_out, came_up, came_qkv, came_down, came_out, all_up, all_qkv,
        load, dp_send, dp_recv, z_send, z_recv, near_send, near_recv, far_send, far_recv, held_send, held_recv,
        plane_send, plane_recv,
    ):
        s = lax.axis_index("shard")
        r = lax.axis_index("replica")
        t = sum(((r // bit) % 2 * 2**i for i, bit in enumerate(TP)), jnp.int32(0))
        d = sum(((r // bit) % 2 * 2**i for i, bit in enumerate(DP)), jnp.int32(0))

        def flipped(value, mask):
            return sum((bit * (1 - 2 * ((value // bit) % 2)) for bit in bits_of(mask)), value)

        def other(k, m):
            mask = sum(bit for i, bit in enumerate(TP) if m >> i & 1)
            return {"shard": lax.rem(s + k, S), "replica": flipped(r, mask)}

        loads = []
        order = ((hidden_hbm, hidden_v), (second_hbm, second_v), (mixed_hbm, mixed_v), (first_hbm, first_v),
                 (grad_hbm, grad_v), (activated_hbm, activated_v), (attended_hbm, attended_v))
        parts_hbm = (branch_hbm, inner_hbm)
        for i, (source, target) in enumerate(order):
            loads.append(pltpu.make_async_copy(source, target, load.at[i]))
        token_loads = [
            pltpu.make_async_copy(
                parts_hbm[i].at[t] if NT > 1 else parts_hbm[i].at[t, pl.ds(s, 1)], near.at[i], load.at[7 + i]
            )
            for i in range(2)
        ]
        held_load = pltpu.make_async_copy(sums_hbm, held.at[0], load.at[9])
        own_loads = [
            pltpu.make_async_copy(block_hbm, block_v, load.at[16]),
            pltpu.make_async_copy(out_hbm, out_v, load.at[17]),
        ]
        for copy in (loads[6], loads[4], *loads[:2], held_load, *token_loads, *loads[2:4], loads[5], *own_loads):
            copy.start()

        group = [(k, m) for k in range(S) for m in range(NT) if k or m]
        barrier = pltpu.get_barrier_semaphore()
        for k, m in group:
            pl.semaphore_signal(barrier, inc=1, device_id=other(k, m), device_id_type=MESH)
        for bit in DP:
            pl.semaphore_signal(barrier, inc=1, device_id={"replica": flipped(r, bit)}, device_id_type=MESH)
        pl.semaphore_wait(barrier, len(group) + steps)

        left_refs = (second_v, first_v, activated_v, attended_v)
        right_refs = (hidden_v, mixed_v, grad_v, grad_v)
        part = (part_up, part_qkv, part_down, part_out)
        came = (came_up, came_qkv, came_down, came_out)
        own = (own_up, (own_qkv_0, own_qkv_1), own_down, own_out)

        def product(i):
            lead, mid, n, _ = pieces[i]
            if lead > 1:
                width = ND * mid * 2 * n

                def body(l, carry):
                    cols = pl.ds(pl.multiple_of(l * width, width), width)
                    value = dot(left_refs[i][:, cols], right_refs[i][...], 0, 0).astype(BF16)
                    for q in range(ND):
                        for c in range(mid):
                            for h in range(2):
                                at = ((q * mid + c) * 2 + h) * n
                                part[i][h, q, l, c] = value[at : at + n]
                    return carry

                lax.fori_loop(0, lead, body, 0)
            else:
                total = ND * 2 * n
                chunk = min(total, 512)
                per = chunk // (2 * n)

                def body(l, carry):
                    cols = pl.ds(pl.multiple_of(l * chunk, chunk), chunk)
                    value = dot(left_refs[i][:, cols], right_refs[i][...], 0, 0).astype(BF16)
                    for q in range(per):
                        for h in range(2):
                            at = (q * 2 + h) * n
                            part[i][h, l * per + q, 0, 0] = value[at : at + n]
                    return carry

                lax.fori_loop(0, total // chunk, body, 0)

        def halving(i, h, j, u):
            bit, dbit = ways[h][j]
            slot = slots[h][j, u]
            return pltpu.make_async_remote_copy(
                src_ref=part[i].at[h, flipped(d, dbit | u)], dst_ref=came[i].at[h, slot],
                send_sem=dp_send.at[i, h, slot], recv_sem=dp_recv.at[i, h, slot],
                device_id={"replica": flipped(r, bit)}, device_id_type=MESH,
            )

        def summed(i, h, mask, count, write):
            lead, mid, _, _ = pieces[i]
            at = flipped(d, mask)
            for j in range(count):
                halving(i, h, j, mask).wait_recv()

            def body(l, carry):
                for c in range(mid):
                    value = part[i][h, at, l, c].astype(F32)
                    for j in range(count):
                        value = value + came[i][h, slots[h][j, mask], l, c].astype(F32)
                    write(l, c, value.astype(BF16))
                return carry

            lax.fori_loop(0, lead, body, 0)

        def step(i, j):
            for h in range(2):
                for u in masks(ways[h][j + 1 :]):
                    mask = ways[h][j][1] | u
                    at = flipped(d, mask)
                    if j:

                        def write(l, c, value, h=h, at=at):
                            part[i][h, at, l, c] = value

                        summed(i, h, mask, j, write)
                    halving(i, h, j, u).start()

        everyone = (all_up, all_qkv)

        def to_shard(i, h, k, m):
            there = lax.rem(s + k, S)
            return pltpu.make_async_remote_copy(
                src_ref=part[i].at[h, d, there, flipped(t, m)], dst_ref=everyone[i].at[s, t, h],
                send_sem=z_send.at[i, h, k, m], recv_sem=z_recv.at[i, h, k, m],
                device_id=other(k, m), device_id_type=MESH,
            )

        def last(i):
            for h in range(2):
                if i < 2:

                    def write(l, c, value, h=h):
                        part[i][h, d, l, c] = value

                else:

                    def write(l, c, value, h=h):
                        own[i][h] = value

                summed(i, h, 0, steps, write)
            if i < 2:
                for k, m in group:
                    for h in range(2):
                        to_shard(i, h, k, m).start()
                for h in range(2):
                    everyone[i][s, t, h] = part[i][h, d, s, t]

        def collect(i):
            width = pieces[i][3]
            runs = 1 if i == 0 else 3
            n = width // runs
            for k, m in group:
                for h in range(2):
                    to_shard(i, h, k, m).wait_recv()
            for h in range(2):
                for j in range(S):
                    for u in range(NT):
                        block = everyone[i][j, u, h]
                        for v in range(runs):
                            at = (v * S * NT + j * NT + u) * n
                            target = own[i][h] if i == 1 else own[i].at[h]
                            target[:, at : at + n] = block[:, v * n : (v + 1) * n]

        def near_copy(i, m):
            return pltpu.make_async_remote_copy(
                src_ref=parts_hbm[i].at[flipped(t, m)], dst_ref=near_came.at[i, m - 1],
                send_sem=near_send.at[i, m], recv_sem=near_recv.at[i, m], device_id=other(0, m), device_id_type=MESH,
            )

        def far_copy(i, k):
            there = lax.rem(s + k, S)
            return pltpu.make_async_remote_copy(
                src_ref=near.at[i, there] if NT > 1 else parts_hbm[i].at[t, there], dst_ref=far_came.at[i, k - 1],
                send_sem=far_send.at[i, k], recv_sem=far_recv.at[i, k], device_id=other(k, 0), device_id_type=MESH,
            )

        def near_sum(i, j):
            value = near[i, j if NT > 1 else 0].astype(F32)
            for m in range(1, NT):
                value = value + near_came[i, m - 1, j].astype(F32)
            return value

        def tokens_near(i):
            token_loads[i].wait()
            for m in range(1, NT):
                near_copy(i, m).wait_recv()

            def body(k, carry):
                j = lax.rem(s + k, S)
                near[i, j] = near_sum(i, j).astype(BF16)
                return carry

            if NT > 1:
                lax.fori_loop(1, S, body, 0)
            for k in range(1, S):
                far_copy(i, k).start()

        def tokens_far(i):
            value = near_sum(i, s)
            for k in range(1, S):
                far_copy(i, k).wait_recv()
                value = value + far_came[i, k - 1].astype(F32)
            return value

        def finish():
            for copy in own_loads:
                copy.wait()
            wide = block_v[...].astype(F32)
            block_out[...] = (wide + tokens_far(0) + bias_ref[...]).astype(BF16)
            offsets = wide - jnp.mean(wide, axis=-1, keepdims=True)
            inverse = lax.rsqrt(jnp.mean(offsets * offsets, axis=-1, keepdims=True) + epsilon)
            normed = offsets * inverse
            scaled = tokens_far(1)
            term = inverse * (
                scaled
                - jnp.mean(scaled, axis=-1, keepdims=True)
                - normed * jnp.mean(scaled * normed, axis=-1, keepdims=True)
            )
            in_grad[...] = (out_v[...].astype(F32) + term).astype(BF16)

        bits = [(0, bit) for bit in bits_of(R - 1)] + [(1, bit) for bit in bits_of(S - 1)]

        def double(i):
            axis, bit = bits[i]
            to = {"replica": flipped(r, bit)} if axis == 0 else {"shard": flipped(s, bit)}
            return pltpu.make_async_remote_copy(
                src_ref=held.at[i], dst_ref=held_came.at[i], send_sem=held_send.at[i], recv_sem=held_recv.at[i],
                device_id=to, device_id_type=MESH,
            )

        def doubled(i):
            double(i).wait_recv()
            value = held[i] + held_came[i]
            if i + 1 < len(bits):
                held[i + 1] = value
                double(i + 1).start()
            else:
                sums_out[...] = value

        wholes = {0: whole_up, 2: whole_down, 3: whole_out}
        order_of = {0: 0, 2: 1, 3: 2}

        def slot_of(i, h, dd, tt):
            n = pieces[i][2]
            if i == 0:
                at = (dd * NT + tt) * 2 * n + h * n
            else:
                at = tt * (ND * 2 * n) + dd * 2 * n + h * n
            return wholes[i].at[pl.ds(pl.multiple_of(at, n), n), :]

        def gather(i, h, m, b):
            dmask = sum(ways[h][v][1] for v in range(steps) if m >> v & 1)
            tmask = m >> steps
            slot = slot_of(i, h, flipped(d, dmask), flipped(t, tmask))
            bit = ways[h][b][0] if b < steps else TP[b - steps]
            return pltpu.make_async_remote_copy(
                src_ref=own[i].at[h] if m == 0 else slot, dst_ref=slot,
                send_sem=plane_send.at[order_of[i], h, m | 1 << b], recv_sem=plane_recv.at[order_of[i], h, m | 1 << b],
                device_id={"replica": flipped(r, bit)}, device_id_type=MESH,
            )

        positions = steps + len(TP)

        def keep_own(i, h):
            return pltpu.make_async_copy(own[i].at[h], slot_of(i, h, d, t), load.at[10 + order_of[i] * 2 + h])

        def share_own(i):
            for h in range(2):
                for b in range(positions):
                    gather(i, h, 0, b).start()
                keep_own(i, h).start()

        def share_on(i, m):
            top = m.bit_length() - 1
            for h in range(2):
                gather(i, h, m ^ 1 << top, top).wait_recv()
                for b in range(top + 1, positions):
                    gather(i, h, m, b).start()

        for i in range(2):
            for m in range(1, NT):
                near_copy(i, m).start()
        held_load.wait()
        double(0).start()
        loads[4].wait()
        loads[6].wait()
        product(3)
        step(3, 0)
        loads[0].wait()
        loads[1].wait()
        product(0)
        step(0, 0)
        tokens_near(0)
        doubled(0)
        loads[2].wait()
        loads[3].wait()
        product(1)
        step(1, 0)
        for j in range(1, steps):
            step(0, j)
        doubled(1)
        loads[5].wait()
        product(2)
        step(2, 0)
        for j in range(1, steps):
            step(1, j)
        last(0)
        for i in range(2, len(bits)):
            doubled(i)
        for j in range(1, steps):
            step(2, j)
        last(1)
        for j in range(1, steps):
            step(3, j)
        tokens_near(1)
        collect(0)
        share_own(0)
        last(2)
        share_own(2)
        last(3)
        share_own(3)
        for m in range(1, 1 << steps):
            for i in (0, 2, 3):
                share_on(i, m)
            if m == 1:
                collect(1)
                finish()
        for m in range(1 << steps, 1 << positions):
            for i in (0, 2, 3):
                share_on(i, m)

        for i in (2, 3, 0):
            for h in range(2):
                keep_own(i, h).wait()
                for m in range(1 << positions):
                    for b in range(m.bit_length(), positions):
                        gather(i, h, m, b).wait_send()
        for i in range(2):
            for m in range(1, NT):
                near_copy(i, m).wait_send()
            for k in range(1, S):
                far_copy(i, k).wait_send()
        for i in range(len(bits)):
            double(i).wait_send()
        for i in range(4):
            for h in range(2):
                for j, u in slots[h]:
                    halving(i, h, j, u).wait_send()
        for i in range(2):
            for h in range(2):
                for k, m in group:
                    to_shard(i, h, k, m).wait_send()

    def scratch(value):
        return pltpu.VMEM(value.shape, BF16)

    any_spec = pl.BlockSpec(memory_space=pl.ANY)
    vmem_spec = pl.BlockSpec(memory_space=pltpu.VMEM)
    operands = (second, first, activated, attended, hidden, mixed, grad)
    owns = [(2, n, width * S * NT if lead > 1 else width) for lead, _, n, width in pieces]
    wholes = [(2 * n * ND * NT, width) for _, n, width in owns]
    outs = [jax.ShapeDtypeStruct(wholes[i], BF16) for i in (0, 2, 3)]
    outs += [jax.ShapeDtypeStruct(owns[1][1:], BF16)] * 2 + [jax.ShapeDtypeStruct((T, D), BF16)] * 2
    outs += [jax.ShapeDtypeStruct(sums.shape, F32)]
    sent = sum(2 * (ND - 1) * a * b * n * w * 2 for a, b, n, w in pieces)
    count = len(bits_of(R - 1)) + len(bits_of(S - 1))
    return pl.pallas_call(
        kernel,
        out_shape=outs,
        in_specs=[any_spec] * 12 + [vmem_spec],
        out_specs=[any_spec] * 3 + [vmem_spec] * 5,
        scratch_shapes=[pltpu.VMEM(owns[i], BF16) for i in (0, 2, 3)]
        + [
            pltpu.VMEM((T, D), BF16),
            pltpu.VMEM((T, D), BF16),
            pltpu.VMEM((2, S if NT > 1 else 1, T, D), BF16),
            pltpu.VMEM((2, NT - 1, S, T, D) if NT > 1 else (1, 1, 1, 16, 128), BF16),
            pltpu.VMEM((2, S - 1, T, D), BF16),
            pltpu.VMEM((count,) + sums.shape, F32),
            pltpu.VMEM((count,) + sums.shape, F32),
        ]
        + [scratch(v) for v in operands]
        + [pltpu.VMEM((2, ND) + piece, BF16) for piece in pieces]
        + [pltpu.VMEM((2, ND - 1) + piece, BF16) for piece in pieces]
        + [pltpu.VMEM((S, NT, 2) + piece[2:], BF16) for piece in pieces[:2]]
        + [
            pltpu.SemaphoreType.DMA((18,)),
            pltpu.SemaphoreType.DMA((4, 2, ND - 1)),
            pltpu.SemaphoreType.DMA((4, 2, ND - 1)),
            pltpu.SemaphoreType.DMA((2, 2, S, NT)),
            pltpu.SemaphoreType.DMA((2, 2, S, NT)),
            pltpu.SemaphoreType.DMA((2, NT)),
            pltpu.SemaphoreType.DMA((2, NT)),
            pltpu.SemaphoreType.DMA((2, S)),
            pltpu.SemaphoreType.DMA((2, S)),
            pltpu.SemaphoreType.DMA((count,)),
            pltpu.SemaphoreType.DMA((count,)),
            pltpu.SemaphoreType.DMA((3, 2, ND * NT)),
            pltpu.SemaphoreType.DMA((3, 2, ND * NT)),
        ],
        compiler_params=pltpu.CompilerParams(
            collective_id=1, has_side_effects=True, vmem_limit_bytes=67043328
        ),
        cost_estimate=pl.CostEstimate(
            flops=2 * N * sum(v.shape[1] * w.shape[1] for v, w in zip(lefts, rights)),
            bytes_accessed=sent * 8, transcendentals=0,
        ),
        name="grads",
    )(*operands, branch, inner, sums, block_in, out_grad, bias)


def solution(mesh):
    S = mesh.shape["shard"]
    R = mesh.shape["replica"]
    TP = [1] if R > 1 and H % (2 * S) == 0 else []
    DP = [bit for bit in bits_of(R - 1) if bit not in TP]
    NT = 2 ** len(TP)

    def flip(value, bit):
        return lax.ppermute(value, "replica", [(i, i ^ bit) for i in range(R)])

    def body(
        block_in, positions, out_grad, w_qkv, b_qkv, w_out, b_out, w_up, b_up, w_down, b_down,
        first_gain, first_shift, second_gain, second_shift,
    ):
        T, D = block_in.shape
        FS = w_down.shape[0]
        s = lax.axis_index("shard")
        r = lax.axis_index("replica")
        mine = {bit: (r // bit) % 2 for bit in bits_of(R - 1)}
        t = sum((mine[bit] * 2**i for i, bit in enumerate(TP)), jnp.int32(0))

        vectors = [
            b_qkv, b_out, b_down, first_gain, first_shift, second_gain, second_shift, b_up, positions.astype(BF16)
        ]
        ends = [sum(v.shape[0] for v in vectors[: i + 1]) for i in range(len(vectors))]
        small = sum(lax.pad(v, jnp.zeros((), BF16), [(end - v.shape[0], ends[-1] - end, 0)]) for v, end in zip(vectors, ends))
        small = small.reshape(-1, 128)
        (
            first_low, second_low, attended, activated, mixed_low, hidden_low, branch_part, inner_part, grad_all,
            _, sums, bias,
        ) = layer(block_in, out_grad, small, rotary_freqs(), w_up, w_qkv, w_down, w_out, S, TP, DP)
        first_low, second_low, attended, activated, mixed_low, hidden_low, grad_all = [
            v.reshape(NT * S * T, -1)
            for v in (first_low, second_low, attended, activated, mixed_low, hidden_low, grad_all)
        ]
        d = sum((mine[bit] * 2**i for i, bit in enumerate(DP)), jnp.int32(0))

        whole_up, whole_down, whole_out, *own_qkv, block_out, in_grad, sums = grads(
            first_low, second_low, attended, activated, mixed_low, hidden_low, grad_all, branch_part, inner_part,
            sums, block_in, out_grad, bias, S, R, TP, DP,
        )

        ways = [DP + TP, DP[::-1] + TP]
        n = own_qkv[0].shape[0]

        def over(bit, value):
            return flip(value, bit)

        def placed(result, pieces):
            at = []
            for half, m, _ in pieces:
                dmask = sum(2**i for i, bit in enumerate(DP) if m & bit)
                tmask = sum(2**i for i, bit in enumerate(TP) if m & bit)
                at.append(((d ^ dmask) * NT + (t ^ tmask)) * 2 * n + half * n)
            return place([value for _, _, value in pieces], jnp.stack(at), result)

        def with_partners(pieces):
            for bit in TP:
                pieces = pieces + [(half, m | bit, flip(value, bit)) for half, m, value in pieces]
            return pieces

        got = [{0: own_qkv[half]} for half in range(2)]
        for i in range(len(DP)):
            for half in range(2):
                bit = ways[half][i]
                got[half].update({m | bit: over(bit, v) for m, v in list(got[half].items())})
        late = [ways[half][len(DP) - 1] for half in range(2)]
        early = [(half, m, v) for half in range(2) for m, v in got[half].items() if not m & late[half]]
        final = [(half, m, v) for half in range(2) for m, v in got[half].items() if m & late[half]]
        grad_w_down = widen(whole_down)
        grad_w_up = widen(whole_up)
        grad_w_out = widen(whole_out)
        grad_w_qkv = placed(unwritten(w_qkv.shape, F32), with_partners(early))
        grad_w_qkv = placed(grad_w_qkv, with_partners(final))

        sums = sums.reshape(-1)
        width = w_out.shape[0] * S
        lengths = [width] * 3 + [D, FS * S] + [D] * 4
        at = [sum(lengths[:i]) for i in range(len(lengths))]

        def owned(start, length):
            return lax.dynamic_slice_in_dim(sums, start + s * (length // S), length // S, 0)

        grad_b_qkv = owned(at[0], 3 * width)
        grad_b_out = owned(at[3], D)
        grad_b_up = owned(at[4], FS * S)
        smalls = [owned(at[5 + i], D) for i in range(4)]
        return (
            block_out, in_grad, grad_w_qkv, grad_b_qkv, grad_w_out, grad_b_out, grad_w_up, grad_b_up,
            grad_w_down, grad_b_out, *smalls,
        )

    rows2, row1, par2, par1 = P(("shard", "replica"), None), P(("shard", "replica")), P("shard", None), P("shard")
    return jax.shard_map(
        body,
        mesh=mesh,
        in_specs=(
            rows2, row1, rows2, par2, par1, par2, par1, par2, par1, par2, par1, par1, par1, par1, par1,
        ),
        out_specs=(
            rows2, rows2, par2, par1, par2, par1, par2, par1, par2, par1, par1, par1, par1, par1,
        ),
        check_vma=False,
    )
```

profile of v0, /device:TPU:0, one launch (start us, length us, event | category | flops | bytes accessed | tf_op | source)
XLA Modules:
  0.0 397.7 jit_solution(9230738613460425400)
XLA Ops:
  0.6 0.7 convert_element_type.3
  1.3 1.4 add_bitcast_fusion.small_ref
  2.7 131.9 %layer.1 = (bf16[2,4,128,2048]{3,2,1,0:T(8,128)(2,1)}, bf16[2,4,128,2048]{3,2,1,0:T(8,128)(2,1)}, bf16[2,4,128,256]{3,2,1,0:T(8,128)(2,1)}, bf16[2,4,128,1024]{3...) custom-call(bf16[53,128]{1,0:T(8,128)(2,1)} %add_bitcast_fusion.smal, ...), custom_call_target="tpu_custom_call" | custom-call | flops 25769803776 | bytes 83886080 | tf_op jit(solution)/shard_map/layer/pallas_call | solution.py:489
  134.7 192.0 %grads.1 = (bf16[512,8192]{1,0:T(8,128)(2,1)}, bf16[2048,2048]{1,0:T(8,128)(2,1)}, bf16[512,2048]{1,0:T(8,128)(2,1)}, bf16[32,6144]{1,0:T(8,128)(2,1)}, bf16[32,...) custom-call(bf16[1024,2048]{1,0:T(8,128)(2,1)} %bitcast.30, ...), custom_call_target="tpu_custom_call" | custom-call | flops 12884901888 | bytes 75497472 | tf_op jit(solution)/shard_map/grads/pallas_call | solution.py:935
  326.7 1.7 collective-permute-start.1
  328.4 0.4 collective-permute-start.4
  328.7 0.0 collective-permute-start.10
  328.7 0.5 collective-permute-start.12
  329.2 1.7 collective-permute-start
  330.9 7.3 %collective-permute-done.1.refs_1_ = bf16[32,6144]{1,0:T(8,128)(2,1)S(1)} collective-permute-done((bf16[32,6144]{1,0:T(8,128)(2,1)}, bf16[32,6144]{1,0:T(8,128)(2,1)S(1)}, u32[]{:S(2)}, u32[]{:S(2)}) %collective-permute-start.1) | collective-permute-done | bytes 393248 | tf_op jit(solution)/shard_map/ppermute | solution.py:988
  338.2 0.0 copy-start.3
  338.2 1.5 collective-permute-start.3
  339.7 0.9 collective-permute-done.4.refs_3_
  340.6 0.0 copy-start.5
  340.6 0.0 collective-permute-start.11
  340.6 0.0 collective-permute-done.10.refs_4_
  340.6 0.0 copy-start.6
  340.6 0.4 collective-permute-start.2
  341.0 0.0 collective-permute-done.12.refs_6_
  341.0 0.0 copy-start.7
  341.0 1.9 collective-permute-start.5
  342.9 6.1 %collective-permute-done.refs_0_ = bf16[32,6144]{1,0:T(8,128)(2,1)S(1)} collective-permute-done((bf16[32,6144]{1,0:T(8,128)(2,1)}, bf16[32,6144]{1,0:T(8,128)(2,1)S(1)}, u32[]{:S(2)}, u32[]{:S(2)}) %collective-permute-start) | collective-permute-done | bytes 393248 | tf_op jit(solution)/shard_map/ppermute | solution.py:988
  349.0 0.0 collective-permute-start.13
  349.0 1.4 collective-permute-done.3.refs_2_
  350.4 0.0 collective-permute-start.6
  350.4 0.0 collective-permute-done.11.refs_5_
  350.4 0.0 copy-start.10
  350.4 0.5 collective-permute-start.8
  350.9 5.4 %collective-permute-done.2.refs_1_ = bf16[32,6144]{1,0:T(8,128)(2,1)S(1)} collective-permute-done((bf16[32,6144]{1,0:T(8,128)(2,1)S(1)}, bf16[32,6144]{1,0:T(8,128)(2,1)S(1)}, u32[]{:S(2)}, u32[]{:S(2)}) %collective-permute-start.2) | collective-permute-done | bytes 393248 | tf_op jit(solution)/shard_map/ppermute | solution.py:988
  356.3 0.0 collective-permute-start.7
  356.3 0.9 collective-permute-done.5.refs_3_
  357.2 0.0 copy-done.10
  357.2 0.0 collective-permute-start.9
  357.3 0.0 copy-done.3
  357.3 0.0 copy-done.5
  357.3 0.0 copy-done.6
  357.3 0.0 copy-done.7
  357.4 0.0 copy-done.2
  357.4 0.0 copy-done.4
  357.4 0.0 copy-done.8
  357.4 0.6 copy-done.9
  358.0 1.4 fusion
  359.3 1.4 dynamic_slice.21
  360.7 1.3 dynamic_slice.23
  362.0 9.5 %widen.4 = f32[512,8192]{1,0:T(8,128)} custom-call(bf16[512,8192]{1,0:T(8,128)(2,1)} %get-tuple-element.50.in_ref), custom_call_target="tpu_custom_call" | custom-call | bytes 25165824 | tf_op jit(solution)/shard_map/widen/pallas_call | solution.py:40
  371.5 9.5 %widen.5 = f32[2048,2048]{1,0:T(8,128)} custom-call(bf16[2048,2048]{1,0:T(8,128)(2,1)} %get-tuple-element.51.in_ref), custom_call_target="tpu_custom_call" | custom-call | bytes 25165824 | tf_op jit(solution)/shard_map/widen/pallas_call | solution.py:40
  381.1 3.9 widen.3
  384.9 0.6 stack.71.rows_ref
  385.6 0.7 stack.62.rows_ref
  386.2 0.0 collective-permute-done.13.refs_7_
  386.2 4.5 %place.2.refs_8_ = f32[512,6144]{1,0:T(8,128)} custom-call(s32[8]{0:T(128)} %stack.71.rows_ref, bf16[32,6144]{1,0:T(8,128)(2,1)} %get-tuple-element.46.refs_0_, bf16[32,6144]{1,0:T(8,128)(2,1)} %copy-done.3, bf16[32,6144]{1,0:T(8,128)(2,1)} %get-tuple-element.47.refs_2_, bf16[32,6144]{1,0:T(8,128)(2,1)} %copy-done.5, ...), custom_call_target="tpu_custom_call", output_to_operand_aliasing={{}: (9, {})} | custom-call | bytes 9437184 | tf_op jit(solution)/shard_map/place/pallas_call | solution.py:71
  390.8 0.0 copy-start.1
  390.8 0.0 copy-start
  390.8 0.0 collective-permute-done.6.refs_4_
  390.8 0.0 collective-permute-done.8.refs_6_
  390.8 0.0 collective-permute-done.7.refs_5_
  390.8 0.0 collective-permute-done.9.refs_7_
  390.8 4.7 %place.3 = f32[512,6144]{1,0:T(8,128)} custom-call(s32[8]{0:T(128)} %stack.62.rows_ref, bf16[32,6144]{1,0:T(8,128)(2,1)} %copy-done.2, bf16[32,6144]{1,0:T(8,128)(2,1)} %copy-done.8, bf16[32,6144]{1,0:T(8,128)(2,1)} %copy-done.4, bf16[32,6144]{1,0:T(8,128)(2,1)} %copy-done.9, ...), custom_call_target="tpu_custom_call", output_to_operand_aliasing={{}: (9, {})} | custom-call | bytes 9437184 | tf_op jit(solution)/shard_map/place/pallas_call | solution.py:71
  395.5 0.0 copy-done.11
  395.5 0.6 copy.37
  396.1 0.0 copy-done.1
  396.1 0.8 copy.38
  396.9 0.0 copy-done
  396.9 0.8 copy.39
  (6 shorter events, 0.0 us)
Async XLA Ops:
  326.7 11.5 %collective-permute-start.1 = (bf16[32,6144]{1,0:T(8,128)(2,1)}, bf16[32,6144]{1,0:T(8,128)(2,1)S(1)}, u32[]{:S(2)}, u32[]{:S(2)}) collective-permute-start(bf16[32,6144]{1,0:T(8,128)(2,1)} %get-tuple-element.46.refs_0_), channel_id=1, source_target_pairs={{0,2},{1,3},{2,0},{3,1},{4,6},{5,7},{6,4},{7,5},{8,10},{9,11},{10,... | collective-permute-start | bytes 1179656 | tf_op jit(solution)/shard_map/ppermute | solution.py:988
  328.4 12.2 %collective-permute-start.4 = (bf16[32,6144]{1,0:T(8,128)(2,1)}, bf16[32,6144]{1,0:T(8,128)(2,1)S(1)}, u32[]{:S(2)}, u32[]{:S(2)}) collective-permute-start(bf16[32,6144]{1,0:T(8,128)(2,1)} %get-tuple-element.47.refs_2_), channel_id=1, source_target_pairs={{0,4},{1,5},{2,6},{3,7},{4,0},{5,1},{6,2},{7,3},{8,12},{9,13},{10,... | collective-permute-start | bytes 1179656 | tf_op jit(solution)/shard_map/ppermute | solution.py:988
  328.7 11.8 %collective-permute-start.10 = (bf16[32,6144]{1,0:T(8,128)(2,1)}, bf16[32,6144]{1,0:T(8,128)(2,1)S(1)}, u32[]{:S(2)}, u32[]{:S(2)}) collective-permute-start(bf16[32,6144]{1,0:T(8,128)(2,1)} %get-tuple-element.46.refs_0_), channel_id=1, source_target_pairs={{0,1},{1,0},{2,3},{3,2},{4,5},{5,4},{6,7},{7,6},{8,9},{9,8},{10,11... | collective-permute-start | bytes 1179656 | tf_op jit(solution)/shard_map/ppermute | solution.py:988
  328.7 12.3 %collective-permute-start.12 = (bf16[32,6144]{1,0:T(8,128)(2,1)}, bf16[32,6144]{1,0:T(8,128)(2,1)S(1)}, u32[]{:S(2)}, u32[]{:S(2)}) collective-permute-start(bf16[32,6144]{1,0:T(8,128)(2,1)} %get-tuple-element.47.refs_2_), channel_id=1, source_target_pairs={{0,1},{1,0},{2,3},{3,2},{4,5},{5,4},{6,7},{7,6},{8,9},{9,8},{10,11... | collective-permute-start | bytes 1179656 | tf_op jit(solution)/shard_map/ppermute | solution.py:988
  329.2 19.8 %collective-permute-start = (bf16[32,6144]{1,0:T(8,128)(2,1)}, bf16[32,6144]{1,0:T(8,128)(2,1)S(1)}, u32[]{:S(2)}, u32[]{:S(2)}) collective-permute-start(bf16[32,6144]{1,0:T(8,128)(2,1)} %get-tuple-element.46.refs_0_), channel_id=1, source_target_pairs={{0,4},{1,5},{2,6},{3,7},{4,0},{5,1},{6,2},{7,3},{8,12},{9,13},{10,... | collective-permute-start | bytes 1179656 | tf_op jit(solution)/shard_map/ppermute | solution.py:988
  338.2 19.1 %copy-start.3 = (bf16[32,6144]{1,0:T(8,128)(2,1)}, bf16[32,6144]{1,0:T(8,128)(2,1)S(1)}, u32[]{:S(2)}) copy-start(bf16[32,6144]{1,0:T(8,128)(2,1)S(1)} %collective-permute-done.1.refs_1_) | copy-start | bytes 1179652
  338.2 12.2 %collective-permute-start.3 = (bf16[32,6144]{1,0:T(8,128)(2,1)}, bf16[32,6144]{1,0:T(8,128)(2,1)S(1)}, u32[]{:S(2)}, u32[]{:S(2)}) collective-permute-start(bf16[32,6144]{1,0:T(8,128)(2,1)} %get-tuple-element.47.refs_2_), channel_id=1, source_target_pairs={{0,2},{1,3},{2,0},{3,1},{4,6},{5,7},{6,4},{7,5},{8,10},{9,11},{10,... | collective-permute-start | bytes 1179656 | tf_op jit(solution)/shard_map/ppermute | solution.py:988
  340.6 16.8 %copy-start.5 = (bf16[32,6144]{1,0:T(8,128)(2,1)}, bf16[32,6144]{1,0:T(8,128)(2,1)S(1)}, u32[]{:S(2)}) copy-start(bf16[32,6144]{1,0:T(8,128)(2,1)S(1)} %collective-permute-done.4.refs_3_) | copy-start | bytes 1179652
  340.6 9.8 %collective-permute-start.11 = (bf16[32,6144]{1,0:T(8,128)(2,1)S(1)}, bf16[32,6144]{1,0:T(8,128)(2,1)S(1)}, u32[]{:S(2)}, u32[]{:S(2)}) collective-permute-start(bf16[32,6144]{1,0:T(8,128)(2,1)S(1)} %collective-permute-done.1.refs_1_), channel_id=1, source_target_pairs={{0,1},{1,0},{2,3},{3,2},{4,5},{5,4},{6,7},{7,6},{8,9},{9,8},{10,11... | collective-permute-start | bytes 1179656 | tf_op jit(solution)/shard_map/ppermute | solution.py:988
  340.6 16.8 %copy-start.6 = (bf16[32,6144]{1,0:T(8,128)(2,1)}, bf16[32,6144]{1,0:T(8,128)(2,1)S(1)}, u32[]{:S(2)}) copy-start(bf16[32,6144]{1,0:T(8,128)(2,1)S(1)} %collective-permute-done.10.refs_4_) | copy-start | bytes 1179652
  340.6 15.7 %collective-permute-start.2 = (bf16[32,6144]{1,0:T(8,128)(2,1)S(1)}, bf16[32,6144]{1,0:T(8,128)(2,1)S(1)}, u32[]{:S(2)}, u32[]{:S(2)}) collective-permute-start(bf16[32,6144]{1,0:T(8,128)(2,1)S(1)} %collective-permute-done.1.refs_1_), channel_id=1, source_target_pairs={{0,4},{1,5},{2,6},{3,7},{4,0},{5,1},{6,2},{7,3},{8,12},{9,13},{10,... | collective-permute-start | bytes 1179656 | tf_op jit(solution)/shard_map/ppermute | solution.py:988
  341.0 16.3 %copy-start.7 = (bf16[32,6144]{1,0:T(8,128)(2,1)}, bf16[32,6144]{1,0:T(8,128)(2,1)S(1)}, u32[]{:S(2)}) copy-start(bf16[32,6144]{1,0:T(8,128)(2,1)S(1)} %collective-permute-done.12.refs_6_) | copy-start | bytes 1179652
  341.0 16.2 %collective-permute-start.5 = (bf16[32,6144]{1,0:T(8,128)(2,1)S(1)}, bf16[32,6144]{1,0:T(8,128)(2,1)S(1)}, u32[]{:S(2)}, u32[]{:S(2)}) collective-permute-start(bf16[32,6144]{1,0:T(8,128)(2,1)S(1)} %collective-permute-done.4.refs_3_), channel_id=1, source_target_pairs={{0,2},{1,3},{2,0},{3,1},{4,6},{5,7},{6,4},{7,5},{8,10},{9,11},{10,... | collective-permute-start | bytes 1179656 | tf_op jit(solution)/shard_map/ppermute | solution.py:988
  349.0 8.4 %copy-start.2 = (bf16[32,6144]{1,0:T(8,128)(2,1)}, bf16[32,6144]{1,0:T(8,128)(2,1)S(1)}, u32[]{:S(2)}) copy-start(bf16[32,6144]{1,0:T(8,128)(2,1)S(1)} %collective-permute-done.refs_0_) | copy-start | bytes 1179652
  349.0 37.2 %collective-permute-start.13 = (bf16[32,6144]{1,0:T(8,128)(2,1)S(1)}, bf16[32,6144]{1,0:T(8,128)(2,1)}, u32[]{:S(2)}, u32[]{:S(2)}) collective-permute-start(bf16[32,6144]{1,0:T(8,128)(2,1)S(1)} %collective-permute-done.4.refs_3_), channel_id=1, source_target_pairs={{0,1},{1,0},{2,3},{3,2},{4,5},{5,4},{6,7},{7,6},{8,9},{9,8},{10,11... | collective-permute-start | bytes 1179656 | tf_op jit(solution)/shard_map/ppermute | solution.py:988
  350.4 7.0 %copy-start.4 = (bf16[32,6144]{1,0:T(8,128)(2,1)}, bf16[32,6144]{1,0:T(8,128)(2,1)S(1)}, u32[]{:S(2)}) copy-start(bf16[32,6144]{1,0:T(8,128)(2,1)S(1)} %collective-permute-done.3.refs_2_) | copy-start | bytes 1179652
  350.4 40.4 %collective-permute-start.6 = (bf16[32,6144]{1,0:T(8,128)(2,1)S(1)}, bf16[32,6144]{1,0:T(8,128)(2,1)}, u32[]{:S(2)}, u32[]{:S(2)}) collective-permute-start(bf16[32,6144]{1,0:T(8,128)(2,1)S(1)} %collective-permute-done.refs_0_), channel_id=1, source_target_pairs={{0,1},{1,0},{2,3},{3,2},{4,5},{5,4},{6,7},{7,6},{8,9},{9,8},{10,11... | collective-permute-start | bytes 1179656 | tf_op jit(solution)/shard_map/ppermute | solution.py:988
  350.4 6.8 %copy-start.10 = (bf16[32,6144]{1,0:T(8,128)(2,1)}, bf16[32,6144]{1,0:T(8,128)(2,1)S(1)}, u32[]{:S(2)}) copy-start(bf16[32,6144]{1,0:T(8,128)(2,1)S(1)} %collective-permute-done.11.refs_5_) | copy-start | bytes 1179652
  350.4 40.4 %collective-permute-start.8 = (bf16[32,6144]{1,0:T(8,128)(2,1)S(1)}, bf16[32,6144]{1,0:T(8,128)(2,1)}, u32[]{:S(2)}, u32[]{:S(2)}) collective-permute-start(bf16[32,6144]{1,0:T(8,128)(2,1)S(1)} %collective-permute-done.3.refs_2_), channel_id=1, source_target_pairs={{0,1},{1,0},{2,3},{3,2},{4,5},{5,4},{6,7},{7,6},{8,9},{9,8},{10,11... | collective-permute-start | bytes 1179656 | tf_op jit(solution)/shard_map/ppermute | solution.py:988
  356.3 1.1 copy-start.8
  356.3 34.5 %collective-permute-start.7 = (bf16[32,6144]{1,0:T(8,128)(2,1)S(1)}, bf16[32,6144]{1,0:T(8,128)(2,1)}, u32[]{:S(2)}, u32[]{:S(2)}) collective-permute-start(bf16[32,6144]{1,0:T(8,128)(2,1)S(1)} %collective-permute-done.2.refs_1_), channel_id=1, source_target_pairs={{0,1},{1,0},{2,3},{3,2},{4,5},{5,4},{6,7},{7,6},{8,9},{9,8},{10,11... | collective-permute-start | bytes 1179656 | tf_op jit(solution)/shard_map/ppermute | solution.py:988
  357.2 0.7 copy-start.9
  357.2 33.6 %collective-permute-start.9 = (bf16[32,6144]{1,0:T(8,128)(2,1)S(1)}, bf16[32,6144]{1,0:T(8,128)(2,1)}, u32[]{:S(2)}, u32[]{:S(2)}) collective-permute-start(bf16[32,6144]{1,0:T(8,128)(2,1)S(1)} %collective-permute-done.5.refs_3_), channel_id=1, source_target_pairs={{0,1},{1,0},{2,3},{3,2},{4,5},{5,4},{6,7},{7,6},{8,9},{9,8},{10,11... | collective-permute-start | bytes 1179656 | tf_op jit(solution)/shard_map/ppermute | solution.py:988
  359.3 36.2 %copy-start.11 = (f32[512]{0:T(512)}, f32[512]{0:T(512)S(1)}, u32[]{:S(2)}) copy-start(f32[512]{0:T(512)S(1)} %get-tuple-element.104) | copy-start | bytes 6148
  390.8 5.3 %copy-start.1 = (bf16[128,2048]{1,0:T(8,128)(2,1)S(1)}, bf16[128,2048]{1,0:T(8,128)(2,1)}, u32[]{:S(2)}) copy-start(bf16[128,2048]{1,0:T(8,128)(2,1)} %get-tuple-element.99) | copy-start | bytes 1572868
  390.8 6.1 %copy-start = (bf16[128,2048]{1,0:T(8,128)(2,1)S(1)}, bf16[128,2048]{1,0:T(8,128)(2,1)}, u32[]{:S(2)}) copy-start(bf16[128,2048]{1,0:T(8,128)(2,1)} %get-tuple-element.100) | copy-start | bytes 1572868
where the time goes:
time: 398 us
  Pallas kernels  356 us (89%)
  waiting for transfers between devices  22 us (6%)
  starting transfers between devices  8.51 us (2%)
  local copies, waits for them, and re-layouts  8.13 us (2%)
    pallas_call x1, Pallas kernels, grads(): pl.pallas_call(kernel, out_shape=outs, in_specs=[any_spec] * 12 + [vmem_s...  192 us
    pallas_call x1, Pallas kernels, layer(): pl.pallas_call(kernel, out_shape=outs, in_specs=[any_spec] * 7 + [vmem_sp...  132 us
    pallas_call x3, Pallas kernels, widen(): pl.pallas_call(kernel, grid=(rows // n,), in_specs=[spec], out_specs=spec...  22.9 us
    ppermute x14, waiting for transfers between devices, flip(): return lax.ppermute(value, 'replica', [(i, i ^ bit) for i in range(R)])  22 us
    pallas_call x2, Pallas kernels, place(): pl.pallas_call(kernel, in_specs=[pl.BlockSpec(memory_space=pltpu.SMEM)] +...  9.17 us
    ppermute x14, starting transfers between devices, flip(): return lax.ppermute(value, 'replica', [(i, i ^ bit) for i in range(R)])  8.51 us
  transfers between devices with their start and end apart: 14, of which 6 were waited for; matrix products, arithmetic and copies ran while one was open for 1% of the time, Pallas kernels for 7%

commit v1 on v0

--- a/solution.py
+++ b/solution.py
@@ -21,6 +21,13 @@
 def rotary_freqs():
     freqs = 10000.0 ** (-(np.arange(ROT // 2) * (2.0 / ROT)))
     return np.concatenate([freqs, freqs, np.zeros(128 - ROT)]).astype(np.float32).reshape(1, 128)
+
+
+def all_masks(bits):
+    out = [0]
+    for bit in bits:
+        out += [v | bit for v in out]
+    return sorted(out, key=lambda v: (v.bit_count(), v))
 
 
 def dot(left, right, left_dim, right_dim):
@@ -83,6 +90,30 @@
         cost_estimate=pl.CostEstimate(flops=0, bytes_accessed=6 * count * n * width, transcendentals=0),
         name="place",
     )(rows, *pieces, result)
+
+
+def input_grad(block_in, out_grad, own, others):
+    def kernel(block_ref, out_ref, own_ref, *refs):
+        wide = block_ref[...].astype(F32)
+        offsets = wide - jnp.mean(wide, axis=-1, keepdims=True)
+        inverse = lax.rsqrt(jnp.mean(offsets * offsets, axis=-1, keepdims=True) + epsilon)
+        normed = offsets * inverse
+        scaled = own_ref[...]
+        for ref in refs[:-1]:
+            scaled = scaled + ref[...].astype(F32)
+        term = inverse * (
+            scaled
+            - jnp.mean(scaled, axis=-1, keepdims=True)
+            - normed * jnp.mean(scaled * normed, axis=-1, keepdims=True)
+        )
+        refs[-1][...] = (out_ref[...].astype(F32) + term).astype(BF16)
+
+    return pl.pallas_call(
+        kernel,
+        out_shape=jax.ShapeDtypeStruct(block_in.shape, BF16),
+        cost_estimate=pl.CostEstimate(flops=0, bytes_accessed=8 * 2**20, transcendentals=0),
+        name="input_grad",
+    )(block_in, out_grad, own, *others)
 
 
 def unwritten(shape, dtype):
@@ -337,7 +368,11 @@
                     for m in plane:
                         shared(0, k, m).wait_recv()
 
-            @pl.when(i >= 2)
+            @pl.when(i == 1)
+            def _():
+                advance(2)
+
+            @pl.when(i >= 3)
             def _():
                 advance(i)
 
@@ -529,7 +564,7 @@
 
 
 def grads(
-    first, second, attended, activated, mixed, hidden, grad, branch, inner, sums, block_in, out_grad, bias, S, R, TP, DP
+    first, second, attended, activated, mixed, hidden, grad, branch, inner, sums, block_in, bias, S, R, TP, DP
 ):
     N, D = grad.shape
     T = block_in.shape[0]
@@ -559,9 +594,9 @@
 
     def kernel(
         second_hbm, first_hbm, activated_hbm, attended_hbm, hidden_hbm, mixed_hbm, grad_hbm, branch_hbm, inner_hbm, sums_hbm,
-        block_hbm, out_hbm, bias_ref,
-        whole_up, whole_down, whole_out, own_qkv_0, own_qkv_1, block_out, in_grad, sums_out,
-        own_up, own_down, own_out, block_v, out_v, near, near_came, far_came, held, held_came,
+        block_hbm, bias_ref,
+        whole_up, whole_out, own_down_0, own_down_1, own_qkv_0, own_qkv_1, block_out, inner_own, inner_rest, sums_out,
+        own_up, own_out, block_v, near, near_came, far_came, held, held_came,
         second_v, first_v, activated_v, attended_v, hidden_v, mixed_v, grad_v,
         part_up, part_qkv, part_down, part_out, came_up, came_qkv, came_down, came_out, all_up, all_qkv,
         load, dp_send, dp_recv, z_send, z_recv, near_send, near_recv, far_send, far_recv, held_send, held_recv,
@@ -586,17 +621,11 @@
         for i, (source, target) in enumerate(order):
             loads.append(pltpu.make_async_copy(source, target, load.at[i]))
         token_loads = [
-            pltpu.make_async_copy(
-                parts_hbm[i].at[t] if NT > 1 else parts_hbm[i].at[t, pl.ds(s, 1)], near.at[i], load.at[7 + i]
-            )
-            for i in range(2)
+            pltpu.make_async_copy(parts_hbm[i].at[t], near.at[i], load.at[7 + i]) for i in range(2)
         ]
         held_load = pltpu.make_async_copy(sums_hbm, held.at[0], load.at[9])
-        own_loads = [
-            pltpu.make_async_copy(block_hbm, block_v, load.at[16]),
-            pltpu.make_async_copy(out_hbm, out_v, load.at[17]),
-        ]
-        for copy in (loads[6], loads[4], *loads[:2], held_load, *token_loads, *loads[2:4], loads[5], *own_loads):
+        own_load = pltpu.make_async_copy(block_hbm, block_v, load.at[16])
+        for copy in (loads[6], loads[4], *loads[:2], held_load, *token_loads, *loads[2:4], loads[5], own_load):
             copy.start()
 
         group = [(k, m) for k in range(S) for m in range(NT) if k or m]
@@ -611,7 +640,7 @@
         right_refs = (hidden_v, mixed_v, grad_v, grad_v)
         part = (part_up, part_qkv, part_down, part_out)
         came = (came_up, came_qkv, came_down, came_out)
-        own = (own_up, (own_qkv_0, own_qkv_1), own_down, own_out)
+        own = (own_up, (own_qkv_0, own_qkv_1), (own_down_0, own_down_1), own_out)
 
         def product(i):
             lead, mid, n, _ = pieces[i]
@@ -703,7 +732,10 @@
                 else:
 
                     def write(l, c, value, h=h):
-                        own[i][h] = value
+                        if i == 2:
+                            own[i][h][...] = value
+                        else:
+                            own[i][h] = value
 
                 summed(i, h, 0, steps, write)
             if i < 2:
@@ -735,56 +767,50 @@
                 send_sem=near_send.at[i, m], recv_sem=near_recv.at[i, m], device_id=other(0, m), device_id_type=MESH,
             )
 
-        def far_copy(i, k):
+        def far_copy(k):
             there = lax.rem(s + k, S)
             return pltpu.make_async_remote_copy(
-                src_ref=near.at[i, there] if NT > 1 else parts_hbm[i].at[t, there], dst_ref=far_came.at[i, k - 1],
-                send_sem=far_send.at[i, k], recv_sem=far_recv.at[i, k], device_id=other(k, 0), device_id_type=MESH,
+                src_ref=near.at[0, there] if NT > 1 else branch_hbm.at[t, there], dst_ref=far_came.at[k - 1],
+                send_sem=far_send.at[k], recv_sem=far_recv.at[k], device_id=other(k, 0), device_id_type=MESH,
             )
 
         def near_sum(i, j):
-            value = near[i, j if NT > 1 else 0].astype(F32)
+            value = near[i, j].astype(F32)
             for m in range(1, NT):
                 value = value + near_came[i, m - 1, j].astype(F32)
             return value
 
-        def tokens_near(i):
+        def near_wait(i):
             token_loads[i].wait()
             for m in range(1, NT):
                 near_copy(i, m).wait_recv()
 
+        def branch_near():
+            near_wait(0)
+
             def body(k, carry):
                 j = lax.rem(s + k, S)
-                near[i, j] = near_sum(i, j).astype(BF16)
+                near[0, j] = near_sum(0, j).astype(BF16)
                 return carry
 
             if NT > 1:
                 lax.fori_loop(1, S, body, 0)
             for k in range(1, S):
-                far_copy(i, k).start()
-
-        def tokens_far(i):
-            value = near_sum(i, s)
+                far_copy(k).start()
+
+        def branch_far():
+            value = near_sum(0, s)
             for k in range(1, S):
-                far_copy(i, k).wait_recv()
-                value = value + far_came[i, k - 1].astype(F32)
-            return value
-
-        def finish():
-            for copy in own_loads:
-                copy.wait()
-            wide = block_v[...].astype(F32)
-            block_out[...] = (wide + tokens_far(0) + bias_ref[...]).astype(BF16)
-            offsets = wide - jnp.mean(wide, axis=-1, keepdims=True)
-            inverse = lax.rsqrt(jnp.mean(offsets * offsets, axis=-1, keepdims=True) + epsilon)
-            normed = offsets * inverse
-            scaled = tokens_far(1)
-            term = inverse * (
-                scaled
-                - jnp.mean(scaled, axis=-1, keepdims=True)
-                - normed * jnp.mean(scaled * normed, axis=-1, keepdims=True)
-            )
-            in_grad[...] = (out_v[...].astype(F32) + term).astype(BF16)
+                far_copy(k).wait_recv()
+                value = value + far_came[k - 1].astype(F32)
+            own_load.wait()
+            block_out[...] = (block_v[...].astype(F32) + value + bias_ref[...]).astype(BF16)
+
+        def inner_near():
+            near_wait(1)
+            inner_own[...] = near_sum(1, s)
+            for k in range(1, S):
+                inner_rest[k - 1] = near_sum(1, lax.rem(s + k, S)).astype(BF16)
 
         bits = [(0, bit) for bit in bits_of(R - 1)] + [(1, bit) for bit in bits_of(S - 1)]
 
@@ -805,8 +831,8 @@
             else:
                 sums_out[...] = value
 
-        wholes = {0: whole_up, 2: whole_down, 3: whole_out}
-        order_of = {0: 0, 2: 1, 3: 2}
+        wholes = {0: whole_up, 3: whole_out}
+        order_of = {0: 0, 3: 1}
 
         def slot_of(i, h, dd, tt):
             n = pieces[i][2]
@@ -858,7 +884,7 @@
         loads[1].wait()
         product(0)
         step(0, 0)
-        tokens_near(0)
+        branch_near()
         doubled(0)
         loads[2].wait()
         loads[3].wait()
@@ -880,24 +906,23 @@
         last(1)
         for j in range(1, steps):
             step(3, j)
-        tokens_near(1)
         collect(0)
         share_own(0)
         last(2)
-        share_own(2)
         last(3)
         share_own(3)
         for m in range(1, 1 << steps):
-            for i in (0, 2, 3):
+            for i in (0, 3):
                 share_on(i, m)
             if m == 1:
                 collect(1)
-                finish()
+                branch_far()
+                inner_near()
         for m in range(1 << steps, 1 << positions):
-            for i in (0, 2, 3):
+            for i in (0, 3):
                 share_on(i, m)
 
-        for i in (2, 3, 0):
+        for i in (3, 0):
             for h in range(2):
                 keep_own(i, h).wait()
                 for m in range(1 << positions):
@@ -906,8 +931,8 @@
         for i in range(2):
             for m in range(1, NT):
                 near_copy(i, m).wait_send()
-            for k in range(1, S):
-                far_copy(i, k).wait_send()
+        for k in range(1, S):
+            far_copy(k).wait_send()
         for i in range(len(bits)):
             double(i).wait_send()
         for i in range(4):
@@ -927,23 +952,23 @@
     operands = (second, first, activated, attended, hidden, mixed, grad)
     owns = [(2, n, width * S * NT if lead > 1 else width) for lead, _, n, width in pieces]
     wholes = [(2 * n * ND * NT, width) for _, n, width in owns]
-    outs = [jax.ShapeDtypeStruct(wholes[i], BF16) for i in (0, 2, 3)]
-    outs += [jax.ShapeDtypeStruct(owns[1][1:], BF16)] * 2 + [jax.ShapeDtypeStruct((T, D), BF16)] * 2
+    outs = [jax.ShapeDtypeStruct(wholes[i], BF16) for i in (0, 3)]
+    outs += [jax.ShapeDtypeStruct(owns[i][1:], BF16) for i in (2, 2, 1, 1)] + [jax.ShapeDtypeStruct((T, D), BF16)]
+    outs += [jax.ShapeDtypeStruct((T, D), F32), jax.ShapeDtypeStruct((S - 1, T, D), BF16)]
     outs += [jax.ShapeDtypeStruct(sums.shape, F32)]
     sent = sum(2 * (ND - 1) * a * b * n * w * 2 for a, b, n, w in pieces)
     count = len(bits_of(R - 1)) + len(bits_of(S - 1))
     return pl.pallas_call(
         kernel,
         out_shape=outs,
-        in_specs=[any_spec] * 12 + [vmem_spec],
-        out_specs=[any_spec] * 3 + [vmem_spec] * 5,
-        scratch_shapes=[pltpu.VMEM(owns[i], BF16) for i in (0, 2, 3)]
+        in_specs=[any_spec] * 11 + [vmem_spec],
+        out_specs=[any_spec] * 2 + [vmem_spec] * 8,
+        scratch_shapes=[pltpu.VMEM(owns[i], BF16) for i in (0, 3)]
         + [
             pltpu.VMEM((T, D), BF16),
-            pltpu.VMEM((T, D), BF16),
-            pltpu.VMEM((2, S if NT > 1 else 1, T, D), BF16),
+            pltpu.VMEM((2, S, T, D), BF16),
             pltpu.VMEM((2, NT - 1, S, T, D) if NT > 1 else (1, 1, 1, 16, 128), BF16),
-            pltpu.VMEM((2, S - 1, T, D), BF16),
+            pltpu.VMEM((S - 1, T, D), BF16),
             pltpu.VMEM((count,) + sums.shape, F32),
             pltpu.VMEM((count,) + sums.shape, F32),
         ]
@@ -959,12 +984,12 @@
             pltpu.SemaphoreType.DMA((2, 2, S, NT)),
             pltpu.SemaphoreType.DMA((2, NT)),
             pltpu.SemaphoreType.DMA((2, NT)),
-            pltpu.SemaphoreType.DMA((2, S)),
-            pltpu.SemaphoreType.DMA((2, S)),
+            pltpu.SemaphoreType.DMA((S,)),
+            pltpu.SemaphoreType.DMA((S,)),
             pltpu.SemaphoreType.DMA((count,)),
             pltpu.SemaphoreType.DMA((count,)),
-            pltpu.SemaphoreType.DMA((3, 2, ND * NT)),
-            pltpu.SemaphoreType.DMA((3, 2, ND * NT)),
+            pltpu.SemaphoreType.DMA((2, 2, ND * NT)),
+            pltpu.SemaphoreType.DMA((2, 2, ND * NT)),
         ],
         compiler_params=pltpu.CompilerParams(
             collective_id=1, has_side_effects=True, vmem_limit_bytes=67043328
@@ -974,7 +999,7 @@
             bytes_accessed=sent * 8, transcendentals=0,
         ),
         name="grads",
-    )(*operands, branch, inner, sums, block_in, out_grad, bias)
+    )(*operands, branch, inner, sums, block_in, bias)
 
 
 def solution(mesh):
@@ -993,6 +1018,7 @@
     ):
         T, D = block_in.shape
         FS = w_down.shape[0]
+        FD = FS // NT
         s = lax.axis_index("shard")
         r = lax.axis_index("replica")
         mine = {bit: (r // bit) % 2 for bit in bits_of(R - 1)}
@@ -1014,43 +1040,10 @@
         ]
         d = sum((mine[bit] * 2**i for i, bit in enumerate(DP)), jnp.int32(0))
 
-        whole_up, whole_down, whole_out, *own_qkv, block_out, in_grad, sums = grads(
+        whole_up, whole_out, *owned_rows, block_out, inner_own, inner_rest, sums = grads(
             first_low, second_low, attended, activated, mixed_low, hidden_low, grad_all, branch_part, inner_part,
-            sums, block_in, out_grad, bias, S, R, TP, DP,
+            sums, block_in, bias, S, R, TP, DP,
         )
-
-        ways = [DP + TP, DP[::-1] + TP]
-        n = own_qkv[0].shape[0]
-
-        def over(bit, value):
-            return flip(value, bit)
-
-        def placed(result, pieces):
-            at = []
-            for half, m, _ in pieces:
-                dmask = sum(2**i for i, bit in enumerate(DP) if m & bit)
-                tmask = sum(2**i for i, bit in enumerate(TP) if m & bit)
-                at.append(((d ^ dmask) * NT + (t ^ tmask)) * 2 * n + half * n)
-            return place([value for _, _, value in pieces], jnp.stack(at), result)
-
-        def with_partners(pieces):
-            for bit in TP:
-                pieces = pieces + [(half, m | bit, flip(value, bit)) for half, m, value in pieces]
-            return pieces
-
-        got = [{0: own_qkv[half]} for half in range(2)]
-        for i in range(len(DP)):
-            for half in range(2):
-                bit = ways[half][i]
-                got[half].update({m | bit: over(bit, v) for m, v in list(got[half].items())})
-        late = [ways[half][len(DP) - 1] for half in range(2)]
-        early = [(half, m, v) for half in range(2) for m, v in got[half].items() if not m & late[half]]
-        final = [(half, m, v) for half in range(2) for m, v in got[half].items() if m & late[half]]
-        grad_w_down = widen(whole_down)
-        grad_w_up = widen(whole_up)
-        grad_w_out = widen(whole_out)
-        grad_w_qkv = placed(unwritten(w_qkv.shape, F32), with_partners(early))
-        grad_w_qkv = placed(grad_w_qkv, with_partners(final))
 
         sums = sums.reshape(-1)
         width = w_out.shape[0] * S
@@ -1064,6 +1057,59 @@
         grad_b_out = owned(at[3], D)
         grad_b_up = owned(at[4], FS * S)
         smalls = [owned(at[5 + i], D) for i in range(4)]
+        whole_out, grad_b_qkv, grad_b_out, grad_b_up, smalls = lax.optimization_barrier(
+            (whole_out, grad_b_qkv, grad_b_out, grad_b_up, smalls)
+        )
+
+        ways = [DP, DP[::-1]]
+
+        def indices(m):
+            dmask = sum(2**i for i, bit in enumerate(DP) if m & bit)
+            tmask = sum(2**i for i, bit in enumerate(TP) if m & bit)
+            return d ^ dmask, t ^ tmask
+
+        def down_row(half, m, n):
+            dd, tt = indices(m)
+            return tt * FD + (dd * 2 + half) * n
+
+        def qkv_row(half, m, n):
+            dd, tt = indices(m)
+            return ((dd * NT + tt) * 2 + half) * n
+
+        def placed(result, pieces, row):
+            for bit in TP:
+                pieces = pieces + [(half, m | bit, flip(value, bit)) for half, m, value in pieces]
+            at = jnp.stack([row(half, m, value.shape[0]) for half, m, value in pieces])
+            return place([value for _, _, value in pieces], at, result)
+
+        got = [[{0: owned_rows[2 * i + half]} for half in range(2)] for i in range(2)]
+
+        def fetched(i, half, masks):
+            for m in masks:
+                bit = [b for b in ways[half] if m & b][-1]
+                got[i][half][m] = flip(got[i][half][m ^ bit], bit)
+
+        several = [m for m in all_masks(DP) if m and m not in DP]
+        for masks in (DP, several):
+            for i in range(2):
+                for half in range(2):
+                    fetched(i, half, masks)
+
+        def pieces_of(i, masks):
+            return [(half, m, got[i][half][m]) for half in range(2) for m in masks]
+
+        scaled = []
+        for k in range(1, S):
+            scaled.append(lax.ppermute(inner_rest[k - 1], "shard", [(i, (i + k) % S) for i in range(S)]))
+        in_grad = input_grad(block_in, out_grad, inner_own, scaled)
+        grad_w_up = widen(whole_up)
+        grad_w_out = widen(whole_out)
+        grad_w_down = placed(unwritten(w_down.shape, F32), pieces_of(0, [0] + DP), down_row)
+        grad_w_qkv = placed(unwritten(w_qkv.shape, F32), pieces_of(1, [0] + DP), qkv_row)
+        if several:
+            grad_w_down = placed(grad_w_down, pieces_of(0, several), down_row)
+            grad_w_qkv = placed(grad_w_qkv, pieces_of(1, several), qkv_row)
+
         return (
             block_out, in_grad, grad_w_qkv, grad_b_qkv, grad_w_out, grad_b_out, grad_w_up, grad_b_up,
             grad_w_down, grad_b_out, *smalls,

time: 398 us -> 441 us (1.11)
  the two profiles are of different devices: /device:TPU:0 before, /device:TPU:9 now
where the time goes in v1:
time: 441 us; the launch traced here: 440 us
  Pallas kernels  323 us (73%)
  waiting for transfers between devices  76.3 us (17%)
  starting transfers between devices  28.2 us (6%)
  local copies, waits for them, and re-layouts  8.62 us (2%)
    pallas_call x1, Pallas kernels, grads(): pl.pallas_call(kernel, out_shape=outs, in_specs=[any_spec] * 11 + [vmem_s...  163 us
    pallas_call x1, Pallas kernels, layer(): pl.pallas_call(kernel, out_shape=outs, in_specs=[any_spec] * 7 + [vmem_sp...  122 us
    ppermute x28, waiting for transfers between devices, flip(): return lax.ppermute(value, 'replica', [(i, i ^ bit) for i in range(R)])  43.4 us
    ppermute x3, waiting for transfers between devices, body(): lax.ppermute(inner_rest[k - 1], 'shard', [(i, (i + k) % S) for i in range...  32.9 us
    ppermute x28, starting transfers between devices, flip(): return lax.ppermute(value, 'replica', [(i, i ^ bit) for i in range(R)])  26.4 us
    pallas_call x4, Pallas kernels, place(): pl.pallas_call(kernel, in_specs=[pl.BlockSpec(memory_space=pltpu.SMEM)] +...  19.8 us
    pallas_call x2, Pallas kernels, widen(): pl.pallas_call(kernel, grid=(rows // n,), in_specs=[spec], out_specs=spec...  13.4 us
  transfers between devices with their start and end apart: 31, of which 9 were waited for; matrix products, arithmetic and copies ran while one was open for 2% of the time, Pallas kernels for 7%

profile of v1, /device:TPU:9, one launch (start us, length us, event | category | flops | bytes accessed | tf_op | source)
XLA Modules:
  0.0 440.0 jit_solution(14248541469298951168)
XLA Ops:
  0.6 0.7 convert_element_type.3
  1.3 1.4 add_bitcast_fusion.small_ref
  2.7 122.5 %layer.1 = (bf16[2,4,128,2048]{3,2,1,0:T(8,128)(2,1)}, bf16[2,4,128,2048]{3,2,1,0:T(8,128)(2,1)}, bf16[2,4,128,256]{3,2,1,0:T(8,128)(2,1)}, bf16[2,4,128,1024]{3...) custom-call(bf16[53,128]{1,0:T(8,128)(2,1)} %add_bitcast_fusion.smal, ...), custom_call_target="tpu_custom_call" | custom-call | flops 25769803776 | bytes 83886080 | tf_op jit(solution)/shard_map/layer/pallas_call | solution.py:524
  125.2 163.3 %grads.1 = (bf16[512,8192]{1,0:T(8,128)(2,1)}, bf16[512,2048]{1,0:T(8,128)(2,1)}, bf16[128,2048]{1,0:T(8,128)(2,1)}, bf16[128,2048]{1,0:T(8,128)(2,1)}, bf16[32,...) custom-call(bf16[1024,2048]{1,0:T(8,128)(2,1)} %bitcast.52, ...), custom_call_target="tpu_custom_call" | custom-call | flops 12884901888 | bytes 75497472 | tf_op jit(solution)/shard_map/grads/pallas_call | solution.py:961
  288.5 1.1 collective-permute-start.3
  289.6 0.4 collective-permute-start.5
  290.1 1.0 collective-permute-start.9
  291.1 0.4 collective-permute-start.10
  291.5 1.2 collective-permute-start.11
  292.7 6.6 %collective-permute-done.3.refs_1_ = bf16[32,6144]{1,0:T(8,128)(2,1)S(1)} collective-permute-done((bf16[32,6144]{1,0:T(8,128)(2,1)}, bf16[32,6144]{1,0:T(8,128)(2,1)S(1)}, u32[]{:S(2)}, u32[]{:S(2)}) %collective-permute-start.3) | collective-permute-done | bytes 393248 | tf_op jit(solution)/shard_map/ppermute | solution.py:1013
  299.3 1.5 collective-permute-start.14
  300.9 1.1 collective-permute-start.17
  301.9 6.6 %collective-permute-done.9.refs_2_ = bf16[32,6144]{1,0:T(8,128)(2,1)S(1)} collective-permute-done((bf16[32,6144]{1,0:T(8,128)(2,1)}, bf16[32,6144]{1,0:T(8,128)(2,1)S(1)}, u32[]{:S(2)}, u32[]{:S(2)}) %collective-permute-start.9) | collective-permute-done | bytes 393248 | tf_op jit(solution)/shard_map/ppermute | solution.py:1013
  308.5 0.5 collective-permute-start.19
  309.0 0.0 collective-permute-done.10.refs_4_
  309.0 1.0 collective-permute-start.23
  310.0 0.4 collective-permute-start.24
  310.4 2.1 collective-permute-start.25
  312.5 1.5 slice_bitcast_fusion
  314.1 4.9 %collective-permute-done.17.refs_1_ = bf16[128,2048]{1,0:T(8,128)(2,1)S(1)} collective-permute-done((bf16[128,2048]{1,0:T(8,128)(2,1)}, bf16[128,2048]{1,0:T(8,128)(2,1)S(1)}, u32[]{:S(2)}, u32[]{:S(2)}) %collective-permute-start.17) | collective-permute-done | bytes 524320 | tf_op jit(solution)/shard_map/ppermute | solution.py:1013
  319.0 1.5 collective-permute-start.28
  320.5 0.4 collective-permute-done.19.refs_5_
  321.0 0.3 collective-permute-start
  321.2 10.9 %collective-permute-done.23.refs_2_ = bf16[128,2048]{1,0:T(8,128)(2,1)S(1)} collective-permute-done((bf16[128,2048]{1,0:T(8,128)(2,1)}, bf16[128,2048]{1,0:T(8,128)(2,1)S(1)}, u32[]{:S(2)}, u32[]{:S(2)}) %collective-permute-start.23) | collective-permute-done | bytes 524320 | tf_op jit(solution)/shard_map/ppermute | solution.py:1013
  332.2 1.4 collective-permute-start.1
  333.6 0.0 collective-permute-start.2
  333.7 2.7 collective-permute-start.12
  336.4 0.1 collective-permute-start.16
  336.5 0.4 collective-permute-start.13
  336.9 30.6 %collective-permute-done.1.refs_1_ = bf16[128,2048]{1,0:T(8,128)(2,1)S(1)} collective-permute-done((bf16[128,2048]{1,0:T(8,128)(2,1)S(1)}, bf16[128,2048]{1,0:T(8,128)(2,1)S(1)}, u32[]{:S(2)}, u32[]{:S(2)}) %collective-permute-start.1) | collective-permute-done | bytes 524320 | tf_op jit(solution)/shard_map/ppermute | solution.py:1103
  367.5 0.5 collective-permute-start.15
  368.0 2.3 collective-permute-done.2.refs_2_
  370.3 0.9 collective-permute-start.4
  371.2 0.8 collective-permute-start.6
  372.0 1.1 collective-permute-start.26
  373.1 0.4 collective-permute-start.18
  373.6 0.8 collective-permute-start.20
  374.4 6.2 %collective-permute-done.4.refs_0_ = bf16[32,6144]{1,0:T(8,128)(2,1)} collective-permute-done((bf16[32,6144]{1,0:T(8,128)(2,1)S(1)}, bf16[32,6144]{1,0:T(8,128)(2,1)}, u32[]{:S(2)}, u32[]{:S(2)}) %collective-permute-start.4) | collective-permute-done | bytes 393248 | tf_op jit(solution)/shard_map/ppermute | solution.py:1013
  380.6 2.3 collective-permute-start.30
  382.9 1.2 collective-permute-start.27
  384.1 0.1 collective-permute-start.29
  384.1 7.7 %collective-permute-done.18.refs_0_ = bf16[128,2048]{1,0:T(8,128)(2,1)} collective-permute-done((bf16[128,2048]{1,0:T(8,128)(2,1)S(1)}, bf16[128,2048]{1,0:T(8,128)(2,1)}, u32[]{:S(2)}, u32[]{:S(2)}) %collective-permute-start.18) | collective-permute-done | bytes 524320 | tf_op jit(solution)/shard_map/ppermute | solution.py:1013
  391.8 1.3 collective-permute-start.21
  393.2 0.9 collective-permute-start.22
  394.1 0.1 collective-permute-start.7
  394.1 0.5 collective-permute-start.8
  394.7 0.2 copy-done.7
  394.9 0.2 copy-done.8
  395.1 1.4 dynamic_slice.21
  396.5 1.3 dynamic_slice.23
  397.8 1.4 fusion
  399.2 3.9 widen.2
  403.1 9.5 %widen.3 = f32[512,8192]{1,0:T(8,128)} custom-call(bf16[512,8192]{1,0:T(8,128)(2,1)} %get-tuple-element.64.in_ref), custom_call_target="tpu_custom_call" | custom-call | bytes 25165824 | tf_op jit(solution)/shard_map/widen/pallas_call | solution.py:47
  412.6 0.6 stack.143.rows_ref
  413.2 0.7 stack.125.rows_ref
  413.8 0.7 pad_add_fusion.1.rows_ref
  414.5 0.6 pad_add_fusion.rows_ref
  415.1 3.6 input_grad.1
  418.8 5.5 %place.4.refs_4_ = f32[512,6144]{1,0:T(8,128)} custom-call(s32[12]{0:T(128)} %stack.125.rows_ref, bf16[32,6144]{1,0:T(8,128)(2,1)} %get-tuple-element.57.refs_0_, bf16[32,6144]{1,0:T(8,128)(2,1)} %copy-done.13, bf16[32,6144]{1,0:T(8,128)(2,1)} %copy-done.15, bf16[32,6144]{1,0:T(8,128)(2,1)} %get-tuple-element.58.refs_3_, ...), custom_call_target="tpu_custom_call", output_to_operand_aliasing={{}: (13, {})} | custom-call | bytes 14155776 | tf_op jit(solution)/shard_map/place/pallas_call | solution.py:78
  424.3 6.8 %place.6.refs_4_ = f32[2048,2048]{1,0:T(8,128)} custom-call(s32[12]{0:T(128)} %stack.143.rows_ref, bf16[128,2048]{1,0:T(8,128)(2,1)} %get-tuple-element.66.refs_0_, bf16[128,2048]{1,0:T(8,128)(2,1)} %copy-done, bf16[128,2048]{1,0:T(8,128)(2,1)} %copy-done.2, bf16[128,2048]{1,0:T(8,128)(2,1)} %get-tuple-element.67.refs_3_, ...), custom_call_target="tpu_custom_call", output_to_operand_aliasing={{}: (13, {})} | custom-call | bytes 18874368 | tf_op jit(solution)/shard_map/place/pallas_call | solution.py:78
  431.2 3.4 place.5
  434.6 4.0 place.7
  438.6 0.6 copy.40
  439.2 0.8 copy.41
  (65 shorter events, 0.1 us)
Async XLA Ops:
  288.5 10.8 %collective-permute-start.3 = (bf16[32,6144]{1,0:T(8,128)(2,1)}, bf16[32,6144]{1,0:T(8,128)(2,1)S(1)}, u32[]{:S(2)}, u32[]{:S(2)}) collective-permute-start(bf16[32,6144]{1,0:T(8,128)(2,1)} %get-tuple-element.57.refs_0_), channel_id=1, source_target_pairs={{0,2},{1,3},{2,0},{3,1},{4,6},{5,7},{6,4},{7,5},{8,10},{9,11},{10,... | collective-permute-start | bytes 1179656 | tf_op jit(solution)/shard_map/ppermute | solution.py:1013
  289.6 11.3 %collective-permute-start.5 = (bf16[32,6144]{1,0:T(8,128)(2,1)}, bf16[32,6144]{1,0:T(8,128)(2,1)S(1)}, u32[]{:S(2)}, u32[]{:S(2)}) collective-permute-start(bf16[32,6144]{1,0:T(8,128)(2,1)} %get-tuple-element.58.refs_3_), channel_id=1, source_target_pairs={{0,4},{1,5},{2,6},{3,7},{4,0},{5,1},{6,2},{7,3},{8,12},{9,13},{10,... | collective-permute-start | bytes 1179656 | tf_op jit(solution)/shard_map/ppermute | solution.py:1013
  290.1 18.5 %collective-permute-start.9 = (bf16[32,6144]{1,0:T(8,128)(2,1)}, bf16[32,6144]{1,0:T(8,128)(2,1)S(1)}, u32[]{:S(2)}, u32[]{:S(2)}) collective-permute-start(bf16[32,6144]{1,0:T(8,128)(2,1)} %get-tuple-element.57.refs_0_), channel_id=1, source_target_pairs={{0,4},{1,5},{2,6},{3,7},{4,0},{5,1},{6,2},{7,3},{8,12},{9,13},{10,... | collective-permute-start | bytes 1179656 | tf_op jit(solution)/shard_map/ppermute | solution.py:1013
  291.1 17.9 %collective-permute-start.10 = (bf16[32,6144]{1,0:T(8,128)(2,1)}, bf16[32,6144]{1,0:T(8,128)(2,1)S(1)}, u32[]{:S(2)}, u32[]{:S(2)}) collective-permute-start(bf16[32,6144]{1,0:T(8,128)(2,1)} %get-tuple-element.58.refs_3_), channel_id=1, source_target_pairs={{0,2},{1,3},{2,0},{3,1},{4,6},{5,7},{6,4},{7,5},{8,10},{9,11},{10,... | collective-permute-start | bytes 1179656 | tf_op jit(solution)/shard_map/ppermute | solution.py:1013
  291.5 18.5 %collective-permute-start.11 = (bf16[32,6144]{1,0:T(8,128)(2,1)}, bf16[32,6144]{1,0:T(8,128)(2,1)}, u32[]{:S(2)}, u32[]{:S(2)}) collective-permute-start(bf16[32,6144]{1,0:T(8,128)(2,1)} %get-tuple-element.57.refs_0_), channel_id=1, source_target_pairs={{0,1},{1,0},{2,3},{3,2},{4,5},{5,4},{6,7},{7,6},{8,9},{9,8},{10,11... | collective-permute-start | bytes 1179656 | tf_op jit(solution)/shard_map/ppermute | solution.py:1013
  299.3 95.7 %copy-start.13 = (bf16[32,6144]{1,0:T(8,128)(2,1)}, bf16[32,6144]{1,0:T(8,128)(2,1)S(1)}, u32[]{:S(2)}) copy-start(bf16[32,6144]{1,0:T(8,128)(2,1)S(1)} %collective-permute-done.3.refs_1_) | copy-start | bytes 1179652
  299.3 11.1 %collective-permute-start.14 = (bf16[32,6144]{1,0:T(8,128)(2,1)}, bf16[32,6144]{1,0:T(8,128)(2,1)}, u32[]{:S(2)}, u32[]{:S(2)}) collective-permute-start(bf16[32,6144]{1,0:T(8,128)(2,1)} %get-tuple-element.58.refs_3_), channel_id=1, source_target_pairs={{0,1},{1,0},{2,3},{3,2},{4,5},{5,4},{6,7},{7,6},{8,9},{9,8},{10,11... | collective-permute-start | bytes 1179656 | tf_op jit(solution)/shard_map/ppermute | solution.py:1013
  300.9 93.8 %copy-start.14 = (bf16[32,6144]{1,0:T(8,128)(2,1)}, bf16[32,6144]{1,0:T(8,128)(2,1)S(1)}, u32[]{:S(2)}) copy-start(bf16[32,6144]{1,0:T(8,128)(2,1)S(1)} %collective-permute-done.5.refs_5_) | copy-start | bytes 1179652
  300.9 18.1 %collective-permute-start.17 = (bf16[128,2048]{1,0:T(8,128)(2,1)}, bf16[128,2048]{1,0:T(8,128)(2,1)S(1)}, u32[]{:S(2)}, u32[]{:S(2)}) collective-permute-start(bf16[128,2048]{1,0:T(8,128)(2,1)} %get-tuple-element.66.refs_0_), channel_id=1, source_target_pairs={{0,2},{1,3},{2,0},{3,1},{4,6},{5,7},{6,4},{7,5},{8,10},{9,11},{10,... | collective-permute-start | bytes 1572872 | tf_op jit(solution)/shard_map/ppermute | solution.py:1013
  308.5 86.1 %copy-start.15 = (bf16[32,6144]{1,0:T(8,128)(2,1)}, bf16[32,6144]{1,0:T(8,128)(2,1)S(1)}, u32[]{:S(2)}) copy-start(bf16[32,6144]{1,0:T(8,128)(2,1)S(1)} %collective-permute-done.9.refs_2_) | copy-start | bytes 1179652
  308.5 12.4 %collective-permute-start.19 = (bf16[128,2048]{1,0:T(8,128)(2,1)}, bf16[128,2048]{1,0:T(8,128)(2,1)S(1)}, u32[]{:S(2)}, u32[]{:S(2)}) collective-permute-start(bf16[128,2048]{1,0:T(8,128)(2,1)} %get-tuple-element.67.refs_3_), channel_id=1, source_target_pairs={{0,4},{1,5},{2,6},{3,7},{4,0},{5,1},{6,2},{7,3},{8,12},{9,13},{10,... | collective-permute-start | bytes 1572872 | tf_op jit(solution)/shard_map/ppermute | solution.py:1013
  309.0 85.7 %copy-start.16 = (bf16[32,6144]{1,0:T(8,128)(2,1)}, bf16[32,6144]{1,0:T(8,128)(2,1)S(1)}, u32[]{:S(2)}) copy-start(bf16[32,6144]{1,0:T(8,128)(2,1)S(1)} %collective-permute-done.10.refs_4_) | copy-start | bytes 1179652
  309.0 23.2 %collective-permute-start.23 = (bf16[128,2048]{1,0:T(8,128)(2,1)}, bf16[128,2048]{1,0:T(8,128)(2,1)S(1)}, u32[]{:S(2)}, u32[]{:S(2)}) collective-permute-start(bf16[128,2048]{1,0:T(8,128)(2,1)} %get-tuple-element.66.refs_0_), channel_id=1, source_target_pairs={{0,4},{1,5},{2,6},{3,7},{4,0},{5,1},{6,2},{7,3},{8,12},{9,13},{10,... | collective-permute-start | bytes 1572872 | tf_op jit(solution)/shard_map/ppermute | solution.py:1013
  310.0 23.6 %collective-permute-start.24 = (bf16[128,2048]{1,0:T(8,128)(2,1)}, bf16[128,2048]{1,0:T(8,128)(2,1)S(1)}, u32[]{:S(2)}, u32[]{:S(2)}) collective-permute-start(bf16[128,2048]{1,0:T(8,128)(2,1)} %get-tuple-element.67.refs_3_), channel_id=1, source_target_pairs={{0,2},{1,3},{2,0},{3,1},{4,6},{5,7},{6,4},{7,5},{8,10},{9,11},{10,... | collective-permute-start | bytes 1572872 | tf_op jit(solution)/shard_map/ppermute | solution.py:1013
  310.4 23.2 %collective-permute-start.25 = (bf16[128,2048]{1,0:T(8,128)(2,1)}, bf16[128,2048]{1,0:T(8,128)(2,1)S(1)}, u32[]{:S(2)}, u32[]{:S(2)}) collective-permute-start(bf16[128,2048]{1,0:T(8,128)(2,1)} %get-tuple-element.66.refs_0_), channel_id=1, source_target_pairs={{0,1},{1,0},{2,3},{3,2},{4,5},{5,4},{6,7},{7,6},{8,9},{9,8},{10,11... | collective-permute-start | bytes 1572872 | tf_op jit(solution)/shard_map/ppermute | solution.py:1013
  319.0 76.0 %copy-start = (bf16[128,2048]{1,0:T(8,128)(2,1)}, bf16[128,2048]{1,0:T(8,128)(2,1)S(1)}, u32[]{:S(2)}) copy-start(bf16[128,2048]{1,0:T(8,128)(2,1)S(1)} %collective-permute-done.17.refs_1_) | copy-start | bytes 1572868
  319.0 17.4 %collective-permute-start.28 = (bf16[128,2048]{1,0:T(8,128)(2,1)}, bf16[128,2048]{1,0:T(8,128)(2,1)S(1)}, u32[]{:S(2)}, u32[]{:S(2)}) collective-permute-start(bf16[128,2048]{1,0:T(8,128)(2,1)} %get-tuple-element.67.refs_3_), channel_id=1, source_target_pairs={{0,1},{1,0},{2,3},{3,2},{4,5},{5,4},{6,7},{7,6},{8,9},{9,8},{10,11... | collective-permute-start | bytes 1572872 | tf_op jit(solution)/shard_map/ppermute | solution.py:1013
  320.9 74.1 %copy-start.1 = (bf16[128,2048]{1,0:T(8,128)(2,1)}, bf16[128,2048]{1,0:T(8,128)(2,1)S(1)}, u32[]{:S(2)}) copy-start(bf16[128,2048]{1,0:T(8,128)(2,1)S(1)} %collective-permute-done.19.refs_5_) | copy-start | bytes 1572868
  321.0 15.5 %collective-permute-start = (bf16[128,2048]{1,0:T(8,128)(2,1)S(1)}, bf16[128,2048]{1,0:T(8,128)(2,1)S(1)}, u32[]{:S(2)}, u32[]{:S(2)}) collective-permute-start(bf16[128,2048]{1,0:T(8,128)(2,1)S(1)} %get-tuple-element.74), channel_id=1, source_target_pairs={{0,8},{8,16},{16,24},{24,0},{1,9},{9,17},{17,25},{25,1},{2,10},{10... | collective-permute-start | bytes 1572872 | tf_op jit(solution)/shard_map/ppermute | solution.py:1103
  332.2 62.9 %copy-start.2 = (bf16[128,2048]{1,0:T(8,128)(2,1)}, bf16[128,2048]{1,0:T(8,128)(2,1)S(1)}, u32[]{:S(2)}) copy-start(bf16[128,2048]{1,0:T(8,128)(2,1)S(1)} %collective-permute-done.23.refs_2_) | copy-start | bytes 1572868
  332.2 35.3 %collective-permute-start.1 = (bf16[128,2048]{1,0:T(8,128)(2,1)S(1)}, bf16[128,2048]{1,0:T(8,128)(2,1)S(1)}, u32[]{:S(2)}, u32[]{:S(2)}) collective-permute-start(bf16[128,2048]{1,0:T(8,128)(2,1)S(1)} %get-tuple-element.73), channel_id=1, source_target_pairs={{0,16},{8,24},{16,0},{24,8},{1,17},{9,25},{17,1},{25,9},{2,18},{10... | collective-permute-start | bytes 1572872 | tf_op jit(solution)/shard_map/ppermute | solution.py:1103
  333.6 61.4 %copy-start.3 = (bf16[128,2048]{1,0:T(8,128)(2,1)}, bf16[128,2048]{1,0:T(8,128)(2,1)S(1)}, u32[]{:S(2)}) copy-start(bf16[128,2048]{1,0:T(8,128)(2,1)S(1)} %collective-permute-done.24.refs_4_) | copy-start | bytes 1572868
  333.6 36.7 %collective-permute-start.2 = (bf16[128,2048]{1,0:T(8,128)(2,1)S(1)}, bf16[128,2048]{1,0:T(8,128)(2,1)S(1)}, u32[]{:S(2)}, u32[]{:S(2)}) collective-permute-start(bf16[128,2048]{1,0:T(8,128)(2,1)S(1)} %get-tuple-element.72), channel_id=1, source_target_pairs={{0,24},{8,0},{16,8},{24,16},{1,25},{9,1},{17,9},{25,17},{2,26},{10... | collective-permute-start | bytes 1572872 | tf_op jit(solution)/shard_map/ppermute | solution.py:1103
  333.7 61.4 %copy-start.4 = (bf16[128,2048]{1,0:T(8,128)(2,1)}, bf16[128,2048]{1,0:T(8,128)(2,1)S(1)}, u32[]{:S(2)}) copy-start(bf16[128,2048]{1,0:T(8,128)(2,1)S(1)} %collective-permute-done.25.refs_6_) | copy-start | bytes 1572868
  333.7 37.5 %collective-permute-start.12 = (bf16[32,6144]{1,0:T(8,128)(2,1)S(1)}, bf16[32,6144]{1,0:T(8,128)(2,1)S(1)}, u32[]{:S(2)}, u32[]{:S(2)}) collective-permute-start(bf16[32,6144]{1,0:T(8,128)(2,1)S(1)} %collective-permute-done.3.refs_1_), channel_id=1, source_target_pairs={{0,1},{1,0},{2,3},{3,2},{4,5},{5,4},{6,7},{7,6},{8,9},{9,8},{10,11... | collective-permute-start | bytes 1179656 | tf_op jit(solution)/shard_map/ppermute | solution.py:1013
  336.4 58.7 %copy-start.5 = (bf16[128,2048]{1,0:T(8,128)(2,1)}, bf16[128,2048]{1,0:T(8,128)(2,1)S(1)}, u32[]{:S(2)}) copy-start(bf16[128,2048]{1,0:T(8,128)(2,1)S(1)} %collective-permute-done.28.refs_9_) | copy-start | bytes 1572868
  336.4 35.6 %collective-permute-start.16 = (bf16[32,6144]{1,0:T(8,128)(2,1)S(1)}, bf16[32,6144]{1,0:T(8,128)(2,1)S(1)}, u32[]{:S(2)}, u32[]{:S(2)}) collective-permute-start(bf16[32,6144]{1,0:T(8,128)(2,1)S(1)} %collective-permute-done.5.refs_5_), channel_id=1, source_target_pairs={{0,1},{1,0},{2,3},{3,2},{4,5},{5,4},{6,7},{7,6},{8,9},{9,8},{10,11... | collective-permute-start | bytes 1179656 | tf_op jit(solution)/shard_map/ppermute | solution.py:1013
  336.5 35.5 %copy-start.10 = (bf16[128,2048]{1,0:T(8,128)(2,1)}, bf16[128,2048]{1,0:T(8,128)(2,1)S(1)}, u32[]{:S(2)}) copy-start(bf16[128,2048]{1,0:T(8,128)(2,1)S(1)} %collective-permute-done.refs_0_) | copy-start | bytes 1572868
  336.5 36.6 %collective-permute-start.13 = (bf16[32,6144]{1,0:T(8,128)(2,1)S(1)}, bf16[32,6144]{1,0:T(8,128)(2,1)S(1)}, u32[]{:S(2)}, u32[]{:S(2)}) collective-permute-start(bf16[32,6144]{1,0:T(8,128)(2,1)S(1)} %collective-permute-done.9.refs_2_), channel_id=1, source_target_pairs={{0,1},{1,0},{2,3},{3,2},{4,5},{5,4},{6,7},{7,6},{8,9},{9,8},{10,11... | collective-permute-start | bytes 1179656 | tf_op jit(solution)/shard_map/ppermute | solution.py:1013
  367.5 6.9 %copy-start.11 = (bf16[128,2048]{1,0:T(8,128)(2,1)}, bf16[128,2048]{1,0:T(8,128)(2,1)S(1)}, u32[]{:S(2)}) copy-start(bf16[128,2048]{1,0:T(8,128)(2,1)S(1)} %collective-permute-done.1.refs_1_) | copy-start | bytes 1572868
  367.5 6.1 %collective-permute-start.15 = (bf16[32,6144]{1,0:T(8,128)(2,1)S(1)}, bf16[32,6144]{1,0:T(8,128)(2,1)S(1)}, u32[]{:S(2)}, u32[]{:S(2)}) collective-permute-start(bf16[32,6144]{1,0:T(8,128)(2,1)S(1)} %collective-permute-done.10.refs_4_), channel_id=1, source_target_pairs={{0,1},{1,0},{2,3},{3,2},{4,5},{5,4},{6,7},{7,6},{8,9},{9,8},{10,11... | collective-permute-start | bytes 1179656 | tf_op jit(solution)/shard_map/ppermute | solution.py:1013
  370.3 12.6 %copy-start.12 = (bf16[128,2048]{1,0:T(8,128)(2,1)}, bf16[128,2048]{1,0:T(8,128)(2,1)S(1)}, u32[]{:S(2)}) copy-start(bf16[128,2048]{1,0:T(8,128)(2,1)S(1)} %collective-permute-done.2.refs_2_) | copy-start | bytes 1572868
  370.3 10.3 %collective-permute-start.4 = (bf16[32,6144]{1,0:T(8,128)(2,1)S(1)}, bf16[32,6144]{1,0:T(8,128)(2,1)}, u32[]{:S(2)}, u32[]{:S(2)}) collective-permute-start(bf16[32,6144]{1,0:T(8,128)(2,1)S(1)} %collective-permute-done.3.refs_1_), channel_id=1, source_target_pairs={{0,4},{1,5},{2,6},{3,7},{4,0},{5,1},{6,2},{7,3},{8,12},{9,13},{10,... | collective-permute-start | bytes 1179656 | tf_op jit(solution)/shard_map/ppermute | solution.py:1013
  371.2 23.5 %copy-start.17 = (bf16[32,6144]{1,0:T(8,128)(2,1)}, bf16[32,6144]{1,0:T(8,128)(2,1)S(1)}, u32[]{:S(2)}) copy-start(bf16[32,6144]{1,0:T(8,128)(2,1)S(1)} %collective-permute-done.12.refs_7_) | copy-start | bytes 1179652
  371.2 11.7 %collective-permute-start.6 = (bf16[32,6144]{1,0:T(8,128)(2,1)S(1)}, bf16[32,6144]{1,0:T(8,128)(2,1)}, u32[]{:S(2)}, u32[]{:S(2)}) collective-permute-start(bf16[32,6144]{1,0:T(8,128)(2,1)S(1)} %collective-permute-done.5.refs_5_), channel_id=1, source_target_pairs={{0,2},{1,3},{2,0},{3,1},{4,6},{5,7},{6,4},{7,5},{8,10},{9,11},{10,... | collective-permute-start | bytes 1179656 | tf_op jit(solution)/shard_map/ppermute | solution.py:1013
  372.0 22.7 %copy-start.18 = (bf16[32,6144]{1,0:T(8,128)(2,1)}, bf16[32,6144]{1,0:T(8,128)(2,1)S(1)}, u32[]{:S(2)}) copy-start(bf16[32,6144]{1,0:T(8,128)(2,1)S(1)} %collective-permute-done.16.refs_11_) | copy-start | bytes 1179652
  372.0 12.1 %collective-permute-start.26 = (bf16[128,2048]{1,0:T(8,128)(2,1)S(1)}, bf16[128,2048]{1,0:T(8,128)(2,1)S(1)}, u32[]{:S(2)}, u32[]{:S(2)}) collective-permute-start(bf16[128,2048]{1,0:T(8,128)(2,1)S(1)} %collective-permute-done.17.refs_1_), channel_id=1, source_target_pairs={{0,1},{1,0},{2,3},{3,2},{4,5},{5,4},{6,7},{7,6},{8,9},{9,8},{10,11... | collective-permute-start | bytes 1572872 | tf_op jit(solution)/shard_map/ppermute | solution.py:1013
  373.1 21.6 %copy-start.19 = (bf16[32,6144]{1,0:T(8,128)(2,1)}, bf16[32,6144]{1,0:T(8,128)(2,1)S(1)}, u32[]{:S(2)}) copy-start(bf16[32,6144]{1,0:T(8,128)(2,1)S(1)} %collective-permute-done.13.refs_8_) | copy-start | bytes 1179652
  373.1 18.7 %collective-permute-start.18 = (bf16[128,2048]{1,0:T(8,128)(2,1)S(1)}, bf16[128,2048]{1,0:T(8,128)(2,1)}, u32[]{:S(2)}, u32[]{:S(2)}) collective-permute-start(bf16[128,2048]{1,0:T(8,128)(2,1)S(1)} %collective-permute-done.17.refs_1_), channel_id=1, source_target_pairs={{0,4},{1,5},{2,6},{3,7},{4,0},{5,1},{6,2},{7,3},{8,12},{9,13},{10,... | collective-permute-start | bytes 1572872 | tf_op jit(solution)/shard_map/ppermute | solution.py:1013
  373.6 21.1 %copy-start.20 = (bf16[32,6144]{1,0:T(8,128)(2,1)}, bf16[32,6144]{1,0:T(8,128)(2,1)S(1)}, u32[]{:S(2)}) copy-start(bf16[32,6144]{1,0:T(8,128)(2,1)S(1)} %collective-permute-done.15.refs_10_) | copy-start | bytes 1179652
  373.6 19.6 %collective-permute-start.20 = (bf16[128,2048]{1,0:T(8,128)(2,1)S(1)}, bf16[128,2048]{1,0:T(8,128)(2,1)}, u32[]{:S(2)}, u32[]{:S(2)}) collective-permute-start(bf16[128,2048]{1,0:T(8,128)(2,1)S(1)} %collective-permute-done.19.refs_5_), channel_id=1, source_target_pairs={{0,2},{1,3},{2,0},{3,1},{4,6},{5,7},{6,4},{7,5},{8,10},{9,11},{10,... | collective-permute-start | bytes 1572872 | tf_op jit(solution)/shard_map/ppermute | solution.py:1013
  380.6 13.5 %collective-permute-start.30 = (bf16[128,2048]{1,0:T(8,128)(2,1)S(1)}, bf16[128,2048]{1,0:T(8,128)(2,1)S(1)}, u32[]{:S(2)}, u32[]{:S(2)}) collective-permute-start(bf16[128,2048]{1,0:T(8,128)(2,1)S(1)} %collective-permute-done.19.refs_5_), channel_id=1, source_target_pairs={{0,1},{1,0},{2,3},{3,2},{4,5},{5,4},{6,7},{7,6},{8,9},{9,8},{10,11... | collective-permute-start | bytes 1572872 | tf_op jit(solution)/shard_map/ppermute | solution.py:1013
  382.9 11.2 %collective-permute-start.27 = (bf16[128,2048]{1,0:T(8,128)(2,1)S(1)}, bf16[128,2048]{1,0:T(8,128)(2,1)S(1)}, u32[]{:S(2)}, u32[]{:S(2)}) collective-permute-start(bf16[128,2048]{1,0:T(8,128)(2,1)S(1)} %collective-permute-done.23.refs_2_), channel_id=1, source_target_pairs={{0,1},{1,0},{2,3},{3,2},{4,5},{5,4},{6,7},{7,6},{8,9},{9,8},{10,11... | collective-permute-start | bytes 1572872 | tf_op jit(solution)/shard_map/ppermute | solution.py:1013
  384.1 10.1 %copy-start.6 = (bf16[128,2048]{1,0:T(8,128)(2,1)}, bf16[128,2048]{1,0:T(8,128)(2,1)S(1)}, u32[]{:S(2)}) copy-start(bf16[128,2048]{1,0:T(8,128)(2,1)S(1)} %collective-permute-done.26.refs_7_) | copy-start | bytes 1572868
  384.1 40.2 %collective-permute-start.29 = (bf16[128,2048]{1,0:T(8,128)(2,1)S(1)}, bf16[128,2048]{1,0:T(8,128)(2,1)}, u32[]{:S(2)}, u32[]{:S(2)}) collective-permute-start(bf16[128,2048]{1,0:T(8,128)(2,1)S(1)} %collective-permute-done.24.refs_4_), channel_id=1, source_target_pairs={{0,1},{1,0},{2,3},{3,2},{4,5},{5,4},{6,7},{7,6},{8,9},{9,8},{10,11... | collective-permute-start | bytes 1572872 | tf_op jit(solution)/shard_map/ppermute | solution.py:1013
  391.8 42.8 %collective-permute-start.21 = (bf16[128,2048]{1,0:T(8,128)(2,1)}, bf16[128,2048]{1,0:T(8,128)(2,1)}, u32[]{:S(2)}, u32[]{:S(2)}) collective-permute-start(bf16[128,2048]{1,0:T(8,128)(2,1)} %collective-permute-done.18.refs_0_), channel_id=1, source_target_pairs={{0,1},{1,0},{2,3},{3,2},{4,5},{5,4},{6,7},{7,6},{8,9},{9,8},{10,11... | collective-permute-start | bytes 1572872 | tf_op jit(solution)/shard_map/ppermute | solution.py:1013
  393.2 41.5 %collective-permute-start.22 = (bf16[128,2048]{1,0:T(8,128)(2,1)}, bf16[128,2048]{1,0:T(8,128)(2,1)}, u32[]{:S(2)}, u32[]{:S(2)}) collective-permute-start(bf16[128,2048]{1,0:T(8,128)(2,1)} %collective-permute-done.20.refs_1_), channel_id=1, source_target_pairs={{0,1},{1,0},{2,3},{3,2},{4,5},{5,4},{6,7},{7,6},{8,9},{9,8},{10,11... | collective-permute-start | bytes 1572872 | tf_op jit(solution)/shard_map/ppermute | solution.py:1013
  394.1 0.8 copy-start.7
  394.1 37.1 %collective-permute-start.7 = (bf16[32,6144]{1,0:T(8,128)(2,1)}, bf16[32,6144]{1,0:T(8,128)(2,1)}, u32[]{:S(2)}, u32[]{:S(2)}) collective-permute-start(bf16[32,6144]{1,0:T(8,128)(2,1)} %collective-permute-done.4.refs_0_), channel_id=1, source_target_pairs={{0,1},{1,0},{2,3},{3,2},{4,5},{5,4},{6,7},{7,6},{8,9},{9,8},{10,11... | collective-permute-start | bytes 1179656 | tf_op jit(solution)/shard_map/ppermute | solution.py:1013
  394.1 0.9 copy-start.8
  394.1 37.0 %collective-permute-start.8 = (bf16[32,6144]{1,0:T(8,128)(2,1)}, bf16[32,6144]{1,0:T(8,128)(2,1)}, u32[]{:S(2)}, u32[]{:S(2)}) collective-permute-start(bf16[32,6144]{1,0:T(8,128)(2,1)} %collective-permute-done.6.refs_1_), channel_id=1, source_target_pairs={{0,1},{1,0},{2,3},{3,2},{4,5},{5,4},{6,7},{7,6},{8,9},{9,8},{10,11... | collective-permute-start | bytes 1179656 | tf_op jit(solution)/shard_map/ppermute | solution.py:1013
  399.2 39.4 %copy-start.21 = (f32[512]{0:T(512)}, f32[512]{0:T(512)S(1)}, u32[]{:S(2)}) copy-start(f32[512]{0:T(512)S(1)} %get-tuple-element.127) | copy-start | bytes 6148
  434.6 4.6 %copy-start.9 = (bf16[128,2048]{1,0:T(8,128)(2,1)S(1)}, bf16[128,2048]{1,0:T(8,128)(2,1)}, u32[]{:S(2)}) copy-start(bf16[128,2048]{1,0:T(8,128)(2,1)} %get-tuple-element.122) | copy-start | bytes 1572868

commit v2 on v1

--- a/solution.py
+++ b/solution.py
@@ -38,7 +38,7 @@
 
 def widen(value):
     rows, width = value.shape
-    n = min(rows, max(8, 2**20 // width))
+    n = min(rows // 2, max(8, 2**20 // width))
 
     def kernel(in_ref, out_ref):
         out_ref[...] = in_ref[...].astype(F32)
@@ -61,13 +61,10 @@
 
     def kernel(rows_ref, *refs):
         sources, target = refs[:count], refs[count + 1]
-        low, wide, come, go = refs[count + 2 :]
-        for i in range(count):
-            pltpu.make_async_copy(sources[i], low.at[i], come.at[i]).start()
+        wide, go = refs[count + 2 :]
         copies = []
         for i in range(count):
-            pltpu.make_async_copy(sources[i], low.at[i], come.at[i]).wait()
-            wide[i] = low[i].astype(F32)
+            wide[i] = sources[i][...].astype(F32)
             at = pl.multiple_of(rows_ref[i], n)
             copies.append(pltpu.make_async_copy(wide.at[i], target.at[pl.ds(at, n), :], go.at[i]))
             copies[-1].start()
@@ -77,43 +74,51 @@
     any_spec = pl.BlockSpec(memory_space=pl.ANY)
     return pl.pallas_call(
         kernel,
-        in_specs=[pl.BlockSpec(memory_space=pltpu.SMEM)] + [any_spec] * (count + 1),
+        in_specs=[pl.BlockSpec(memory_space=pltpu.SMEM)] + [pl.BlockSpec(memory_space=pltpu.VMEM)] * count + [any_spec],
         out_specs=any_spec,
         out_shape=jax.ShapeDtypeStruct(result.shape, F32),
-        scratch_shapes=[
-            pltpu.VMEM((count, n, width), BF16),
-            pltpu.VMEM((count, n, width), F32),
-            pltpu.SemaphoreType.DMA((count,)),
-            pltpu.SemaphoreType.DMA((count,)),
-        ],
+        scratch_shapes=[pltpu.VMEM((count, n, width), F32), pltpu.SemaphoreType.DMA((count,))],
         input_output_aliases={count + 1: 0},
         cost_estimate=pl.CostEstimate(flops=0, bytes_accessed=6 * count * n * width, transcendentals=0),
         name="place",
     )(rows, *pieces, result)
 
 
-def input_grad(block_in, out_grad, own, others):
-    def kernel(block_ref, out_ref, own_ref, *refs):
+def finish(block_in, out_grad, branch, bias, own, others, sums, s, lengths, S):
+    count = len(others)
+    order = [0, 1, 1] + list(range(2, len(lengths)))
+
+    def kernel(s_ref, block_ref, out_ref, branch_ref, bias_ref, own_ref, sums_ref, *refs):
+        block_out, in_grad, *smalls = refs[count:]
         wide = block_ref[...].astype(F32)
+        block_out[...] = (wide + branch_ref[...] + bias_ref[...]).astype(BF16)
         offsets = wide - jnp.mean(wide, axis=-1, keepdims=True)
         inverse = lax.rsqrt(jnp.mean(offsets * offsets, axis=-1, keepdims=True) + epsilon)
         normed = offsets * inverse
         scaled = own_ref[...]
-        for ref in refs[:-1]:
+        for ref in refs[:count]:
             scaled = scaled + ref[...].astype(F32)
         term = inverse * (
             scaled
             - jnp.mean(scaled, axis=-1, keepdims=True)
             - normed * jnp.mean(scaled * normed, axis=-1, keepdims=True)
         )
-        refs[-1][...] = (out_ref[...].astype(F32) + term).astype(BF16)
-
+        in_grad[...] = (out_ref[...].astype(F32) + term).astype(BF16)
+        for ref, i in zip(smalls, order):
+            n = lengths[i] // S
+            ref[...] = sums_ref[pl.ds(sum(lengths[:i]) + s_ref[0] * n, n), :]
+
+    outs = [jax.ShapeDtypeStruct(block_in.shape, BF16)] * 2
+    outs += [jax.ShapeDtypeStruct((lengths[i] // S, 128), F32) for i in order]
+    vmem_spec = pl.BlockSpec(memory_space=pltpu.VMEM)
     return pl.pallas_call(
         kernel,
-        out_shape=jax.ShapeDtypeStruct(block_in.shape, BF16),
+        in_specs=[pl.BlockSpec(memory_space=pltpu.SMEM)] + [vmem_spec] * (6 + count),
+        out_specs=[vmem_spec] * len(outs),
+        out_shape=outs,
         cost_estimate=pl.CostEstimate(flops=0, bytes_accessed=8 * 2**20, transcendentals=0),
-        name="input_grad",
-    )(block_in, out_grad, own, *others)
+        name="finish",
+    )(s.reshape(1), block_in, out_grad, branch, bias, own, sums, *others)
 
 
 def unwritten(shape, dtype):
@@ -564,10 +569,9 @@
 
 
 def grads(
-    first, second, attended, activated, mixed, hidden, grad, branch, inner, sums, block_in, bias, S, R, TP, DP
+    first, second, attended, activated, mixed, hidden, grad, branch, inner, sums, S, R, T, TP, DP
 ):
     N, D = grad.shape
-    T = block_in.shape[0]
     NT, ND, steps = 2 ** len(TP), 2 ** len(DP), len(DP)
     lefts = (second, first, activated, attended)
     rights = (hidden, mixed, grad, grad)
@@ -594,14 +598,17 @@
 
     def kernel(
         second_hbm, first_hbm, activated_hbm, attended_hbm, hidden_hbm, mixed_hbm, grad_hbm, branch_hbm, inner_hbm, sums_hbm,
-        block_hbm, bias_ref,
-        whole_up, whole_out, own_down_0, own_down_1, own_qkv_0, own_qkv_1, block_out, inner_own, inner_rest, sums_out,
-        own_up, own_out, block_v, near, near_came, far_came, held, held_came,
-        second_v, first_v, activated_v, attended_v, hidden_v, mixed_v, grad_v,
-        part_up, part_qkv, part_down, part_out, came_up, came_qkv, came_down, came_out, all_up, all_qkv,
-        load, dp_send, dp_recv, z_send, z_recv, near_send, near_recv, far_send, far_recv, held_send, held_recv,
-        plane_send, plane_recv,
+        whole_up, whole_out, own_down_0, own_down_1, own_qkv_0, own_qkv_1, branch_own, inner_own, *more,
     ):
+        inner_rest, sums_out = more[: S - 1], more[S - 1]
+        mates = [more[S + 4 * m : S + 4 * m + 4] for m in range(NT - 1)]
+        (
+            own_up, own_out, near, near_came, far_came, held, held_came,
+            second_v, first_v, activated_v, attended_v, hidden_v, mixed_v, grad_v,
+            part_up, part_qkv, part_down, part_out, came_up, came_qkv, came_down, came_out, all_up, all_qkv,
+            load, dp_send, dp_recv, z_send, z_recv, near_send, near_recv, far_send, far_recv, held_send, held_recv,
+            plane_send, plane_recv, mate_send, mate_recv,
+        ) = more[S + 4 * (NT - 1) :]
         s = lax.axis_index("shard")
         r = lax.axis_index("replica")
         t = sum(((r // bit) % 2 * 2**i for i, bit in enumerate(TP)), jnp.int32(0))
@@ -624,8 +631,7 @@
             pltpu.make_async_copy(parts_hbm[i].at[t], near.at[i], load.at[7 + i]) for i in range(2)
         ]
         held_load = pltpu.make_async_copy(sums_hbm, held.at[0], load.at[9])
-        own_load = pltpu.make_async_copy(block_hbm, block_v, load.at[16])
-        for copy in (loads[6], loads[4], *loads[:2], held_load, *token_loads, *loads[2:4], loads[5], own_load):
+        for copy in (loads[6], loads[4], *loads[:2], held_load, *token_loads, *loads[2:4], loads[5]):
             copy.start()
 
         group = [(k, m) for k in range(S) for m in range(NT) if k or m]
@@ -803,14 +809,13 @@
             for k in range(1, S):
                 far_copy(k).wait_recv()
                 value = value + far_came[k - 1].astype(F32)
-            own_load.wait()
-            block_out[...] = (block_v[...].astype(F32) + value + bias_ref[...]).astype(BF16)
+            branch_own[...] = value
 
         def inner_near():
             near_wait(1)
             inner_own[...] = near_sum(1, s)
             for k in range(1, S):
-                inner_rest[k - 1] = near_sum(1, lax.rem(s + k, S)).astype(BF16)
+                inner_rest[k - 1][...] = near_sum(1, lax.rem(s + k, S)).astype(BF16)
 
         bits = [(0, bit) for bit in bits_of(R - 1)] + [(1, bit) for bit in bits_of(S - 1)]
 
@@ -870,6 +875,18 @@
                 gather(i, h, m ^ 1 << top, top).wait_recv()
                 for b in range(top + 1, positions):
                     gather(i, h, m, b).start()
+
+        def to_mate(i, h, m):
+            at = (2 - i) * 2 + h
+            return pltpu.make_async_remote_copy(
+                src_ref=own[i][h], dst_ref=mates[m - 1][at], send_sem=mate_send.at[at, m], recv_sem=mate_recv.at[at, m],
+                device_id=other(0, m), device_id_type=MESH,
+            )
+
+        def to_mates(i):
+            for h in range(2):
+                for m in range(1, NT):
+                    to_mate(i, h, m).start()
 
         for i in range(2):
             for m in range(1, NT):
@@ -909,6 +926,7 @@
         collect(0)
         share_own(0)
         last(2)
+        to_mates(2)
         last(3)
         share_own(3)
         for m in range(1, 1 << steps):
@@ -916,12 +934,17 @@
                 share_on(i, m)
             if m == 1:
                 collect(1)
+                to_mates(1)
                 branch_far()
                 inner_near()
         for m in range(1 << steps, 1 << positions):
             for i in (0, 3):
                 share_on(i, m)
 
+        for i in (1, 2):
+            for h in range(2):
+                for m in range(1, NT):
+                    to_mate(i, h, m).wait()
         for i in (3, 0):
             for h in range(2):
                 keep_own(i, h).wait()
@@ -953,19 +976,18 @@
     owns = [(2, n, width * S * NT if lead > 1 else width) for lead, _, n, width in pieces]
     wholes = [(2 * n * ND * NT, width) for _, n, width in owns]
     outs = [jax.ShapeDtypeStruct(wholes[i], BF16) for i in (0, 3)]
-    outs += [jax.ShapeDtypeStruct(owns[i][1:], BF16) for i in (2, 2, 1, 1)] + [jax.ShapeDtypeStruct((T, D), BF16)]
-    outs += [jax.ShapeDtypeStruct((T, D), F32), jax.ShapeDtypeStruct((S - 1, T, D), BF16)]
-    outs += [jax.ShapeDtypeStruct(sums.shape, F32)]
+    owned = [jax.ShapeDtypeStruct(owns[i][1:], BF16) for i in (2, 2, 1, 1)]
+    outs += owned + [jax.ShapeDtypeStruct((T, D), F32)] * 2 + [jax.ShapeDtypeStruct((T, D), BF16)] * (S - 1)
+    outs += [jax.ShapeDtypeStruct(sums.shape, F32)] + owned * (NT - 1)
     sent = sum(2 * (ND - 1) * a * b * n * w * 2 for a, b, n, w in pieces)
     count = len(bits_of(R - 1)) + len(bits_of(S - 1))
     return pl.pallas_call(
         kernel,
         out_shape=outs,
-        in_specs=[any_spec] * 11 + [vmem_spec],
-        out_specs=[any_spec] * 2 + [vmem_spec] * 8,
+        in_specs=[any_spec] * 10,
+        out_specs=[any_spec] * 2 + [vmem_spec] * (7 + S - 1 + 4 * (NT - 1)),
         scratch_shapes=[pltpu.VMEM(owns[i], BF16) for i in (0, 3)]
         + [
-            pltpu.VMEM((T, D), BF16),
             pltpu.VMEM((2, S, T, D), BF16),
             pltpu.VMEM((2, NT - 1, S, T, D) if NT > 1 else (1, 1, 1, 16, 128), BF16),
             pltpu.VMEM((S - 1, T, D), BF16),
@@ -990,6 +1012,8 @@
             pltpu.SemaphoreType.DMA((count,)),
             pltpu.SemaphoreType.DMA((2, 2, ND * NT)),
             pltpu.SemaphoreType.DMA((2, 2, ND * NT)),
+            pltpu.SemaphoreType.DMA((4, NT)),
+            pltpu.SemaphoreType.DMA((4, NT)),
         ],
         compiler_params=pltpu.CompilerParams(
             collective_id=1, has_side_effects=True, vmem_limit_bytes=67043328
@@ -999,7 +1023,7 @@
             bytes_accessed=sent * 8, transcendentals=0,
         ),
         name="grads",
-    )(*operands, branch, inner, sums, block_in, bias)
+    )(*operands, branch, inner, sums)
 
 
 def solution(mesh):
@@ -1016,7 +1040,7 @@
         block_in, positions, out_grad, w_qkv, b_qkv, w_out, b_out, w_up, b_up, w_down, b_down,
         first_gain, first_shift, second_gain, second_shift,
     ):
-        T, D = block_in.shape
+        T, _ = block_in.shape
         FS = w_down.shape[0]
         FD = FS // NT
         s = lax.axis_index("shard")
@@ -1040,26 +1064,12 @@
         ]
         d = sum((mine[bit] * 2**i for i, bit in enumerate(DP)), jnp.int32(0))
 
-        whole_up, whole_out, *owned_rows, block_out, inner_own, inner_rest, sums = grads(
+        whole_up, whole_out, *more = grads(
             first_low, second_low, attended, activated, mixed_low, hidden_low, grad_all, branch_part, inner_part,
-            sums, block_in, bias, S, R, TP, DP,
+            sums, S, R, T, TP, DP,
         )
-
-        sums = sums.reshape(-1)
-        width = w_out.shape[0] * S
-        lengths = [width] * 3 + [D, FS * S] + [D] * 4
-        at = [sum(lengths[:i]) for i in range(len(lengths))]
-
-        def owned(start, length):
-            return lax.dynamic_slice_in_dim(sums, start + s * (length // S), length // S, 0)
-
-        grad_b_qkv = owned(at[0], 3 * width)
-        grad_b_out = owned(at[3], D)
-        grad_b_up = owned(at[4], FS * S)
-        smalls = [owned(at[5 + i], D) for i in range(4)]
-        whole_out, grad_b_qkv, grad_b_out, grad_b_up, smalls = lax.optimization_barrier(
-            (whole_out, grad_b_qkv, grad_b_out, grad_b_up, smalls)
-        )
+        owned_rows, (branch_own, inner_own), inner_rest, sums = more[:4], more[4:6], more[6 : 5 + S], more[5 + S]
+        mates = [more[6 + S + 4 * m : 10 + S + 4 * m] for m in range(NT - 1)]
 
         ways = [DP, DP[::-1]]
 
@@ -1076,9 +1086,12 @@
             dd, tt = indices(m)
             return ((dd * NT + tt) * 2 + half) * n
 
-        def placed(result, pieces, row):
+        def placed(result, which, pieces, row):
             for bit in TP:
-                pieces = pieces + [(half, m | bit, flip(value, bit)) for half, m, value in pieces]
+                pieces = pieces + [
+                    (half, m | bit, mates[0][2 * which + half] if m == 0 else flip(value, bit))
+                    for half, m, value in pieces
+                ]
             at = jnp.stack([row(half, m, value.shape[0]) for half, m, value in pieces])
             return place([value for _, _, value in pieces], at, result)
 
@@ -1101,18 +1114,22 @@
         scaled = []
         for k in range(1, S):
             scaled.append(lax.ppermute(inner_rest[k - 1], "shard", [(i, (i + k) % S) for i in range(S)]))
-        in_grad = input_grad(block_in, out_grad, inner_own, scaled)
+        block_out, in_grad, *smalls = finish(
+            block_in, out_grad, branch_own, bias, inner_own, scaled, sums, s,
+            [v.shape[0] * S // 128 for v in (b_qkv, b_out, b_up) + (first_gain,) * 4], S,
+        )
         grad_w_up = widen(whole_up)
         grad_w_out = widen(whole_out)
-        grad_w_down = placed(unwritten(w_down.shape, F32), pieces_of(0, [0] + DP), down_row)
-        grad_w_qkv = placed(unwritten(w_qkv.shape, F32), pieces_of(1, [0] + DP), qkv_row)
+        grad_w_down = placed(unwritten(w_down.shape, F32), 0, pieces_of(0, [0] + DP), down_row)
+        grad_w_qkv = placed(unwritten(w_qkv.shape, F32), 1, pieces_of(1, [0] + DP), qkv_row)
         if several:
-            grad_w_down = placed(grad_w_down, pieces_of(0, several), down_row)
-            grad_w_qkv = placed(grad_w_qkv, pieces_of(1, several), qkv_row)
-
+            grad_w_down = placed(grad_w_down, 0, pieces_of(0, several), down_row)
+            grad_w_qkv = placed(grad_w_qkv, 1, pieces_of(1, several), qkv_row)
+
+        grad_b_qkv, grad_b_out, grad_b_down, grad_b_up, *norm_grads = [v.reshape(-1) for v in smalls]
         return (
             block_out, in_grad, grad_w_qkv, grad_b_qkv, grad_w_out, grad_b_out, grad_w_up, grad_b_up,
-            grad_w_down, grad_b_out, *smalls,
+            grad_w_down, grad_b_down, *norm_grads,
         )
 
     rows2, row1, par2, par1 = P(("shard", "replica"), None), P(("shard", "replica")), P("shard", None), P("shard")

time: 441 us -> 434 us (0.984)
  the two profiles are of different devices: /device:TPU:9 before, /device:TPU:0 now
where the time goes in v2:
time: 434 us; the launch traced here: 426 us
  Pallas kernels  326 us (75%)
  waiting for transfers between devices  75.7 us (17%)
  starting transfers between devices  18.2 us (4%)
    pallas_call x1, Pallas kernels, grads(): pl.pallas_call(kernel, out_shape=outs, in_specs=[any_spec] * 10, out_spec...  164 us
    pallas_call x1, Pallas kernels, layer(): pl.pallas_call(kernel, out_shape=outs, in_specs=[any_spec] * 7 + [vmem_sp...  124 us
    ppermute x24, waiting for transfers between devices, flip(): return lax.ppermute(value, 'replica', [(i, i ^ bit) for i in range(R)])  50.5 us
    ppermute x3, waiting for transfers between devices, body(): lax.ppermute(inner_rest[k - 1], 'shard', [(i, (i + k) % S) for i in range...  25.2 us
    pallas_call x4, Pallas kernels, place(): pl.pallas_call(kernel, in_specs=[pl.BlockSpec(memory_space=pltpu.SMEM)] +...  20.4 us
    ppermute x24, starting transfers between devices, flip(): return lax.ppermute(value, 'replica', [(i, i ^ bit) for i in range(R)])  14.3 us
    pallas_call x2, Pallas kernels, widen(): pl.pallas_call(kernel, grid=(rows // n,), in_specs=[spec], out_specs=spec...  12.9 us
  transfers between devices with their start and end apart: 27, of which 10 were waited for; matrix products, arithmetic and copies ran while one was open for 1% of the time, Pallas kernels for 8%

profile of v2, /device:TPU:0, one launch (start us, length us, event | category | flops | bytes accessed | tf_op | source)
XLA Modules:
  0.0 425.9 jit_solution(13362120227590197342)
XLA Ops:
  0.6 0.7 convert_element_type.3
  1.3 1.4 add_bitcast_fusion.small_ref
  2.7 124.3 %layer.1 = (bf16[2,4,128,2048]{3,2,1,0:T(8,128)(2,1)}, bf16[2,4,128,2048]{3,2,1,0:T(8,128)(2,1)}, bf16[2,4,128,256]{3,2,1,0:T(8,128)(2,1)}, bf16[2,4,128,1024]{3...) custom-call(bf16[53,128]{1,0:T(8,128)(2,1)} %add_bitcast_fusion.smal, ...), custom_call_target="tpu_custom_call" | custom-call | flops 25769803776 | bytes 83886080 | tf_op jit(solution)/shard_map/layer/pallas_call | solution.py:529
  127.1 163.7 %grads.1 = (bf16[512,8192]{1,0:T(8,128)(2,1)}, bf16[512,2048]{1,0:T(8,128)(2,1)}, bf16[128,2048]{1,0:T(8,128)(2,1)}, bf16[128,2048]{1,0:T(8,128)(2,1)}, bf16[32,...) custom-call(bf16[1024,2048]{1,0:T(8,128)(2,1)} %bitcast.59, ...), custom_call_target="tpu_custom_call" | custom-call | flops 12884901888 | bytes 75497472 | tf_op jit(solution)/shard_map/grads/pallas_call | solution.py:984
  290.8 1.4 collective-permute-start.3
  292.2 0.7 collective-permute-start.5
  292.9 1.5 collective-permute-start.15
  294.4 0.5 collective-permute-start.9
  294.9 1.5 collective-permute-start.17
  296.4 6.6 %collective-permute-done.3.refs_1_ = bf16[32,6144]{1,0:T(8,128)(2,1)S(1)} collective-permute-done((bf16[32,6144]{1,0:T(8,128)(2,1)}, bf16[32,6144]{1,0:T(8,128)(2,1)S(1)}, u32[]{:S(2)}, u32[]{:S(2)}) %collective-permute-start.3) | collective-permute-done | bytes 393248 | tf_op jit(solution)/shard_map/ppermute | solution.py:1037
  303.1 1.3 collective-permute-start.10
  304.4 0.0 collective-permute-done.5.refs_5_
  304.4 0.7 collective-permute-start.21
  305.1 7.7 %collective-permute-done.9.refs_2_ = bf16[32,6144]{1,0:T(8,128)(2,1)S(1)} collective-permute-done((bf16[32,6144]{1,0:T(8,128)(2,1)}, bf16[32,6144]{1,0:T(8,128)(2,1)S(1)}, u32[]{:S(2)}, u32[]{:S(2)}) %collective-permute-start.9) | collective-permute-done | bytes 393248 | tf_op jit(solution)/shard_map/ppermute | solution.py:1037
  312.8 0.7 collective-permute-start.22
  313.5 9.2 %collective-permute-done.10.refs_4_ = bf16[32,6144]{1,0:T(8,128)(2,1)S(1)} collective-permute-done((bf16[32,6144]{1,0:T(8,128)(2,1)}, bf16[32,6144]{1,0:T(8,128)(2,1)S(1)}, u32[]{:S(2)}, u32[]{:S(2)}) %collective-permute-start.10) | collective-permute-done | bytes 393248 | tf_op jit(solution)/shard_map/ppermute | solution.py:1037
  322.7 0.6 collective-permute-start
  323.3 0.0 collective-permute-done.15.refs_1_
  323.3 2.8 collective-permute-start.1
  326.0 0.0 collective-permute-done.17.refs_5_
  326.1 0.6 collective-permute-start.2
  326.6 7.8 %collective-permute-done.21.refs_2_ = bf16[128,2048]{1,0:T(8,128)(2,1)S(1)} collective-permute-done((bf16[128,2048]{1,0:T(8,128)(2,1)}, bf16[128,2048]{1,0:T(8,128)(2,1)S(1)}, u32[]{:S(2)}, u32[]{:S(2)}) %collective-permute-start.21) | collective-permute-done | bytes 524320 | tf_op jit(solution)/shard_map/ppermute | solution.py:1037
  334.4 0.0 collective-permute-start.11
  334.4 0.0 collective-permute-done.22.refs_4_
  334.5 0.5 collective-permute-start.14
  335.0 4.7 %collective-permute-done.refs_0_ = bf16[128,2048]{1,0:T(8,128)(2,1)S(1)} collective-permute-done((bf16[128,2048]{1,0:T(8,128)(2,1)}, bf16[128,2048]{1,0:T(8,128)(2,1)S(1)}, u32[]{:S(2)}, u32[]{:S(2)}) %collective-permute-start) | collective-permute-done | bytes 524320 | tf_op jit(solution)/shard_map/ppermute | solution.py:1116
  339.6 0.0 collective-permute-start.12
  339.6 20.5 %collective-permute-done.1.refs_1_ = bf16[128,2048]{1,0:T(8,128)(2,1)S(1)} collective-permute-done((bf16[128,2048]{1,0:T(8,128)(2,1)}, bf16[128,2048]{1,0:T(8,128)(2,1)S(1)}, u32[]{:S(2)}, u32[]{:S(2)}) %collective-permute-start.1) | collective-permute-done | bytes 524320 | tf_op jit(solution)/shard_map/ppermute | solution.py:1116
  360.2 0.0 collective-permute-start.13
  360.2 1.6 collective-permute-start.4
  361.8 0.5 collective-permute-start.6
  362.3 0.1 collective-permute-start.23
  362.4 0.0 collective-permute-done.12.refs_8_
  362.4 1.4 collective-permute-start.16
  363.8 0.0 collective-permute-done.13.refs_10_
  363.8 0.8 collective-permute-start.18
  364.5 7.8 %collective-permute-done.4.refs_0_ = bf16[32,6144]{1,0:T(8,128)(2,1)} collective-permute-done((bf16[32,6144]{1,0:T(8,128)(2,1)S(1)}, bf16[32,6144]{1,0:T(8,128)(2,1)}, u32[]{:S(2)}, u32[]{:S(2)}) %collective-permute-start.4) | collective-permute-done | bytes 393248 | tf_op jit(solution)/shard_map/ppermute | solution.py:1037
  372.3 1.5 collective-permute-done.6.refs_1_
  373.9 0.0 collective-permute-done.23.refs_7_
  373.9 0.5 collective-permute-start.25
  374.4 8.6 %collective-permute-done.16.refs_0_ = bf16[128,2048]{1,0:T(8,128)(2,1)S(1)} collective-permute-done((bf16[128,2048]{1,0:T(8,128)(2,1)S(1)}, bf16[128,2048]{1,0:T(8,128)(2,1)S(1)}, u32[]{:S(2)}, u32[]{:S(2)}) %collective-permute-start.16) | collective-permute-done | bytes 524320 | tf_op jit(solution)/shard_map/ppermute | solution.py:1037
  382.9 0.0 collective-permute-start.19
  382.9 1.2 collective-permute-done.18.refs_1_
  384.2 0.0 collective-permute-start.20
  384.2 0.0 collective-permute-done.26.refs_11_
  384.2 0.5 collective-permute-start.7
  384.7 0.0 collective-permute-done.24.refs_8_
  384.7 0.1 collective-permute-start.8
  384.9 0.2 copy-done.7
  385.0 0.5 copy-done.8
  385.6 9.5 %widen.3 = f32[512,8192]{1,0:T(8,128)} custom-call(bf16[512,8192]{1,0:T(8,128)(2,1)} %get-tuple-element.77.in_ref), custom_call_target="tpu_custom_call" | custom-call | bytes 25165824 | tf_op jit(solution)/shard_map/widen/pallas_call | solution.py:47
  395.2 3.4 widen.2
  398.5 0.6 stack.143.rows_ref
  399.2 0.6 stack.125.rows_ref
  399.8 0.7 pad_add_fusion.1.rows_ref
  400.4 0.7 pad_add_fusion.rows_ref
  401.1 4.2 finish.1
  405.3 6.1 %place.4.refs_4_ = f32[512,6144]{1,0:T(8,128)} custom-call(s32[12]{0:T(128)} %stack.125.rows_ref, bf16[32,6144]{1,0:T(8,128)(2,1)} %get-tuple-element.70.refs_0_, bf16[32,6144]{1,0:T(8,128)(2,1)} %copy-done.12, bf16[32,6144]{1,0:T(8,128)(2,1)} %copy-done.14, bf16[32,6144]{1,0:T(8,128)(2,1)} %get-tuple-element.71.refs_3_, ...), custom_call_target="tpu_custom_call", output_to_operand_aliasing={{}: (13, {})} | custom-call | bytes 14155776 | tf_op jit(solution)/shard_map/place/pallas_call | solution.py:75
  411.4 0.0 collective-permute-done.25.refs_10_
  411.4 7.5 %place.6.refs_4_ = f32[2048,2048]{1,0:T(8,128)} custom-call(s32[12]{0:T(128)} %stack.143.rows_ref, bf16[128,2048]{1,0:T(8,128)(2,1)} %get-tuple-element.79.refs_0_, bf16[128,2048]{1,0:T(8,128)(2,1)} %copy-done, bf16[128,2048]{1,0:T(8,128)(2,1)} %copy-done.2, bf16[128,2048]{1,0:T(8,128)(2,1)} %get-tuple-element.80.refs_3_, ...), custom_call_target="tpu_custom_call", output_to_operand_aliasing={{}: (13, {})} | custom-call | bytes 18874368 | tf_op jit(solution)/shard_map/place/pallas_call | solution.py:75
  419.0 0.0 collective-permute-done.8.refs_3_
  419.0 3.1 place.5
  422.1 0.0 collective-permute-done.20.refs_3_
  422.1 3.6 place.7
  (47 shorter events, 0.1 us)
Async XLA Ops:
  290.8 12.3 %collective-permute-start.3 = (bf16[32,6144]{1,0:T(8,128)(2,1)}, bf16[32,6144]{1,0:T(8,128)(2,1)S(1)}, u32[]{:S(2)}, u32[]{:S(2)}) collective-permute-start(bf16[32,6144]{1,0:T(8,128)(2,1)} %get-tuple-element.70.refs_0_), channel_id=1, source_target_pairs={{0,2},{1,3},{2,0},{3,1},{4,6},{5,7},{6,4},{7,5},{8,10},{9,11},{10,... | collective-permute-start | bytes 1179656 | tf_op jit(solution)/shard_map/ppermute | solution.py:1037
  292.2 12.2 %collective-permute-start.5 = (bf16[32,6144]{1,0:T(8,128)(2,1)}, bf16[32,6144]{1,0:T(8,128)(2,1)S(1)}, u32[]{:S(2)}, u32[]{:S(2)}) collective-permute-start(bf16[32,6144]{1,0:T(8,128)(2,1)} %get-tuple-element.71.refs_3_), channel_id=1, source_target_pairs={{0,4},{1,5},{2,6},{3,7},{4,0},{5,1},{6,2},{7,3},{8,12},{9,13},{10,... | collective-permute-start | bytes 1179656 | tf_op jit(solution)/shard_map/ppermute | solution.py:1037
  292.9 30.4 %collective-permute-start.15 = (bf16[128,2048]{1,0:T(8,128)(2,1)}, bf16[128,2048]{1,0:T(8,128)(2,1)S(1)}, u32[]{:S(2)}, u32[]{:S(2)}) collective-permute-start(bf16[128,2048]{1,0:T(8,128)(2,1)} %get-tuple-element.79.refs_0_), channel_id=1, source_target_pairs={{0,2},{1,3},{2,0},{3,1},{4,6},{5,7},{6,4},{7,5},{8,10},{9,11},{10,... | collective-permute-start | bytes 1572872 | tf_op jit(solution)/shard_map/ppermute | solution.py:1037
  294.4 18.4 %collective-permute-start.9 = (bf16[32,6144]{1,0:T(8,128)(2,1)}, bf16[32,6144]{1,0:T(8,128)(2,1)S(1)}, u32[]{:S(2)}, u32[]{:S(2)}) collective-permute-start(bf16[32,6144]{1,0:T(8,128)(2,1)} %get-tuple-element.70.refs_0_), channel_id=1, source_target_pairs={{0,4},{1,5},{2,6},{3,7},{4,0},{5,1},{6,2},{7,3},{8,12},{9,13},{10,... | collective-permute-start | bytes 1179656 | tf_op jit(solution)/shard_map/ppermute | solution.py:1037
  294.9 31.1 %collective-permute-start.17 = (bf16[128,2048]{1,0:T(8,128)(2,1)}, bf16[128,2048]{1,0:T(8,128)(2,1)S(1)}, u32[]{:S(2)}, u32[]{:S(2)}) collective-permute-start(bf16[128,2048]{1,0:T(8,128)(2,1)} %get-tuple-element.80.refs_3_), channel_id=1, source_target_pairs={{0,4},{1,5},{2,6},{3,7},{4,0},{5,1},{6,2},{7,3},{8,12},{9,13},{10,... | collective-permute-start | bytes 1572872 | tf_op jit(solution)/shard_map/ppermute | solution.py:1037
  303.1 92.1 %copy-start.12 = (bf16[32,6144]{1,0:T(8,128)(2,1)}, bf16[32,6144]{1,0:T(8,128)(2,1)S(1)}, u32[]{:S(2)}) copy-start(bf16[32,6144]{1,0:T(8,128)(2,1)S(1)} %collective-permute-done.3.refs_1_) | copy-start | bytes 1179652
  303.1 19.7 %collective-permute-start.10 = (bf16[32,6144]{1,0:T(8,128)(2,1)}, bf16[32,6144]{1,0:T(8,128)(2,1)S(1)}, u32[]{:S(2)}, u32[]{:S(2)}) collective-permute-start(bf16[32,6144]{1,0:T(8,128)(2,1)} %get-tuple-element.71.refs_3_), channel_id=1, source_target_pairs={{0,2},{1,3},{2,0},{3,1},{4,6},{5,7},{6,4},{7,5},{8,10},{9,11},{10,... | collective-permute-start | bytes 1179656 | tf_op jit(solution)/shard_map/ppermute | solution.py:1037
  304.4 80.4 %copy-start.13 = (bf16[32,6144]{1,0:T(8,128)(2,1)}, bf16[32,6144]{1,0:T(8,128)(2,1)S(1)}, u32[]{:S(2)}) copy-start(bf16[32,6144]{1,0:T(8,128)(2,1)S(1)} %collective-permute-done.5.refs_5_) | copy-start | bytes 1179652
  304.4 30.0 %collective-permute-start.21 = (bf16[128,2048]{1,0:T(8,128)(2,1)}, bf16[128,2048]{1,0:T(8,128)(2,1)S(1)}, u32[]{:S(2)}, u32[]{:S(2)}) collective-permute-start(bf16[128,2048]{1,0:T(8,128)(2,1)} %get-tuple-element.79.refs_0_), channel_id=1, source_target_pairs={{0,4},{1,5},{2,6},{3,7},{4,0},{5,1},{6,2},{7,3},{8,12},{9,13},{10,... | collective-permute-start | bytes 1572872 | tf_op jit(solution)/shard_map/ppermute | solution.py:1037
  312.8 49.6 %copy-start.14 = (bf16[32,6144]{1,0:T(8,128)(2,1)}, bf16[32,6144]{1,0:T(8,128)(2,1)S(1)}, u32[]{:S(2)}) copy-start(bf16[32,6144]{1,0:T(8,128)(2,1)S(1)} %collective-permute-done.9.refs_2_) | copy-start | bytes 1179652
  312.8 21.6 %collective-permute-start.22 = (bf16[128,2048]{1,0:T(8,128)(2,1)}, bf16[128,2048]{1,0:T(8,128)(2,1)S(1)}, u32[]{:S(2)}, u32[]{:S(2)}) collective-permute-start(bf16[128,2048]{1,0:T(8,128)(2,1)} %get-tuple-element.80.refs_3_), channel_id=1, source_target_pairs={{0,2},{1,3},{2,0},{3,1},{4,6},{5,7},{6,4},{7,5},{8,10},{9,11},{10,... | collective-permute-start | bytes 1572872 | tf_op jit(solution)/shard_map/ppermute | solution.py:1037
  322.7 41.1 %copy-start.15 = (bf16[32,6144]{1,0:T(8,128)(2,1)}, bf16[32,6144]{1,0:T(8,128)(2,1)S(1)}, u32[]{:S(2)}) copy-start(bf16[32,6144]{1,0:T(8,128)(2,1)S(1)} %collective-permute-done.10.refs_4_) | copy-start | bytes 1179652
  322.7 16.9 %collective-permute-start = (bf16[128,2048]{1,0:T(8,128)(2,1)}, bf16[128,2048]{1,0:T(8,128)(2,1)S(1)}, u32[]{:S(2)}, u32[]{:S(2)}) collective-permute-start(bf16[128,2048]{1,0:T(8,128)(2,1)} %get-tuple-element.65), channel_id=1, source_target_pairs={{0,8},{8,16},{16,24},{24,0},{1,9},{9,17},{17,25},{25,1},{2,10},{10... | collective-permute-start | bytes 1572872 | tf_op jit(solution)/shard_map/ppermute | solution.py:1116
  323.3 62.2 %copy-start = (bf16[128,2048]{1,0:T(8,128)(2,1)}, bf16[128,2048]{1,0:T(8,128)(2,1)S(1)}, u32[]{:S(2)}) copy-start(bf16[128,2048]{1,0:T(8,128)(2,1)S(1)} %collective-permute-done.15.refs_1_) | copy-start | bytes 1572868
  323.3 36.9 %collective-permute-start.1 = (bf16[128,2048]{1,0:T(8,128)(2,1)}, bf16[128,2048]{1,0:T(8,128)(2,1)S(1)}, u32[]{:S(2)}, u32[]{:S(2)}) collective-permute-start(bf16[128,2048]{1,0:T(8,128)(2,1)} %get-tuple-element.66), channel_id=1, source_target_pairs={{0,16},{8,24},{16,0},{24,8},{1,17},{9,25},{17,1},{25,9},{2,18},{10... | collective-permute-start | bytes 1572872 | tf_op jit(solution)/shard_map/ppermute | solution.py:1116
  326.1 59.5 %copy-start.1 = (bf16[128,2048]{1,0:T(8,128)(2,1)}, bf16[128,2048]{1,0:T(8,128)(2,1)S(1)}, u32[]{:S(2)}) copy-start(bf16[128,2048]{1,0:T(8,128)(2,1)S(1)} %collective-permute-done.17.refs_5_) | copy-start | bytes 1572868
  326.1 34.1 %collective-permute-start.2 = (bf16[128,2048]{1,0:T(8,128)(2,1)}, bf16[128,2048]{1,0:T(8,128)(2,1)S(1)}, u32[]{:S(2)}, u32[]{:S(2)}) collective-permute-start(bf16[128,2048]{1,0:T(8,128)(2,1)} %get-tuple-element.67), channel_id=1, source_target_pairs={{0,24},{8,0},{16,8},{24,16},{1,25},{9,1},{17,9},{25,17},{2,26},{10... | collective-permute-start | bytes 1572872 | tf_op jit(solution)/shard_map/ppermute | solution.py:1116
  334.4 51.1 %copy-start.2 = (bf16[128,2048]{1,0:T(8,128)(2,1)}, bf16[128,2048]{1,0:T(8,128)(2,1)S(1)}, u32[]{:S(2)}) copy-start(bf16[128,2048]{1,0:T(8,128)(2,1)S(1)} %collective-permute-done.21.refs_2_) | copy-start | bytes 1572868
  334.4 27.3 %collective-permute-start.11 = (bf16[32,6144]{1,0:T(8,128)(2,1)S(1)}, bf16[32,6144]{1,0:T(8,128)(2,1)S(1)}, u32[]{:S(2)}, u32[]{:S(2)}) collective-permute-start(bf16[32,6144]{1,0:T(8,128)(2,1)S(1)} %collective-permute-done.3.refs_1_), channel_id=1, source_target_pairs={{0,1},{1,0},{2,3},{3,2},{4,5},{5,4},{6,7},{7,6},{8,9},{9,8},{10,11... | collective-permute-start | bytes 1179656 | tf_op jit(solution)/shard_map/ppermute | solution.py:1037
  334.4 51.1 %copy-start.3 = (bf16[128,2048]{1,0:T(8,128)(2,1)}, bf16[128,2048]{1,0:T(8,128)(2,1)S(1)}, u32[]{:S(2)}) copy-start(bf16[128,2048]{1,0:T(8,128)(2,1)S(1)} %collective-permute-done.22.refs_4_) | copy-start | bytes 1572868
  334.5 27.8 %collective-permute-start.14 = (bf16[32,6144]{1,0:T(8,128)(2,1)S(1)}, bf16[32,6144]{1,0:T(8,128)(2,1)S(1)}, u32[]{:S(2)}, u32[]{:S(2)}) collective-permute-start(bf16[32,6144]{1,0:T(8,128)(2,1)S(1)} %collective-permute-done.5.refs_5_), channel_id=1, source_target_pairs={{0,1},{1,0},{2,3},{3,2},{4,5},{5,4},{6,7},{7,6},{8,9},{9,8},{10,11... | collective-permute-start | bytes 1179656 | tf_op jit(solution)/shard_map/ppermute | solution.py:1037
  339.6 22.7 %copy-start.9 = (bf16[128,2048]{1,0:T(8,128)(2,1)}, bf16[128,2048]{1,0:T(8,128)(2,1)S(1)}, u32[]{:S(2)}) copy-start(bf16[128,2048]{1,0:T(8,128)(2,1)S(1)} %collective-permute-done.refs_0_) | copy-start | bytes 1572868
  339.6 22.8 %collective-permute-start.12 = (bf16[32,6144]{1,0:T(8,128)(2,1)S(1)}, bf16[32,6144]{1,0:T(8,128)(2,1)S(1)}, u32[]{:S(2)}, u32[]{:S(2)}) collective-permute-start(bf16[32,6144]{1,0:T(8,128)(2,1)S(1)} %collective-permute-done.9.refs_2_), channel_id=1, source_target_pairs={{0,1},{1,0},{2,3},{3,2},{4,5},{5,4},{6,7},{7,6},{8,9},{9,8},{10,11... | collective-permute-start | bytes 1179656 | tf_op jit(solution)/shard_map/ppermute | solution.py:1037
  360.2 4.4 %copy-start.10 = (bf16[128,2048]{1,0:T(8,128)(2,1)}, bf16[128,2048]{1,0:T(8,128)(2,1)S(1)}, u32[]{:S(2)}) copy-start(bf16[128,2048]{1,0:T(8,128)(2,1)S(1)} %collective-permute-done.1.refs_1_) | copy-start | bytes 1572868
  360.2 3.6 collective-permute-start.13
  360.2 12.2 %copy-start.11 = (bf16[128,2048]{1,0:T(8,128)(2,1)}, bf16[128,2048]{1,0:T(8,128)(2,1)S(1)}, u32[]{:S(2)}) copy-start(bf16[128,2048]{1,0:T(8,128)(2,1)S(1)} %collective-permute-done.2.refs_2_) | copy-start | bytes 1572868
  360.2 12.2 %collective-permute-start.4 = (bf16[32,6144]{1,0:T(8,128)(2,1)S(1)}, bf16[32,6144]{1,0:T(8,128)(2,1)}, u32[]{:S(2)}, u32[]{:S(2)}) collective-permute-start(bf16[32,6144]{1,0:T(8,128)(2,1)S(1)} %collective-permute-done.3.refs_1_), channel_id=1, source_target_pairs={{0,4},{1,5},{2,6},{3,7},{4,0},{5,1},{6,2},{7,3},{8,12},{9,13},{10,... | collective-permute-start | bytes 1179656 | tf_op jit(solution)/shard_map/ppermute | solution.py:1037
  361.8 23.1 %copy-start.16 = (bf16[32,6144]{1,0:T(8,128)(2,1)}, bf16[32,6144]{1,0:T(8,128)(2,1)S(1)}, u32[]{:S(2)}) copy-start(bf16[32,6144]{1,0:T(8,128)(2,1)S(1)} %collective-permute-done.11.refs_7_) | copy-start | bytes 1179652
  361.8 12.1 %collective-permute-start.6 = (bf16[32,6144]{1,0:T(8,128)(2,1)S(1)}, bf16[32,6144]{1,0:T(8,128)(2,1)}, u32[]{:S(2)}, u32[]{:S(2)}) collective-permute-start(bf16[32,6144]{1,0:T(8,128)(2,1)S(1)} %collective-permute-done.5.refs_5_), channel_id=1, source_target_pairs={{0,2},{1,3},{2,0},{3,1},{4,6},{5,7},{6,4},{7,5},{8,10},{9,11},{10,... | collective-permute-start | bytes 1179656 | tf_op jit(solution)/shard_map/ppermute | solution.py:1037
  362.3 22.5 %copy-start.17 = (bf16[32,6144]{1,0:T(8,128)(2,1)}, bf16[32,6144]{1,0:T(8,128)(2,1)S(1)}, u32[]{:S(2)}) copy-start(bf16[32,6144]{1,0:T(8,128)(2,1)S(1)} %collective-permute-done.14.refs_11_) | copy-start | bytes 1179652
  362.3 11.6 %collective-permute-start.23 = (bf16[128,2048]{1,0:T(8,128)(2,1)S(1)}, bf16[128,2048]{1,0:T(8,128)(2,1)S(1)}, u32[]{:S(2)}, u32[]{:S(2)}) collective-permute-start(bf16[128,2048]{1,0:T(8,128)(2,1)S(1)} %collective-permute-done.15.refs_1_), channel_id=1, source_target_pairs={{0,1},{1,0},{2,3},{3,2},{4,5},{5,4},{6,7},{7,6},{8,9},{9,8},{10,11... | collective-permute-start | bytes 1572872 | tf_op jit(solution)/shard_map/ppermute | solution.py:1037
  362.4 22.4 %copy-start.18 = (bf16[32,6144]{1,0:T(8,128)(2,1)}, bf16[32,6144]{1,0:T(8,128)(2,1)S(1)}, u32[]{:S(2)}) copy-start(bf16[32,6144]{1,0:T(8,128)(2,1)S(1)} %collective-permute-done.12.refs_8_) | copy-start | bytes 1179652
  362.4 20.5 %collective-permute-start.16 = (bf16[128,2048]{1,0:T(8,128)(2,1)S(1)}, bf16[128,2048]{1,0:T(8,128)(2,1)S(1)}, u32[]{:S(2)}, u32[]{:S(2)}) collective-permute-start(bf16[128,2048]{1,0:T(8,128)(2,1)S(1)} %collective-permute-done.15.refs_1_), channel_id=1, source_target_pairs={{0,4},{1,5},{2,6},{3,7},{4,0},{5,1},{6,2},{7,3},{8,12},{9,13},{10,... | collective-permute-start | bytes 1572872 | tf_op jit(solution)/shard_map/ppermute | solution.py:1037
  363.8 21.1 %copy-start.19 = (bf16[32,6144]{1,0:T(8,128)(2,1)}, bf16[32,6144]{1,0:T(8,128)(2,1)S(1)}, u32[]{:S(2)}) copy-start(bf16[32,6144]{1,0:T(8,128)(2,1)S(1)} %collective-permute-done.13.refs_10_) | copy-start | bytes 1179652
  363.8 20.4 %collective-permute-start.18 = (bf16[128,2048]{1,0:T(8,128)(2,1)S(1)}, bf16[128,2048]{1,0:T(8,128)(2,1)S(1)}, u32[]{:S(2)}, u32[]{:S(2)}) collective-permute-start(bf16[128,2048]{1,0:T(8,128)(2,1)S(1)} %collective-permute-done.17.refs_5_), channel_id=1, source_target_pairs={{0,2},{1,3},{2,0},{3,1},{4,6},{5,7},{6,4},{7,5},{8,10},{9,11},{10,... | collective-permute-start | bytes 1572872 | tf_op jit(solution)/shard_map/ppermute | solution.py:1037
  372.3 11.8 %collective-permute-start.26 = (bf16[128,2048]{1,0:T(8,128)(2,1)S(1)}, bf16[128,2048]{1,0:T(8,128)(2,1)S(1)}, u32[]{:S(2)}, u32[]{:S(2)}) collective-permute-start(bf16[128,2048]{1,0:T(8,128)(2,1)S(1)} %collective-permute-done.17.refs_5_), channel_id=1, source_target_pairs={{0,1},{1,0},{2,3},{3,2},{4,5},{5,4},{6,7},{7,6},{8,9},{9,8},{10,11... | collective-permute-start | bytes 1572872 | tf_op jit(solution)/shard_map/ppermute | solution.py:1037
  373.9 10.8 %collective-permute-start.24 = (bf16[128,2048]{1,0:T(8,128)(2,1)S(1)}, bf16[128,2048]{1,0:T(8,128)(2,1)S(1)}, u32[]{:S(2)}, u32[]{:S(2)}) collective-permute-start(bf16[128,2048]{1,0:T(8,128)(2,1)S(1)} %collective-permute-done.21.refs_2_), channel_id=1, source_target_pairs={{0,1},{1,0},{2,3},{3,2},{4,5},{5,4},{6,7},{7,6},{8,9},{9,8},{10,11... | collective-permute-start | bytes 1572872 | tf_op jit(solution)/shard_map/ppermute | solution.py:1037
  373.9 10.8 %copy-start.6 = (bf16[128,2048]{1,0:T(8,128)(2,1)}, bf16[128,2048]{1,0:T(8,128)(2,1)S(1)}, u32[]{:S(2)}) copy-start(bf16[128,2048]{1,0:T(8,128)(2,1)S(1)} %collective-permute-done.23.refs_7_) | copy-start | bytes 1572868
  373.9 37.6 %collective-permute-start.25 = (bf16[128,2048]{1,0:T(8,128)(2,1)S(1)}, bf16[128,2048]{1,0:T(8,128)(2,1)}, u32[]{:S(2)}, u32[]{:S(2)}) collective-permute-start(bf16[128,2048]{1,0:T(8,128)(2,1)S(1)} %collective-permute-done.22.refs_4_), channel_id=1, source_target_pairs={{0,1},{1,0},{2,3},{3,2},{4,5},{5,4},{6,7},{7,6},{8,9},{9,8},{10,11... | collective-permute-start | bytes 1572872 | tf_op jit(solution)/shard_map/ppermute | solution.py:1037
  382.9 2.6 copy-start.4
  382.9 39.2 %collective-permute-start.19 = (bf16[128,2048]{1,0:T(8,128)(2,1)S(1)}, bf16[128,2048]{1,0:T(8,128)(2,1)}, u32[]{:S(2)}, u32[]{:S(2)}) collective-permute-start(bf16[128,2048]{1,0:T(8,128)(2,1)S(1)} %collective-permute-done.16.refs_0_), channel_id=1, source_target_pairs={{0,1},{1,0},{2,3},{3,2},{4,5},{5,4},{6,7},{7,6},{8,9},{9,8},{10,11... | collective-permute-start | bytes 1572872 | tf_op jit(solution)/shard_map/ppermute | solution.py:1037
  384.2 1.4 copy-start.5
  384.2 37.9 %collective-permute-start.20 = (bf16[128,2048]{1,0:T(8,128)(2,1)S(1)}, bf16[128,2048]{1,0:T(8,128)(2,1)}, u32[]{:S(2)}, u32[]{:S(2)}) collective-permute-start(bf16[128,2048]{1,0:T(8,128)(2,1)S(1)} %collective-permute-done.18.refs_1_), channel_id=1, source_target_pairs={{0,1},{1,0},{2,3},{3,2},{4,5},{5,4},{6,7},{7,6},{8,9},{9,8},{10,11... | collective-permute-start | bytes 1572872 | tf_op jit(solution)/shard_map/ppermute | solution.py:1037
  384.2 0.8 copy-start.7
  384.2 34.8 %collective-permute-start.7 = (bf16[32,6144]{1,0:T(8,128)(2,1)}, bf16[32,6144]{1,0:T(8,128)(2,1)}, u32[]{:S(2)}, u32[]{:S(2)}) collective-permute-start(bf16[32,6144]{1,0:T(8,128)(2,1)} %collective-permute-done.4.refs_0_), channel_id=1, source_target_pairs={{0,1},{1,0},{2,3},{3,2},{4,5},{5,4},{6,7},{7,6},{8,9},{9,8},{10,11... | collective-permute-start | bytes 1179656 | tf_op jit(solution)/shard_map/ppermute | solution.py:1037
  384.7 0.8 copy-start.8
  384.7 34.3 %collective-permute-start.8 = (bf16[32,6144]{1,0:T(8,128)(2,1)}, bf16[32,6144]{1,0:T(8,128)(2,1)}, u32[]{:S(2)}, u32[]{:S(2)}) collective-permute-start(bf16[32,6144]{1,0:T(8,128)(2,1)} %collective-permute-done.6.refs_1_), channel_id=1, source_target_pairs={{0,1},{1,0},{2,3},{3,2},{4,5},{5,4},{6,7},{7,6},{8,9},{9,8},{10,11... | collective-permute-start | bytes 1179656 | tf_op jit(solution)/shard_map/ppermute | solution.py:1037

commit v3 on v2

--- a/solution.py
+++ b/solution.py
@@ -392,6 +392,11 @@
                 for u in range(NT):
                     leaving[v][0][u, j] = value[u * T : (u + 1) * T]
 
+            def leave_now(*arrays):
+                for v in arrays:
+                    for u in range(NT):
+                        depart(v, u, j).start()
+
             gain_1, shift_1, gain_2, shift_2 = [norms_ref[v : v + 1, :] for v in range(4)]
             wide = join(in_all).astype(F32)
             offsets = wide - jnp.mean(wide, axis=-1, keepdims=True)
@@ -401,6 +406,7 @@
             second = (normed * gain_2 + shift_2).astype(BF16)
             put(0, first)
             put(1, second)
+            leave_now(8)
             grad = join(grad_all)
             sum_grad_ref[...] += jnp.sum(grad.astype(F32), axis=0, keepdims=True)
 
@@ -413,6 +419,7 @@
             sum_up_ref[...] += jnp.sum(hidden_grad, axis=0, keepdims=True)
             hidden_low = hidden_grad.astype(BF16)
             put(5, hidden_low)
+            leave_now(0, 1, 3)
 
             @pl.when(i == 0)
             def _():
@@ -465,6 +472,7 @@
 
             branch = dot(attended, out_all[...], 1, 0) + dot(activated, down_all[...], 1, 0)
             put(6, branch.astype(BF16))
+            leave_now(2, 4, 5)
             first_grad = dot(mixed_low, qkv_all[...], 1, 1)
             second_grad = dot(hidden_low, up_all[...], 1, 1)
             sum_norm_ref[0:1, :] += jnp.sum(first_grad * normed, axis=0, keepdims=True)
@@ -472,9 +480,7 @@
             sum_norm_ref[2:3, :] += jnp.sum(second_grad * normed, axis=0, keepdims=True)
             sum_norm_ref[3:4, :] += jnp.sum(second_grad, axis=0, keepdims=True)
             put(7, (first_grad * gain_1 + second_grad * gain_2).astype(BF16))
-            for v in range(len(leaving)):
-                for u in range(NT):
-                    depart(v, u, j).start()
+            leave_now(6, 7)
             return carry
 
         lax.fori_loop(0, S, compute, 0)
@@ -1114,14 +1120,17 @@
         scaled = []
         for k in range(1, S):
             scaled.append(lax.ppermute(inner_rest[k - 1], "shard", [(i, (i + k) % S) for i in range(S)]))
+        grad_w_up = widen(whole_up)
+        grad_w_out = widen(whole_out)
+        grad_w_down = placed(unwritten(w_down.shape, F32), 0, pieces_of(0, [0]), down_row)
+        grad_w_qkv = placed(unwritten(w_qkv.shape, F32), 1, pieces_of(1, [0]), qkv_row)
+        grad_w_down = placed(grad_w_down, 0, pieces_of(0, DP), down_row)
+        grad_w_qkv = placed(grad_w_qkv, 1, pieces_of(1, DP), qkv_row)
+        bias, grad_w_qkv = lax.optimization_barrier((bias, grad_w_qkv))
         block_out, in_grad, *smalls = finish(
             block_in, out_grad, branch_own, bias, inner_own, scaled, sums, s,
             [v.shape[0] * S // 128 for v in (b_qkv, b_out, b_up) + (first_gain,) * 4], S,
         )
-        grad_w_up = widen(whole_up)
-        grad_w_out = widen(whole_out)
-        grad_w_down = placed(unwritten(w_down.shape, F32), 0, pieces_of(0, [0] + DP), down_row)
-        grad_w_qkv = placed(unwritten(w_qkv.shape, F32), 1, pieces_of(1, [0] + DP), qkv_row)
         if several:
             grad_w_down = placed(grad_w_down, 0, pieces_of(0, several), down_row)
             grad_w_qkv = placed(grad_w_qkv, 1, pieces_of(1, several), qkv_row)

time: 434 us -> 437 us (level); the launches traced: 426 us -> 437 us
  waiting for transfers between devices: 75.7 us -> 84 us
    ppermute x3, waiting for transfers between devices: 25.2 us -> 34.2 us  [body(): lax.ppermute(inner_rest[k - 1], 'shard', [(i, (i + k) % S) for i in range...]
    pallas_call x4 -> x6, Pallas kernels: 20.4 us -> 23.7 us  [place(): pl.pallas_call(kernel, in_specs=[pl.BlockSpec(memory_space=pltpu.SMEM)] +...]
  transfers between devices with their start and end apart: 27 -> 27, of which waited for: 10 -> 11; matrix products, arithmetic and copies ran while one was open for 1% -> 1% of each run, Pallas kernels for 8% -> 9%
where the time goes in v3:
time: 437 us
  Pallas kernels  328 us (75%)
  waiting for transfers between devices  84 us (19%)
  starting transfers between devices  17.1 us (4%)
  other arithmetic  4.66 us (1%)
    pallas_call x1, Pallas kernels, grads(): pl.pallas_call(kernel, out_shape=outs, in_specs=[any_spec] * 10, out_spec...  164 us
    pallas_call x1, Pallas kernels, layer(): pl.pallas_call(kernel, out_shape=outs, in_specs=[any_spec] * 7 + [vmem_sp...  124 us
    ppermute x24, waiting for transfers between devices, flip(): return lax.ppermute(value, 'replica', [(i, i ^ bit) for i in range(R)])  49.9 us
    ppermute x3, waiting for transfers between devices, body(): lax.ppermute(inner_rest[k - 1], 'shard', [(i, (i + k) % S) for i in range...  34.2 us
    pallas_call x6, Pallas kernels, place(): pl.pallas_call(kernel, in_specs=[pl.BlockSpec(memory_space=pltpu.SMEM)] +...  23.7 us
    ppermute x24, starting transfers between devices, flip(): return lax.ppermute(value, 'replica', [(i, i ^ bit) for i in range(R)])  13.8 us
    pallas_call x2, Pallas kernels, widen(): pl.pallas_call(kernel, grid=(rows // n,), in_specs=[spec], out_specs=spec...  12.9 us
  transfers between devices with their start and end apart: 27, of which 11 were waited for; matrix products, arithmetic and copies ran while one was open for 1% of the time, Pallas kernels for 9%

profile of v3, /device:TPU:0, one launch (start us, length us, event | category | flops | bytes accessed | tf_op | source)
XLA Modules:
  0.0 437.0 jit_solution(11132962349244009233)
XLA Ops:
  0.6 0.7 convert_element_type.3
  1.3 1.4 add_bitcast_fusion.small_ref
  2.7 124.1 %layer.1 = (bf16[2,4,128,2048]{3,2,1,0:T(8,128)(2,1)}, bf16[2,4,128,2048]{3,2,1,0:T(8,128)(2,1)}, bf16[2,4,128,256]{3,2,1,0:T(8,128)(2,1)}, bf16[2,4,128,1024]{3...) custom-call(bf16[53,128]{1,0:T(8,128)(2,1)} %add_bitcast_fusion.smal, ...), custom_call_target="tpu_custom_call" | custom-call | flops 25769803776 | bytes 83886080 | tf_op jit(solution)/shard_map/layer/pallas_call | solution.py:535
  126.8 163.6 %grads.1 = (bf16[512,8192]{1,0:T(8,128)(2,1)}, bf16[512,2048]{1,0:T(8,128)(2,1)}, bf16[128,2048]{1,0:T(8,128)(2,1)}, bf16[128,2048]{1,0:T(8,128)(2,1)}, bf16[32,...) custom-call(bf16[1024,2048]{1,0:T(8,128)(2,1)} %bitcast.59, ...), custom_call_target="tpu_custom_call" | custom-call | flops 12884901888 | bytes 75497472 | tf_op jit(solution)/shard_map/grads/pallas_call | solution.py:990
  290.4 1.4 collective-permute-start
  291.8 0.7 collective-permute-start.3
  292.5 1.5 collective-permute-start.15
  294.0 0.5 collective-permute-start.17
  294.5 1.5 collective-permute-start.1
  296.0 6.6 %collective-permute-done.refs_0_ = bf16[32,6144]{1,0:T(8,128)(2,1)S(1)} collective-permute-done((bf16[32,6144]{1,0:T(8,128)(2,1)}, bf16[32,6144]{1,0:T(8,128)(2,1)S(1)}, u32[]{:S(2)}, u32[]{:S(2)}) %collective-permute-start) | collective-permute-done | bytes 393248 | tf_op jit(solution)/shard_map/ppermute | solution.py:1043
  302.6 1.3 collective-permute-start.2
  304.0 0.0 collective-permute-done.3.refs_3_
  304.0 0.7 collective-permute-start.21
  304.7 18.9 %collective-permute-done.1.refs_1_ = bf16[32,6144]{1,0:T(8,128)(2,1)S(1)} collective-permute-done((bf16[32,6144]{1,0:T(8,128)(2,1)}, bf16[32,6144]{1,0:T(8,128)(2,1)S(1)}, u32[]{:S(2)}, u32[]{:S(2)}) %collective-permute-start.1) | collective-permute-done | bytes 393248 | tf_op jit(solution)/shard_map/ppermute | solution.py:1043
  323.6 0.7 collective-permute-start.22
  324.3 2.7 collective-permute-start.10
  327.1 0.0 collective-permute-done.15.refs_0_
  327.1 0.0 collective-permute-start.8
  327.1 0.6 collective-permute-start.9
  327.7 6.3 %collective-permute-done.21.refs_1_ = bf16[128,2048]{1,0:T(8,128)(2,1)S(1)} collective-permute-done((bf16[128,2048]{1,0:T(8,128)(2,1)}, bf16[128,2048]{1,0:T(8,128)(2,1)S(1)}, u32[]{:S(2)}, u32[]{:S(2)}) %collective-permute-start.21) | collective-permute-done | bytes 524320 | tf_op jit(solution)/shard_map/ppermute | solution.py:1043
  334.0 0.0 collective-permute-start.4
  334.0 2.1 collective-permute-done.22.refs_2_
  336.1 11.5 %collective-permute-done.10.refs_2_ = bf16[128,2048]{1,0:T(8,128)(2,1)S(1)} collective-permute-done((bf16[128,2048]{1,0:T(8,128)(2,1)}, bf16[128,2048]{1,0:T(8,128)(2,1)S(1)}, u32[]{:S(2)}, u32[]{:S(2)}) %collective-permute-start.10) | collective-permute-done | bytes 524320 | tf_op jit(solution)/shard_map/ppermute | solution.py:1122
  347.6 3.8 collective-permute-done.8.refs_0_
  351.4 0.0 collective-permute-start.6
  351.4 18.8 %collective-permute-done.9.refs_1_ = bf16[128,2048]{1,0:T(8,128)(2,1)S(1)} collective-permute-done((bf16[128,2048]{1,0:T(8,128)(2,1)}, bf16[128,2048]{1,0:T(8,128)(2,1)S(1)}, u32[]{:S(2)}, u32[]{:S(2)}) %collective-permute-start.9) | collective-permute-done | bytes 524320 | tf_op jit(solution)/shard_map/ppermute | solution.py:1122
  370.2 1.5 collective-permute-start.11
  371.7 0.0 collective-permute-done.4.refs_4_
  371.7 0.6 collective-permute-start.12
  372.3 0.0 collective-permute-done.7.refs_7_
  372.3 0.1 collective-permute-start.23
  372.4 1.3 collective-permute-start.16
  373.8 0.8 collective-permute-start.18
  374.6 7.0 %collective-permute-done.11.refs_0_ = bf16[32,6144]{1,0:T(8,128)(2,1)S(1)} collective-permute-done((bf16[32,6144]{1,0:T(8,128)(2,1)S(1)}, bf16[32,6144]{1,0:T(8,128)(2,1)S(1)}, u32[]{:S(2)}, u32[]{:S(2)}) %collective-permute-start.11) | collective-permute-done | bytes 393248 | tf_op jit(solution)/shard_map/ppermute | solution.py:1043
  381.6 0.0 collective-permute-start.26
  381.6 1.4 collective-permute-done.12.refs_1_
  383.0 0.0 collective-permute-start.24
  383.0 0.0 collective-permute-done.23.refs_4_
  383.0 0.5 collective-permute-start.25
  383.5 6.3 %collective-permute-done.16.refs_0_ = bf16[128,2048]{1,0:T(8,128)(2,1)S(1)} collective-permute-done((bf16[128,2048]{1,0:T(8,128)(2,1)S(1)}, bf16[128,2048]{1,0:T(8,128)(2,1)S(1)}, u32[]{:S(2)}, u32[]{:S(2)}) %collective-permute-start.16) | collective-permute-done | bytes 524320 | tf_op jit(solution)/shard_map/ppermute | solution.py:1043
  389.8 1.2 collective-permute-done.18.refs_1_
  391.0 0.0 collective-permute-start.20
  391.2 0.0 collective-permute-done.26.refs_7_
  391.2 0.5 collective-permute-start.13
  391.7 0.0 collective-permute-done.24.refs_5_
  391.7 0.1 collective-permute-start.14
  391.8 0.6 pad_add_fusion.3.rows_ref
  392.6 9.5 %widen.3 = f32[512,8192]{1,0:T(8,128)} custom-call(bf16[512,8192]{1,0:T(8,128)(2,1)} %get-tuple-element.81.in_ref), custom_call_target="tpu_custom_call" | custom-call | bytes 25165824 | tf_op jit(solution)/shard_map/widen/pallas_call | solution.py:47
  402.2 3.4 widen.2
  405.5 3.6 place.9.refs_8_
  409.2 0.7 pad_add_fusion.rows_ref
  409.8 3.1 place.6.refs_8_
  412.9 0.7 stack.146.rows_ref
  413.6 0.6 stack.122.rows_ref
  414.2 0.7 pad_add_fusion.2.rows_ref
  414.9 0.6 pad_add_fusion.1.rows_ref
  415.5 4.6 %place.7.refs_4_ = f32[512,6144]{1,0:T(8,128)} custom-call(s32[8]{0:T(128)} %stack.122.rows_ref, bf16[32,6144]{1,0:T(8,128)(2,1)} %copy-done.12, bf16[32,6144]{1,0:T(8,128)(2,1)} %copy-done.14, bf16[32,6144]{1,0:T(8,128)(2,1)} %copy-done.15, bf16[32,6144]{1,0:T(8,128)(2,1)} %copy-done.13, ...), custom_call_target="tpu_custom_call", output_to_operand_aliasing={{}: (9, {})} | custom-call | bytes 9437184 | tf_op jit(solution)/shard_map/place/pallas_call | solution.py:75
  420.1 4.2 finish.1
  424.4 5.6 %place.10.refs_4_ = f32[2048,2048]{1,0:T(8,128)} custom-call(s32[8]{0:T(128)} %stack.146.rows_ref, bf16[128,2048]{1,0:T(8,128)(2,1)} %copy-done, bf16[128,2048]{1,0:T(8,128)(2,1)} %copy-done.2, bf16[128,2048]{1,0:T(8,128)(2,1)} %copy-done.3, bf16[128,2048]{1,0:T(8,128)(2,1)} %copy-done.1, ...), custom_call_target="tpu_custom_call", output_to_operand_aliasing={{}: (9, {})} | custom-call | bytes 12582912 | tf_op jit(solution)/shard_map/place/pallas_call | solution.py:75
  430.0 0.0 collective-permute-done.14.refs_3_
  430.0 3.1 place.8
  433.1 0.0 collective-permute-done.19.refs_2_
  433.2 0.0 collective-permute-done.20.refs_3_
  433.2 3.6 place.11
  (49 shorter events, 0.1 us)
Async XLA Ops:
  290.4 12.3 %collective-permute-start = (bf16[32,6144]{1,0:T(8,128)(2,1)}, bf16[32,6144]{1,0:T(8,128)(2,1)S(1)}, u32[]{:S(2)}, u32[]{:S(2)}) collective-permute-start(bf16[32,6144]{1,0:T(8,128)(2,1)} %get-tuple-element.65.refs_0_), channel_id=1, source_target_pairs={{0,2},{1,3},{2,0},{3,1},{4,6},{5,7},{6,4},{7,5},{8,10},{9,11},{10,... | collective-permute-start | bytes 1179656 | tf_op jit(solution)/shard_map/ppermute | solution.py:1043
  291.8 12.2 %collective-permute-start.3 = (bf16[32,6144]{1,0:T(8,128)(2,1)}, bf16[32,6144]{1,0:T(8,128)(2,1)S(1)}, u32[]{:S(2)}, u32[]{:S(2)}) collective-permute-start(bf16[32,6144]{1,0:T(8,128)(2,1)} %get-tuple-element.66.refs_1_), channel_id=1, source_target_pairs={{0,4},{1,5},{2,6},{3,7},{4,0},{5,1},{6,2},{7,3},{8,12},{9,13},{10,... | collective-permute-start | bytes 1179656 | tf_op jit(solution)/shard_map/ppermute | solution.py:1043
  292.5 34.6 %collective-permute-start.15 = (bf16[128,2048]{1,0:T(8,128)(2,1)}, bf16[128,2048]{1,0:T(8,128)(2,1)S(1)}, u32[]{:S(2)}, u32[]{:S(2)}) collective-permute-start(bf16[128,2048]{1,0:T(8,128)(2,1)} %get-tuple-element.83.refs_0_), channel_id=1, source_target_pairs={{0,2},{1,3},{2,0},{3,1},{4,6},{5,7},{6,4},{7,5},{8,10},{9,11},{10,... | collective-permute-start | bytes 1572872 | tf_op jit(solution)/shard_map/ppermute | solution.py:1043
  294.0 33.1 %collective-permute-start.17 = (bf16[128,2048]{1,0:T(8,128)(2,1)}, bf16[128,2048]{1,0:T(8,128)(2,1)S(1)}, u32[]{:S(2)}, u32[]{:S(2)}) collective-permute-start(bf16[128,2048]{1,0:T(8,128)(2,1)} %get-tuple-element.84.refs_1_), channel_id=1, source_target_pairs={{0,4},{1,5},{2,6},{3,7},{4,0},{5,1},{6,2},{7,3},{8,12},{9,13},{10,... | collective-permute-start | bytes 1572872 | tf_op jit(solution)/shard_map/ppermute | solution.py:1043
  294.5 29.1 %collective-permute-start.1 = (bf16[32,6144]{1,0:T(8,128)(2,1)}, bf16[32,6144]{1,0:T(8,128)(2,1)S(1)}, u32[]{:S(2)}, u32[]{:S(2)}) collective-permute-start(bf16[32,6144]{1,0:T(8,128)(2,1)} %get-tuple-element.65.refs_0_), channel_id=1, source_target_pairs={{0,4},{1,5},{2,6},{3,7},{4,0},{5,1},{6,2},{7,3},{8,12},{9,13},{10,... | collective-permute-start | bytes 1179656 | tf_op jit(solution)/shard_map/ppermute | solution.py:1043
  302.6 88.4 %copy-start.12 = (bf16[32,6144]{1,0:T(8,128)(2,1)}, bf16[32,6144]{1,0:T(8,128)(2,1)S(1)}, u32[]{:S(2)}) copy-start(bf16[32,6144]{1,0:T(8,128)(2,1)S(1)} %collective-permute-done.refs_0_) | copy-start | bytes 1179652
  302.6 21.7 %collective-permute-start.2 = (bf16[32,6144]{1,0:T(8,128)(2,1)}, bf16[32,6144]{1,0:T(8,128)(2,1)S(1)}, u32[]{:S(2)}, u32[]{:S(2)}) collective-permute-start(bf16[32,6144]{1,0:T(8,128)(2,1)} %get-tuple-element.66.refs_1_), channel_id=1, source_target_pairs={{0,2},{1,3},{2,0},{3,1},{4,6},{5,7},{6,4},{7,5},{8,10},{9,11},{10,... | collective-permute-start | bytes 1179656 | tf_op jit(solution)/shard_map/ppermute | solution.py:1043
  304.0 87.1 %copy-start.13 = (bf16[32,6144]{1,0:T(8,128)(2,1)}, bf16[32,6144]{1,0:T(8,128)(2,1)S(1)}, u32[]{:S(2)}) copy-start(bf16[32,6144]{1,0:T(8,128)(2,1)S(1)} %collective-permute-done.3.refs_3_) | copy-start | bytes 1179652
  304.0 30.0 %collective-permute-start.21 = (bf16[128,2048]{1,0:T(8,128)(2,1)}, bf16[128,2048]{1,0:T(8,128)(2,1)S(1)}, u32[]{:S(2)}, u32[]{:S(2)}) collective-permute-start(bf16[128,2048]{1,0:T(8,128)(2,1)} %get-tuple-element.83.refs_0_), channel_id=1, source_target_pairs={{0,4},{1,5},{2,6},{3,7},{4,0},{5,1},{6,2},{7,3},{8,12},{9,13},{10,... | collective-permute-start | bytes 1572872 | tf_op jit(solution)/shard_map/ppermute | solution.py:1043
  323.6 48.8 %copy-start.14 = (bf16[32,6144]{1,0:T(8,128)(2,1)}, bf16[32,6144]{1,0:T(8,128)(2,1)S(1)}, u32[]{:S(2)}) copy-start(bf16[32,6144]{1,0:T(8,128)(2,1)S(1)} %collective-permute-done.1.refs_1_) | copy-start | bytes 1179652
  323.6 12.4 %collective-permute-start.22 = (bf16[128,2048]{1,0:T(8,128)(2,1)}, bf16[128,2048]{1,0:T(8,128)(2,1)S(1)}, u32[]{:S(2)}, u32[]{:S(2)}) collective-permute-start(bf16[128,2048]{1,0:T(8,128)(2,1)} %get-tuple-element.84.refs_1_), channel_id=1, source_target_pairs={{0,2},{1,3},{2,0},{3,1},{4,6},{5,7},{6,4},{7,5},{8,10},{9,11},{10,... | collective-permute-start | bytes 1572872 | tf_op jit(solution)/shard_map/ppermute | solution.py:1043
  324.3 49.4 %copy-start.15 = (bf16[32,6144]{1,0:T(8,128)(2,1)}, bf16[32,6144]{1,0:T(8,128)(2,1)S(1)}, u32[]{:S(2)}) copy-start(bf16[32,6144]{1,0:T(8,128)(2,1)S(1)} %collective-permute-done.2.refs_2_) | copy-start | bytes 1179652
  324.3 23.3 %collective-permute-start.10 = (bf16[128,2048]{1,0:T(8,128)(2,1)}, bf16[128,2048]{1,0:T(8,128)(2,1)S(1)}, u32[]{:S(2)}, u32[]{:S(2)}) collective-permute-start(bf16[128,2048]{1,0:T(8,128)(2,1)} %get-tuple-element.74), channel_id=1, source_target_pairs={{0,24},{8,0},{16,8},{24,16},{1,25},{9,1},{17,9},{25,17},{2,26},{10... | collective-permute-start | bytes 1572872 | tf_op jit(solution)/shard_map/ppermute | solution.py:1122
  327.1 65.4 %copy-start = (bf16[128,2048]{1,0:T(8,128)(2,1)}, bf16[128,2048]{1,0:T(8,128)(2,1)S(1)}, u32[]{:S(2)}) copy-start(bf16[128,2048]{1,0:T(8,128)(2,1)S(1)} %collective-permute-done.15.refs_0_) | copy-start | bytes 1572868
  327.1 24.3 %collective-permute-start.8 = (bf16[128,2048]{1,0:T(8,128)(2,1)}, bf16[128,2048]{1,0:T(8,128)(2,1)S(1)}, u32[]{:S(2)}, u32[]{:S(2)}) collective-permute-start(bf16[128,2048]{1,0:T(8,128)(2,1)} %get-tuple-element.72), channel_id=1, source_target_pairs={{0,8},{8,16},{16,24},{24,0},{1,9},{9,17},{17,25},{25,1},{2,10},{10... | collective-permute-start | bytes 1572872 | tf_op jit(solution)/shard_map/ppermute | solution.py:1122
  327.1 65.4 %copy-start.1 = (bf16[128,2048]{1,0:T(8,128)(2,1)}, bf16[128,2048]{1,0:T(8,128)(2,1)S(1)}, u32[]{:S(2)}) copy-start(bf16[128,2048]{1,0:T(8,128)(2,1)S(1)} %collective-permute-done.17.refs_3_) | copy-start | bytes 1572868
  327.1 43.1 %collective-permute-start.9 = (bf16[128,2048]{1,0:T(8,128)(2,1)}, bf16[128,2048]{1,0:T(8,128)(2,1)S(1)}, u32[]{:S(2)}, u32[]{:S(2)}) collective-permute-start(bf16[128,2048]{1,0:T(8,128)(2,1)} %get-tuple-element.73), channel_id=1, source_target_pairs={{0,16},{8,24},{16,0},{24,8},{1,17},{9,25},{17,1},{25,9},{2,18},{10... | collective-permute-start | bytes 1572872 | tf_op jit(solution)/shard_map/ppermute | solution.py:1122
  334.0 58.5 %copy-start.2 = (bf16[128,2048]{1,0:T(8,128)(2,1)}, bf16[128,2048]{1,0:T(8,128)(2,1)S(1)}, u32[]{:S(2)}) copy-start(bf16[128,2048]{1,0:T(8,128)(2,1)S(1)} %collective-permute-done.21.refs_1_) | copy-start | bytes 1572868
  334.0 37.7 %collective-permute-start.4 = (bf16[32,6144]{1,0:T(8,128)(2,1)S(1)}, bf16[32,6144]{1,0:T(8,128)(2,1)}, u32[]{:S(2)}, u32[]{:S(2)}) collective-permute-start(bf16[32,6144]{1,0:T(8,128)(2,1)S(1)} %collective-permute-done.refs_0_), channel_id=1, source_target_pairs={{0,1},{1,0},{2,3},{3,2},{4,5},{5,4},{6,7},{7,6},{8,9},{9,8},{10,11... | collective-permute-start | bytes 1179656 | tf_op jit(solution)/shard_map/ppermute | solution.py:1043
  336.1 56.4 %copy-start.3 = (bf16[128,2048]{1,0:T(8,128)(2,1)}, bf16[128,2048]{1,0:T(8,128)(2,1)S(1)}, u32[]{:S(2)}) copy-start(bf16[128,2048]{1,0:T(8,128)(2,1)S(1)} %collective-permute-done.22.refs_2_) | copy-start | bytes 1572868
  336.1 36.2 %collective-permute-start.7 = (bf16[32,6144]{1,0:T(8,128)(2,1)S(1)}, bf16[32,6144]{1,0:T(8,128)(2,1)S(1)}, u32[]{:S(2)}, u32[]{:S(2)}) collective-permute-start(bf16[32,6144]{1,0:T(8,128)(2,1)S(1)} %collective-permute-done.3.refs_3_), channel_id=1, source_target_pairs={{0,1},{1,0},{2,3},{3,2},{4,5},{5,4},{6,7},{7,6},{8,9},{9,8},{10,11... | collective-permute-start | bytes 1179656 | tf_op jit(solution)/shard_map/ppermute | solution.py:1043
  347.6 24.7 %copy-start.7 = (bf16[128,2048]{1,0:T(8,128)(2,1)}, bf16[128,2048]{1,0:T(8,128)(2,1)S(1)}, u32[]{:S(2)}) copy-start(bf16[128,2048]{1,0:T(8,128)(2,1)S(1)} %collective-permute-done.10.refs_2_) | copy-start | bytes 1572868
  347.6 24.8 %collective-permute-start.5 = (bf16[32,6144]{1,0:T(8,128)(2,1)S(1)}, bf16[32,6144]{1,0:T(8,128)(2,1)S(1)}, u32[]{:S(2)}, u32[]{:S(2)}) collective-permute-start(bf16[32,6144]{1,0:T(8,128)(2,1)S(1)} %collective-permute-done.1.refs_1_), channel_id=1, source_target_pairs={{0,1},{1,0},{2,3},{3,2},{4,5},{5,4},{6,7},{7,6},{8,9},{9,8},{10,11... | collective-permute-start | bytes 1179656 | tf_op jit(solution)/shard_map/ppermute | solution.py:1043
  351.4 39.7 %copy-start.8 = (bf16[128,2048]{1,0:T(8,128)(2,1)}, bf16[128,2048]{1,0:T(8,128)(2,1)S(1)}, u32[]{:S(2)}) copy-start(bf16[128,2048]{1,0:T(8,128)(2,1)S(1)} %collective-permute-done.8.refs_0_) | copy-start | bytes 1572868
  351.4 22.4 %collective-permute-start.6 = (bf16[32,6144]{1,0:T(8,128)(2,1)S(1)}, bf16[32,6144]{1,0:T(8,128)(2,1)S(1)}, u32[]{:S(2)}, u32[]{:S(2)}) collective-permute-start(bf16[32,6144]{1,0:T(8,128)(2,1)S(1)} %collective-permute-done.2.refs_2_), channel_id=1, source_target_pairs={{0,1},{1,0},{2,3},{3,2},{4,5},{5,4},{6,7},{7,6},{8,9},{9,8},{10,11... | collective-permute-start | bytes 1179656 | tf_op jit(solution)/shard_map/ppermute | solution.py:1043
  370.2 20.8 %copy-start.9 = (bf16[128,2048]{1,0:T(8,128)(2,1)}, bf16[128,2048]{1,0:T(8,128)(2,1)S(1)}, u32[]{:S(2)}) copy-start(bf16[128,2048]{1,0:T(8,128)(2,1)S(1)} %collective-permute-done.9.refs_1_) | copy-start | bytes 1572868
  370.2 11.3 %collective-permute-start.11 = (bf16[32,6144]{1,0:T(8,128)(2,1)S(1)}, bf16[32,6144]{1,0:T(8,128)(2,1)S(1)}, u32[]{:S(2)}, u32[]{:S(2)}) collective-permute-start(bf16[32,6144]{1,0:T(8,128)(2,1)S(1)} %collective-permute-done.refs_0_), channel_id=1, source_target_pairs={{0,4},{1,5},{2,6},{3,7},{4,0},{5,1},{6,2},{7,3},{8,12},{9,13},{10,... | collective-permute-start | bytes 1179656 | tf_op jit(solution)/shard_map/ppermute | solution.py:1043
  371.7 11.2 %collective-permute-start.12 = (bf16[32,6144]{1,0:T(8,128)(2,1)S(1)}, bf16[32,6144]{1,0:T(8,128)(2,1)S(1)}, u32[]{:S(2)}, u32[]{:S(2)}) collective-permute-start(bf16[32,6144]{1,0:T(8,128)(2,1)S(1)} %collective-permute-done.3.refs_3_), channel_id=1, source_target_pairs={{0,2},{1,3},{2,0},{3,1},{4,6},{5,7},{6,4},{7,5},{8,10},{9,11},{10,... | collective-permute-start | bytes 1179656 | tf_op jit(solution)/shard_map/ppermute | solution.py:1043
  372.3 18.8 %copy-start.16 = (bf16[32,6144]{1,0:T(8,128)(2,1)}, bf16[32,6144]{1,0:T(8,128)(2,1)S(1)}, u32[]{:S(2)}) copy-start(bf16[32,6144]{1,0:T(8,128)(2,1)S(1)} %collective-permute-done.7.refs_7_) | copy-start | bytes 1179652
  372.3 10.7 %collective-permute-start.23 = (bf16[128,2048]{1,0:T(8,128)(2,1)S(1)}, bf16[128,2048]{1,0:T(8,128)(2,1)S(1)}, u32[]{:S(2)}, u32[]{:S(2)}) collective-permute-start(bf16[128,2048]{1,0:T(8,128)(2,1)S(1)} %collective-permute-done.15.refs_0_), channel_id=1, source_target_pairs={{0,1},{1,0},{2,3},{3,2},{4,5},{5,4},{6,7},{7,6},{8,9},{9,8},{10,11... | collective-permute-start | bytes 1572872 | tf_op jit(solution)/shard_map/ppermute | solution.py:1043
  372.4 18.7 %copy-start.17 = (bf16[32,6144]{1,0:T(8,128)(2,1)}, bf16[32,6144]{1,0:T(8,128)(2,1)S(1)}, u32[]{:S(2)}) copy-start(bf16[32,6144]{1,0:T(8,128)(2,1)S(1)} %collective-permute-done.5.refs_5_) | copy-start | bytes 1179652
  372.4 17.4 %collective-permute-start.16 = (bf16[128,2048]{1,0:T(8,128)(2,1)S(1)}, bf16[128,2048]{1,0:T(8,128)(2,1)S(1)}, u32[]{:S(2)}, u32[]{:S(2)}) collective-permute-start(bf16[128,2048]{1,0:T(8,128)(2,1)S(1)} %collective-permute-done.15.refs_0_), channel_id=1, source_target_pairs={{0,4},{1,5},{2,6},{3,7},{4,0},{5,1},{6,2},{7,3},{8,12},{9,13},{10,... | collective-permute-start | bytes 1572872 | tf_op jit(solution)/shard_map/ppermute | solution.py:1043
  373.8 17.3 %copy-start.18 = (bf16[32,6144]{1,0:T(8,128)(2,1)}, bf16[32,6144]{1,0:T(8,128)(2,1)S(1)}, u32[]{:S(2)}) copy-start(bf16[32,6144]{1,0:T(8,128)(2,1)S(1)} %collective-permute-done.6.refs_6_) | copy-start | bytes 1179652
  373.8 17.3 %collective-permute-start.18 = (bf16[128,2048]{1,0:T(8,128)(2,1)S(1)}, bf16[128,2048]{1,0:T(8,128)(2,1)S(1)}, u32[]{:S(2)}, u32[]{:S(2)}) collective-permute-start(bf16[128,2048]{1,0:T(8,128)(2,1)S(1)} %collective-permute-done.17.refs_3_), channel_id=1, source_target_pairs={{0,2},{1,3},{2,0},{3,1},{4,6},{5,7},{6,4},{7,5},{8,10},{9,11},{10,... | collective-permute-start | bytes 1572872 | tf_op jit(solution)/shard_map/ppermute | solution.py:1043
  381.6 20.6 %copy-start.10 = (bf16[32,6144]{1,0:T(8,128)(2,1)}, bf16[32,6144]{1,0:T(8,128)(2,1)S(1)}, u32[]{:S(2)}) copy-start(bf16[32,6144]{1,0:T(8,128)(2,1)S(1)} %collective-permute-done.11.refs_0_) | copy-start | bytes 1179652
  381.6 9.6 %collective-permute-start.26 = (bf16[128,2048]{1,0:T(8,128)(2,1)S(1)}, bf16[128,2048]{1,0:T(8,128)(2,1)}, u32[]{:S(2)}, u32[]{:S(2)}) collective-permute-start(bf16[128,2048]{1,0:T(8,128)(2,1)S(1)} %collective-permute-done.17.refs_3_), channel_id=1, source_target_pairs={{0,1},{1,0},{2,3},{3,2},{4,5},{5,4},{6,7},{7,6},{8,9},{9,8},{10,11... | collective-permute-start | bytes 1572872 | tf_op jit(solution)/shard_map/ppermute | solution.py:1043
  383.0 8.1 %copy-start.11 = (bf16[32,6144]{1,0:T(8,128)(2,1)}, bf16[32,6144]{1,0:T(8,128)(2,1)S(1)}, u32[]{:S(2)}) copy-start(bf16[32,6144]{1,0:T(8,128)(2,1)S(1)} %collective-permute-done.12.refs_1_) | copy-start | bytes 1179652
  383.0 8.8 %collective-permute-start.24 = (bf16[128,2048]{1,0:T(8,128)(2,1)S(1)}, bf16[128,2048]{1,0:T(8,128)(2,1)}, u32[]{:S(2)}, u32[]{:S(2)}) collective-permute-start(bf16[128,2048]{1,0:T(8,128)(2,1)S(1)} %collective-permute-done.21.refs_1_), channel_id=1, source_target_pairs={{0,1},{1,0},{2,3},{3,2},{4,5},{5,4},{6,7},{7,6},{8,9},{9,8},{10,11... | collective-permute-start | bytes 1572872 | tf_op jit(solution)/shard_map/ppermute | solution.py:1043
  383.0 8.1 %copy-start.6 = (bf16[128,2048]{1,0:T(8,128)(2,1)}, bf16[128,2048]{1,0:T(8,128)(2,1)S(1)}, u32[]{:S(2)}) copy-start(bf16[128,2048]{1,0:T(8,128)(2,1)S(1)} %collective-permute-done.23.refs_4_) | copy-start | bytes 1572868
  383.0 41.4 %collective-permute-start.25 = (bf16[128,2048]{1,0:T(8,128)(2,1)S(1)}, bf16[128,2048]{1,0:T(8,128)(2,1)}, u32[]{:S(2)}, u32[]{:S(2)}) collective-permute-start(bf16[128,2048]{1,0:T(8,128)(2,1)S(1)} %collective-permute-done.22.refs_2_), channel_id=1, source_target_pairs={{0,1},{1,0},{2,3},{3,2},{4,5},{5,4},{6,7},{7,6},{8,9},{9,8},{10,11... | collective-permute-start | bytes 1572872 | tf_op jit(solution)/shard_map/ppermute | solution.py:1043
  389.8 2.7 copy-start.4
  389.8 43.3 %collective-permute-start.19 = (bf16[128,2048]{1,0:T(8,128)(2,1)S(1)}, bf16[128,2048]{1,0:T(8,128)(2,1)}, u32[]{:S(2)}, u32[]{:S(2)}) collective-permute-start(bf16[128,2048]{1,0:T(8,128)(2,1)S(1)} %collective-permute-done.16.refs_0_), channel_id=1, source_target_pairs={{0,1},{1,0},{2,3},{3,2},{4,5},{5,4},{6,7},{7,6},{8,9},{9,8},{10,11... | collective-permute-start | bytes 1572872 | tf_op jit(solution)/shard_map/ppermute | solution.py:1043
  391.0 1.5 copy-start.5
  391.0 42.1 %collective-permute-start.20 = (bf16[128,2048]{1,0:T(8,128)(2,1)S(1)}, bf16[128,2048]{1,0:T(8,128)(2,1)}, u32[]{:S(2)}, u32[]{:S(2)}) collective-permute-start(bf16[128,2048]{1,0:T(8,128)(2,1)S(1)} %collective-permute-done.18.refs_1_), channel_id=1, source_target_pairs={{0,1},{1,0},{2,3},{3,2},{4,5},{5,4},{6,7},{7,6},{8,9},{9,8},{10,11... | collective-permute-start | bytes 1572872 | tf_op jit(solution)/shard_map/ppermute | solution.py:1043
  391.2 38.8 %collective-permute-start.13 = (bf16[32,6144]{1,0:T(8,128)(2,1)S(1)}, bf16[32,6144]{1,0:T(8,128)(2,1)}, u32[]{:S(2)}, u32[]{:S(2)}) collective-permute-start(bf16[32,6144]{1,0:T(8,128)(2,1)S(1)} %collective-permute-done.11.refs_0_), channel_id=1, source_target_pairs={{0,1},{1,0},{2,3},{3,2},{4,5},{5,4},{6,7},{7,6},{8,9},{9,8},{10,11... | collective-permute-start | bytes 1179656 | tf_op jit(solution)/shard_map/ppermute | solution.py:1043
  391.7 38.3 %collective-permute-start.14 = (bf16[32,6144]{1,0:T(8,128)(2,1)}, bf16[32,6144]{1,0:T(8,128)(2,1)}, u32[]{:S(2)}, u32[]{:S(2)}) collective-permute-start(bf16[32,6144]{1,0:T(8,128)(2,1)} %copy-done.11), channel_id=1, source_target_pairs={{0,1},{1,0},{2,3},{3,2},{4,5},{5,4},{6,7},{7,6},{8,9},{9,8},{10,11... | collective-permute-start | bytes 1179656 | tf_op jit(solution)/shard_map/ppermute | solution.py:1043

commit v4 on v3

--- a/solution.py
+++ b/solution.py
@@ -55,7 +55,7 @@
     )(value)
 
 
-def place(pieces, rows, result):
+def place(pieces, rows, first, result):
     n, width = pieces[0].shape
     count = len(pieces)
 
@@ -65,7 +65,7 @@
         copies = []
         for i in range(count):
             wide[i] = sources[i][...].astype(F32)
-            at = pl.multiple_of(rows_ref[i], n)
+            at = pl.multiple_of(rows_ref[first + i], n)
             copies.append(pltpu.make_async_copy(wide.at[i], target.at[pl.ds(at, n), :], go.at[i]))
             copies[-1].start()
         for copy in copies:
@@ -1092,14 +1092,28 @@
             dd, tt = indices(m)
             return ((dd * NT + tt) * 2 + half) * n
 
-        def placed(result, which, pieces, row):
+        several = [m for m in all_masks(DP) if m and m not in DP]
+        keys = [
+            (which, half, m | u)
+            for which in range(2)
+            for masks in ([0], DP, several)
+            for u in all_masks(TP)
+            for half in range(2)
+            for m in masks
+        ]
+        row_table = jnp.stack(
+            [(down_row, qkv_row)[w](half, m, owned_rows[2 * w].shape[0]) for w, half, m in keys]
+        )
+
+        def placed(result, which, pieces):
+            first = keys.index((which,) + pieces[0][:2])
             for bit in TP:
                 pieces = pieces + [
                     (half, m | bit, mates[0][2 * which + half] if m == 0 else flip(value, bit))
                     for half, m, value in pieces
                 ]
-            at = jnp.stack([row(half, m, value.shape[0]) for half, m, value in pieces])
-            return place([value for _, _, value in pieces], at, result)
+            assert keys[first : first + len(pieces)] == [(which, half, m) for half, m, _ in pieces]
+            return place([value for _, _, value in pieces], row_table, first, result)
 
         got = [[{0: owned_rows[2 * i + half]} for half in range(2)] for i in range(2)]
 
@@ -1108,7 +1122,6 @@
                 bit = [b for b in ways[half] if m & b][-1]
                 got[i][half][m] = flip(got[i][half][m ^ bit], bit)
 
-        several = [m for m in all_masks(DP) if m and m not in DP]
         for masks in (DP, several):
             for i in range(2):
                 for half in range(2):
@@ -1122,18 +1135,18 @@
             scaled.append(lax.ppermute(inner_rest[k - 1], "shard", [(i, (i + k) % S) for i in range(S)]))
         grad_w_up = widen(whole_up)
         grad_w_out = widen(whole_out)
-        grad_w_down = placed(unwritten(w_down.shape, F32), 0, pieces_of(0, [0]), down_row)
-        grad_w_qkv = placed(unwritten(w_qkv.shape, F32), 1, pieces_of(1, [0]), qkv_row)
-        grad_w_down = placed(grad_w_down, 0, pieces_of(0, DP), down_row)
-        grad_w_qkv = placed(grad_w_qkv, 1, pieces_of(1, DP), qkv_row)
+        grad_w_down = placed(unwritten(w_down.shape, F32), 0, pieces_of(0, [0]))
+        grad_w_qkv = placed(unwritten(w_qkv.shape, F32), 1, pieces_of(1, [0]))
+        grad_w_down = placed(grad_w_down, 0, pieces_of(0, DP))
+        grad_w_qkv = placed(grad_w_qkv, 1, pieces_of(1, DP))
         bias, grad_w_qkv = lax.optimization_barrier((bias, grad_w_qkv))
         block_out, in_grad, *smalls = finish(
             block_in, out_grad, branch_own, bias, inner_own, scaled, sums, s,
             [v.shape[0] * S // 128 for v in (b_qkv, b_out, b_up) + (first_gain,) * 4], S,
         )
         if several:
-            grad_w_down = placed(grad_w_down, 0, pieces_of(0, several), down_row)
-            grad_w_qkv = placed(grad_w_qkv, 1, pieces_of(1, several), qkv_row)
+            grad_w_down = placed(grad_w_down, 0, pieces_of(0, several))
+            grad_w_qkv = placed(grad_w_qkv, 1, pieces_of(1, several))
 
         grad_b_qkv, grad_b_out, grad_b_down, grad_b_up, *norm_grads = [v.reshape(-1) for v in smalls]
         return (

time: 437 us -> 435 us (level)
  transfers between devices with their start and end apart: 27 -> 27, of which waited for: 11 -> 11; matrix products, arithmetic and copies ran while one was open for 1% -> 0% of each run, Pallas kernels for 9% -> 9%
where the time goes in v4:
time: 435 us; the launch traced here: 434 us
  Pallas kernels  329 us (76%)
  waiting for transfers between devices  84 us (19%)
  starting transfers between devices  17.1 us (4%)
    pallas_call x1, Pallas kernels, grads(): pl.pallas_call(kernel, out_shape=outs, in_specs=[any_spec] * 10, out_spec...  164 us
    pallas_call x1, Pallas kernels, layer(): pl.pallas_call(kernel, out_shape=outs, in_specs=[any_spec] * 7 + [vmem_sp...  124 us
    ppermute x24, waiting for transfers between devices, flip(): return lax.ppermute(value, 'replica', [(i, i ^ bit) for i in range(R)])  49.9 us
    ppermute x3, waiting for transfers between devices, body(): lax.ppermute(inner_rest[k - 1], 'shard', [(i, (i + k) % S) for i in range...  34.1 us
    pallas_call x6, Pallas kernels, place(): pl.pallas_call(kernel, in_specs=[pl.BlockSpec(memory_space=pltpu.SMEM)] +...  23.7 us
    ppermute x24, starting transfers between devices, flip(): return lax.ppermute(value, 'replica', [(i, i ^ bit) for i in range(R)])  13.8 us
    pallas_call x2, Pallas kernels, widen(): pl.pallas_call(kernel, grid=(rows // n,), in_specs=[spec], out_specs=spec...  12.9 us
  transfers between devices with their start and end apart: 27, of which 11 were waited for; matrix products, arithmetic and copies ran while one was open for 0% of the time, Pallas kernels for 9%

profile of v4, /device:TPU:0, one launch (start us, length us, event | category | flops | bytes accessed | tf_op | source)
XLA Modules:
  0.0 434.3 jit_solution(8122402131961874776)
XLA Ops:
  0.6 0.7 convert_element_type.3
  1.3 1.4 add_bitcast_fusion.small_ref
  2.7 124.0 %layer.1 = (bf16[2,4,128,2048]{3,2,1,0:T(8,128)(2,1)}, bf16[2,4,128,2048]{3,2,1,0:T(8,128)(2,1)}, bf16[2,4,128,256]{3,2,1,0:T(8,128)(2,1)}, bf16[2,4,128,1024]{3...) custom-call(bf16[53,128]{1,0:T(8,128)(2,1)} %add_bitcast_fusion.smal, ...), custom_call_target="tpu_custom_call" | custom-call | flops 25769803776 | bytes 83886080 | tf_op jit(solution)/shard_map/layer/pallas_call | solution.py:535
  126.8 163.6 %grads.1 = (bf16[512,8192]{1,0:T(8,128)(2,1)}, bf16[512,2048]{1,0:T(8,128)(2,1)}, bf16[128,2048]{1,0:T(8,128)(2,1)}, bf16[128,2048]{1,0:T(8,128)(2,1)}, bf16[32,...) custom-call(bf16[1024,2048]{1,0:T(8,128)(2,1)} %bitcast.59, ...), custom_call_target="tpu_custom_call" | custom-call | flops 12884901888 | bytes 75497472 | tf_op jit(solution)/shard_map/grads/pallas_call | solution.py:990
  290.4 1.4 collective-permute-start
  291.8 0.7 collective-permute-start.3
  292.5 1.5 collective-permute-start.15
  294.0 0.5 collective-permute-start.17
  294.5 1.5 collective-permute-start.1
  296.0 6.6 %collective-permute-done.refs_0_ = bf16[32,6144]{1,0:T(8,128)(2,1)S(1)} collective-permute-done((bf16[32,6144]{1,0:T(8,128)(2,1)}, bf16[32,6144]{1,0:T(8,128)(2,1)S(1)}, u32[]{:S(2)}, u32[]{:S(2)}) %collective-permute-start) | collective-permute-done | bytes 393248 | tf_op jit(solution)/shard_map/ppermute | solution.py:1043
  302.7 1.3 collective-permute-start.2
  304.0 0.0 collective-permute-done.3.refs_3_
  304.0 0.7 collective-permute-start.21
  304.7 18.9 %collective-permute-done.1.refs_1_ = bf16[32,6144]{1,0:T(8,128)(2,1)S(1)} collective-permute-done((bf16[32,6144]{1,0:T(8,128)(2,1)}, bf16[32,6144]{1,0:T(8,128)(2,1)S(1)}, u32[]{:S(2)}, u32[]{:S(2)}) %collective-permute-start.1) | collective-permute-done | bytes 393248 | tf_op jit(solution)/shard_map/ppermute | solution.py:1043
  323.7 0.7 collective-permute-start.22
  324.4 0.0 collective-permute-done.2.refs_2_
  324.4 2.7 collective-permute-start.10
  327.1 0.0 collective-permute-done.15.refs_0_
  327.1 0.0 collective-permute-start.8
  327.1 0.0 collective-permute-done.17.refs_3_
  327.2 0.6 collective-permute-start.9
  327.8 6.3 %collective-permute-done.21.refs_1_ = bf16[128,2048]{1,0:T(8,128)(2,1)S(1)} collective-permute-done((bf16[128,2048]{1,0:T(8,128)(2,1)}, bf16[128,2048]{1,0:T(8,128)(2,1)S(1)}, u32[]{:S(2)}, u32[]{:S(2)}) %collective-permute-start.21) | collective-permute-done | bytes 524320 | tf_op jit(solution)/shard_map/ppermute | solution.py:1043
  334.1 0.0 collective-permute-start.4
  334.1 2.1 collective-permute-done.22.refs_2_
  336.1 0.0 collective-permute-start.7
  336.1 11.5 %collective-permute-done.10.refs_2_ = bf16[128,2048]{1,0:T(8,128)(2,1)S(1)} collective-permute-done((bf16[128,2048]{1,0:T(8,128)(2,1)}, bf16[128,2048]{1,0:T(8,128)(2,1)S(1)}, u32[]{:S(2)}, u32[]{:S(2)}) %collective-permute-start.10) | collective-permute-done | bytes 524320 | tf_op jit(solution)/shard_map/ppermute | solution.py:1135
  347.7 0.0 collective-permute-start.5
  347.7 3.8 collective-permute-done.8.refs_0_
  351.4 0.0 collective-permute-start.6
  351.4 18.8 %collective-permute-done.9.refs_1_ = bf16[128,2048]{1,0:T(8,128)(2,1)S(1)} collective-permute-done((bf16[128,2048]{1,0:T(8,128)(2,1)}, bf16[128,2048]{1,0:T(8,128)(2,1)S(1)}, u32[]{:S(2)}, u32[]{:S(2)}) %collective-permute-start.9) | collective-permute-done | bytes 524320 | tf_op jit(solution)/shard_map/ppermute | solution.py:1135
  370.3 1.5 collective-permute-start.11
  371.8 0.0 collective-permute-done.4.refs_4_
  371.8 0.5 collective-permute-start.12
  372.3 0.0 collective-permute-done.7.refs_7_
  372.3 0.1 collective-permute-start.23
  372.4 0.0 collective-permute-done.5.refs_5_
  372.5 1.3 collective-permute-start.16
  373.8 0.0 collective-permute-done.6.refs_6_
  373.8 0.8 collective-permute-start.18
  374.6 7.0 %collective-permute-done.11.refs_0_ = bf16[32,6144]{1,0:T(8,128)(2,1)S(1)} collective-permute-done((bf16[32,6144]{1,0:T(8,128)(2,1)S(1)}, bf16[32,6144]{1,0:T(8,128)(2,1)S(1)}, u32[]{:S(2)}, u32[]{:S(2)}) %collective-permute-start.11) | collective-permute-done | bytes 393248 | tf_op jit(solution)/shard_map/ppermute | solution.py:1043
  381.6 0.0 collective-permute-start.26
  381.6 1.5 collective-permute-done.12.refs_1_
  383.1 0.0 collective-permute-start.24
  383.1 0.0 collective-permute-done.23.refs_4_
  383.1 0.5 collective-permute-start.25
  383.6 6.2 %collective-permute-done.16.refs_0_ = bf16[128,2048]{1,0:T(8,128)(2,1)S(1)} collective-permute-done((bf16[128,2048]{1,0:T(8,128)(2,1)S(1)}, bf16[128,2048]{1,0:T(8,128)(2,1)S(1)}, u32[]{:S(2)}, u32[]{:S(2)}) %collective-permute-start.16) | collective-permute-done | bytes 524320 | tf_op jit(solution)/shard_map/ppermute | solution.py:1043
  389.8 1.2 collective-permute-done.18.refs_1_
  391.1 0.5 collective-permute-start.13
  391.6 0.1 collective-permute-start.14
  391.8 0.2 copy-done.7
  391.9 0.5 copy-done.8
  392.5 9.5 %widen.3 = f32[512,8192]{1,0:T(8,128)} custom-call(bf16[512,8192]{1,0:T(8,128)(2,1)} %get-tuple-element.81.in_ref), custom_call_target="tpu_custom_call" | custom-call | bytes 25165824 | tf_op jit(solution)/shard_map/widen/pallas_call | solution.py:47
  402.0 3.4 widen.2
  405.4 0.7 stack.131.rows_ref
  406.1 3.6 place.9.refs_8_
  409.7 3.1 place.6.refs_8_
  412.8 4.6 %place.7.refs_4_ = f32[512,6144]{1,0:T(8,128)} custom-call(s32[32]{0:T(128)} %stack.131.rows_ref, bf16[32,6144]{1,0:T(8,128)(2,1)} %copy-done.13, bf16[32,6144]{1,0:T(8,128)(2,1)} %copy-done.15, bf16[32,6144]{1,0:T(8,128)(2,1)} %copy-done.16, bf16[32,6144]{1,0:T(8,128)(2,1)} %copy-done.14, ...), custom_call_target="tpu_custom_call", output_to_operand_aliasing={{}: (9, {})} | custom-call | bytes 9437184 | tf_op jit(solution)/shard_map/place/pallas_call | solution.py:75
  417.5 4.2 finish.1
  421.7 5.6 %place.10.refs_4_ = f32[2048,2048]{1,0:T(8,128)} custom-call(s32[32]{0:T(128)} %stack.131.rows_ref, bf16[128,2048]{1,0:T(8,128)(2,1)} %copy-done, bf16[128,2048]{1,0:T(8,128)(2,1)} %copy-done.2, bf16[128,2048]{1,0:T(8,128)(2,1)} %copy-done.3, bf16[128,2048]{1,0:T(8,128)(2,1)} %copy-done.1, ...), custom_call_target="tpu_custom_call", output_to_operand_aliasing={{}: (9, {})} | custom-call | bytes 12582912 | tf_op jit(solution)/shard_map/place/pallas_call | solution.py:75
  427.3 0.0 collective-permute-done.13.refs_2_
  427.4 0.0 collective-permute-done.14.refs_3_
  427.4 3.1 place.8
  430.5 0.0 collective-permute-done.19.refs_2_
  430.5 3.6 place.11
  (48 shorter events, 0.1 us)
Async XLA Ops:
  290.4 12.3 %collective-permute-start = (bf16[32,6144]{1,0:T(8,128)(2,1)}, bf16[32,6144]{1,0:T(8,128)(2,1)S(1)}, u32[]{:S(2)}, u32[]{:S(2)}) collective-permute-start(bf16[32,6144]{1,0:T(8,128)(2,1)} %get-tuple-element.65.refs_0_), channel_id=1, source_target_pairs={{0,2},{1,3},{2,0},{3,1},{4,6},{5,7},{6,4},{7,5},{8,10},{9,11},{10,... | collective-permute-start | bytes 1179656 | tf_op jit(solution)/shard_map/ppermute | solution.py:1043
  291.8 12.2 %collective-permute-start.3 = (bf16[32,6144]{1,0:T(8,128)(2,1)}, bf16[32,6144]{1,0:T(8,128)(2,1)S(1)}, u32[]{:S(2)}, u32[]{:S(2)}) collective-permute-start(bf16[32,6144]{1,0:T(8,128)(2,1)} %get-tuple-element.66.refs_1_), channel_id=1, source_target_pairs={{0,4},{1,5},{2,6},{3,7},{4,0},{5,1},{6,2},{7,3},{8,12},{9,13},{10,... | collective-permute-start | bytes 1179656 | tf_op jit(solution)/shard_map/ppermute | solution.py:1043
  292.5 34.6 %collective-permute-start.15 = (bf16[128,2048]{1,0:T(8,128)(2,1)}, bf16[128,2048]{1,0:T(8,128)(2,1)S(1)}, u32[]{:S(2)}, u32[]{:S(2)}) collective-permute-start(bf16[128,2048]{1,0:T(8,128)(2,1)} %get-tuple-element.83.refs_0_), channel_id=1, source_target_pairs={{0,2},{1,3},{2,0},{3,1},{4,6},{5,7},{6,4},{7,5},{8,10},{9,11},{10,... | collective-permute-start | bytes 1572872 | tf_op jit(solution)/shard_map/ppermute | solution.py:1043
  294.0 33.1 %collective-permute-start.17 = (bf16[128,2048]{1,0:T(8,128)(2,1)}, bf16[128,2048]{1,0:T(8,128)(2,1)S(1)}, u32[]{:S(2)}, u32[]{:S(2)}) collective-permute-start(bf16[128,2048]{1,0:T(8,128)(2,1)} %get-tuple-element.84.refs_1_), channel_id=1, source_target_pairs={{0,4},{1,5},{2,6},{3,7},{4,0},{5,1},{6,2},{7,3},{8,12},{9,13},{10,... | collective-permute-start | bytes 1572872 | tf_op jit(solution)/shard_map/ppermute | solution.py:1043
  294.5 29.1 %collective-permute-start.1 = (bf16[32,6144]{1,0:T(8,128)(2,1)}, bf16[32,6144]{1,0:T(8,128)(2,1)S(1)}, u32[]{:S(2)}, u32[]{:S(2)}) collective-permute-start(bf16[32,6144]{1,0:T(8,128)(2,1)} %get-tuple-element.65.refs_0_), channel_id=1, source_target_pairs={{0,4},{1,5},{2,6},{3,7},{4,0},{5,1},{6,2},{7,3},{8,12},{9,13},{10,... | collective-permute-start | bytes 1179656 | tf_op jit(solution)/shard_map/ppermute | solution.py:1043
  302.7 89.1 %copy-start.13 = (bf16[32,6144]{1,0:T(8,128)(2,1)}, bf16[32,6144]{1,0:T(8,128)(2,1)S(1)}, u32[]{:S(2)}) copy-start(bf16[32,6144]{1,0:T(8,128)(2,1)S(1)} %collective-permute-done.refs_0_) | copy-start | bytes 1179652
  302.7 21.7 %collective-permute-start.2 = (bf16[32,6144]{1,0:T(8,128)(2,1)}, bf16[32,6144]{1,0:T(8,128)(2,1)S(1)}, u32[]{:S(2)}, u32[]{:S(2)}) collective-permute-start(bf16[32,6144]{1,0:T(8,128)(2,1)} %get-tuple-element.66.refs_1_), channel_id=1, source_target_pairs={{0,2},{1,3},{2,0},{3,1},{4,6},{5,7},{6,4},{7,5},{8,10},{9,11},{10,... | collective-permute-start | bytes 1179656 | tf_op jit(solution)/shard_map/ppermute | solution.py:1043
  304.0 87.7 %copy-start.14 = (bf16[32,6144]{1,0:T(8,128)(2,1)}, bf16[32,6144]{1,0:T(8,128)(2,1)S(1)}, u32[]{:S(2)}) copy-start(bf16[32,6144]{1,0:T(8,128)(2,1)S(1)} %collective-permute-done.3.refs_3_) | copy-start | bytes 1179652
  304.0 30.0 %collective-permute-start.21 = (bf16[128,2048]{1,0:T(8,128)(2,1)}, bf16[128,2048]{1,0:T(8,128)(2,1)S(1)}, u32[]{:S(2)}, u32[]{:S(2)}) collective-permute-start(bf16[128,2048]{1,0:T(8,128)(2,1)} %get-tuple-element.83.refs_0_), channel_id=1, source_target_pairs={{0,4},{1,5},{2,6},{3,7},{4,0},{5,1},{6,2},{7,3},{8,12},{9,13},{10,... | collective-permute-start | bytes 1572872 | tf_op jit(solution)/shard_map/ppermute | solution.py:1043
  323.7 48.8 %copy-start.15 = (bf16[32,6144]{1,0:T(8,128)(2,1)}, bf16[32,6144]{1,0:T(8,128)(2,1)S(1)}, u32[]{:S(2)}) copy-start(bf16[32,6144]{1,0:T(8,128)(2,1)S(1)} %collective-permute-done.1.refs_1_) | copy-start | bytes 1179652
  323.7 12.4 %collective-permute-start.22 = (bf16[128,2048]{1,0:T(8,128)(2,1)}, bf16[128,2048]{1,0:T(8,128)(2,1)S(1)}, u32[]{:S(2)}, u32[]{:S(2)}) collective-permute-start(bf16[128,2048]{1,0:T(8,128)(2,1)} %get-tuple-element.84.refs_1_), channel_id=1, source_target_pairs={{0,2},{1,3},{2,0},{3,1},{4,6},{5,7},{6,4},{7,5},{8,10},{9,11},{10,... | collective-permute-start | bytes 1572872 | tf_op jit(solution)/shard_map/ppermute | solution.py:1043
  324.4 49.4 %copy-start.16 = (bf16[32,6144]{1,0:T(8,128)(2,1)}, bf16[32,6144]{1,0:T(8,128)(2,1)S(1)}, u32[]{:S(2)}) copy-start(bf16[32,6144]{1,0:T(8,128)(2,1)S(1)} %collective-permute-done.2.refs_2_) | copy-start | bytes 1179652
  324.4 23.3 %collective-permute-start.10 = (bf16[128,2048]{1,0:T(8,128)(2,1)}, bf16[128,2048]{1,0:T(8,128)(2,1)S(1)}, u32[]{:S(2)}, u32[]{:S(2)}) collective-permute-start(bf16[128,2048]{1,0:T(8,128)(2,1)} %get-tuple-element.74), channel_id=1, source_target_pairs={{0,24},{8,0},{16,8},{24,16},{1,25},{9,1},{17,9},{25,17},{2,26},{10... | collective-permute-start | bytes 1572872 | tf_op jit(solution)/shard_map/ppermute | solution.py:1135
  327.1 65.3 %copy-start = (bf16[128,2048]{1,0:T(8,128)(2,1)}, bf16[128,2048]{1,0:T(8,128)(2,1)S(1)}, u32[]{:S(2)}) copy-start(bf16[128,2048]{1,0:T(8,128)(2,1)S(1)} %collective-permute-done.15.refs_0_) | copy-start | bytes 1572868
  327.1 24.3 %collective-permute-start.8 = (bf16[128,2048]{1,0:T(8,128)(2,1)}, bf16[128,2048]{1,0:T(8,128)(2,1)S(1)}, u32[]{:S(2)}, u32[]{:S(2)}) collective-permute-start(bf16[128,2048]{1,0:T(8,128)(2,1)} %get-tuple-element.72), channel_id=1, source_target_pairs={{0,8},{8,16},{16,24},{24,0},{1,9},{9,17},{17,25},{25,1},{2,10},{10... | collective-permute-start | bytes 1572872 | tf_op jit(solution)/shard_map/ppermute | solution.py:1135
  327.1 65.2 %copy-start.1 = (bf16[128,2048]{1,0:T(8,128)(2,1)}, bf16[128,2048]{1,0:T(8,128)(2,1)S(1)}, u32[]{:S(2)}) copy-start(bf16[128,2048]{1,0:T(8,128)(2,1)S(1)} %collective-permute-done.17.refs_3_) | copy-start | bytes 1572868
  327.2 43.1 %collective-permute-start.9 = (bf16[128,2048]{1,0:T(8,128)(2,1)}, bf16[128,2048]{1,0:T(8,128)(2,1)S(1)}, u32[]{:S(2)}, u32[]{:S(2)}) collective-permute-start(bf16[128,2048]{1,0:T(8,128)(2,1)} %get-tuple-element.73), channel_id=1, source_target_pairs={{0,16},{8,24},{16,0},{24,8},{1,17},{9,25},{17,1},{25,9},{2,18},{10... | collective-permute-start | bytes 1572872 | tf_op jit(solution)/shard_map/ppermute | solution.py:1135
  334.1 58.3 %copy-start.2 = (bf16[128,2048]{1,0:T(8,128)(2,1)}, bf16[128,2048]{1,0:T(8,128)(2,1)S(1)}, u32[]{:S(2)}) copy-start(bf16[128,2048]{1,0:T(8,128)(2,1)S(1)} %collective-permute-done.21.refs_1_) | copy-start | bytes 1572868
  334.1 37.7 %collective-permute-start.4 = (bf16[32,6144]{1,0:T(8,128)(2,1)S(1)}, bf16[32,6144]{1,0:T(8,128)(2,1)S(1)}, u32[]{:S(2)}, u32[]{:S(2)}) collective-permute-start(bf16[32,6144]{1,0:T(8,128)(2,1)S(1)} %collective-permute-done.refs_0_), channel_id=1, source_target_pairs={{0,1},{1,0},{2,3},{3,2},{4,5},{5,4},{6,7},{7,6},{8,9},{9,8},{10,11... | collective-permute-start | bytes 1179656 | tf_op jit(solution)/shard_map/ppermute | solution.py:1043
  336.1 56.3 %copy-start.3 = (bf16[128,2048]{1,0:T(8,128)(2,1)}, bf16[128,2048]{1,0:T(8,128)(2,1)S(1)}, u32[]{:S(2)}) copy-start(bf16[128,2048]{1,0:T(8,128)(2,1)S(1)} %collective-permute-done.22.refs_2_) | copy-start | bytes 1572868
  336.1 36.2 %collective-permute-start.7 = (bf16[32,6144]{1,0:T(8,128)(2,1)S(1)}, bf16[32,6144]{1,0:T(8,128)(2,1)S(1)}, u32[]{:S(2)}, u32[]{:S(2)}) collective-permute-start(bf16[32,6144]{1,0:T(8,128)(2,1)S(1)} %collective-permute-done.3.refs_3_), channel_id=1, source_target_pairs={{0,1},{1,0},{2,3},{3,2},{4,5},{5,4},{6,7},{7,6},{8,9},{9,8},{10,11... | collective-permute-start | bytes 1179656 | tf_op jit(solution)/shard_map/ppermute | solution.py:1043
  347.7 24.7 %copy-start.9 = (bf16[128,2048]{1,0:T(8,128)(2,1)}, bf16[128,2048]{1,0:T(8,128)(2,1)S(1)}, u32[]{:S(2)}) copy-start(bf16[128,2048]{1,0:T(8,128)(2,1)S(1)} %collective-permute-done.10.refs_2_) | copy-start | bytes 1572868
  347.7 24.8 %collective-permute-start.5 = (bf16[32,6144]{1,0:T(8,128)(2,1)S(1)}, bf16[32,6144]{1,0:T(8,128)(2,1)S(1)}, u32[]{:S(2)}, u32[]{:S(2)}) collective-permute-start(bf16[32,6144]{1,0:T(8,128)(2,1)S(1)} %collective-permute-done.1.refs_1_), channel_id=1, source_target_pairs={{0,1},{1,0},{2,3},{3,2},{4,5},{5,4},{6,7},{7,6},{8,9},{9,8},{10,11... | collective-permute-start | bytes 1179656 | tf_op jit(solution)/shard_map/ppermute | solution.py:1043
  351.4 23.2 %copy-start.10 = (bf16[128,2048]{1,0:T(8,128)(2,1)}, bf16[128,2048]{1,0:T(8,128)(2,1)S(1)}, u32[]{:S(2)}) copy-start(bf16[128,2048]{1,0:T(8,128)(2,1)S(1)} %collective-permute-done.8.refs_0_) | copy-start | bytes 1572868
  351.4 22.4 %collective-permute-start.6 = (bf16[32,6144]{1,0:T(8,128)(2,1)S(1)}, bf16[32,6144]{1,0:T(8,128)(2,1)S(1)}, u32[]{:S(2)}, u32[]{:S(2)}) collective-permute-start(bf16[32,6144]{1,0:T(8,128)(2,1)S(1)} %collective-permute-done.2.refs_2_), channel_id=1, source_target_pairs={{0,1},{1,0},{2,3},{3,2},{4,5},{5,4},{6,7},{7,6},{8,9},{9,8},{10,11... | collective-permute-start | bytes 1179656 | tf_op jit(solution)/shard_map/ppermute | solution.py:1043
  370.3 11.3 %copy-start.11 = (bf16[128,2048]{1,0:T(8,128)(2,1)}, bf16[128,2048]{1,0:T(8,128)(2,1)S(1)}, u32[]{:S(2)}) copy-start(bf16[128,2048]{1,0:T(8,128)(2,1)S(1)} %collective-permute-done.9.refs_1_) | copy-start | bytes 1572868
  370.3 11.3 %collective-permute-start.11 = (bf16[32,6144]{1,0:T(8,128)(2,1)S(1)}, bf16[32,6144]{1,0:T(8,128)(2,1)S(1)}, u32[]{:S(2)}, u32[]{:S(2)}) collective-permute-start(bf16[32,6144]{1,0:T(8,128)(2,1)S(1)} %collective-permute-done.refs_0_), channel_id=1, source_target_pairs={{0,4},{1,5},{2,6},{3,7},{4,0},{5,1},{6,2},{7,3},{8,12},{9,13},{10,... | collective-permute-start | bytes 1179656 | tf_op jit(solution)/shard_map/ppermute | solution.py:1043
  371.8 19.9 %copy-start.17 = (bf16[32,6144]{1,0:T(8,128)(2,1)}, bf16[32,6144]{1,0:T(8,128)(2,1)S(1)}, u32[]{:S(2)}) copy-start(bf16[32,6144]{1,0:T(8,128)(2,1)S(1)} %collective-permute-done.4.refs_4_) | copy-start | bytes 1179652
  371.8 11.3 %collective-permute-start.12 = (bf16[32,6144]{1,0:T(8,128)(2,1)S(1)}, bf16[32,6144]{1,0:T(8,128)(2,1)}, u32[]{:S(2)}, u32[]{:S(2)}) collective-permute-start(bf16[32,6144]{1,0:T(8,128)(2,1)S(1)} %collective-permute-done.3.refs_3_), channel_id=1, source_target_pairs={{0,2},{1,3},{2,0},{3,1},{4,6},{5,7},{6,4},{7,5},{8,10},{9,11},{10,... | collective-permute-start | bytes 1179656 | tf_op jit(solution)/shard_map/ppermute | solution.py:1043
  372.3 19.4 %copy-start.18 = (bf16[32,6144]{1,0:T(8,128)(2,1)}, bf16[32,6144]{1,0:T(8,128)(2,1)S(1)}, u32[]{:S(2)}) copy-start(bf16[32,6144]{1,0:T(8,128)(2,1)S(1)} %collective-permute-done.7.refs_7_) | copy-start | bytes 1179652
  372.3 10.8 %collective-permute-start.23 = (bf16[128,2048]{1,0:T(8,128)(2,1)S(1)}, bf16[128,2048]{1,0:T(8,128)(2,1)S(1)}, u32[]{:S(2)}, u32[]{:S(2)}) collective-permute-start(bf16[128,2048]{1,0:T(8,128)(2,1)S(1)} %collective-permute-done.15.refs_0_), channel_id=1, source_target_pairs={{0,1},{1,0},{2,3},{3,2},{4,5},{5,4},{6,7},{7,6},{8,9},{9,8},{10,11... | collective-permute-start | bytes 1572872 | tf_op jit(solution)/shard_map/ppermute | solution.py:1043
  372.4 19.3 %copy-start.19 = (bf16[32,6144]{1,0:T(8,128)(2,1)}, bf16[32,6144]{1,0:T(8,128)(2,1)S(1)}, u32[]{:S(2)}) copy-start(bf16[32,6144]{1,0:T(8,128)(2,1)S(1)} %collective-permute-done.5.refs_5_) | copy-start | bytes 1179652
  372.5 17.4 %collective-permute-start.16 = (bf16[128,2048]{1,0:T(8,128)(2,1)S(1)}, bf16[128,2048]{1,0:T(8,128)(2,1)S(1)}, u32[]{:S(2)}, u32[]{:S(2)}) collective-permute-start(bf16[128,2048]{1,0:T(8,128)(2,1)S(1)} %collective-permute-done.15.refs_0_), channel_id=1, source_target_pairs={{0,4},{1,5},{2,6},{3,7},{4,0},{5,1},{6,2},{7,3},{8,12},{9,13},{10,... | collective-permute-start | bytes 1572872 | tf_op jit(solution)/shard_map/ppermute | solution.py:1043
  373.8 18.0 %copy-start.20 = (bf16[32,6144]{1,0:T(8,128)(2,1)}, bf16[32,6144]{1,0:T(8,128)(2,1)S(1)}, u32[]{:S(2)}) copy-start(bf16[32,6144]{1,0:T(8,128)(2,1)S(1)} %collective-permute-done.6.refs_6_) | copy-start | bytes 1179652
  373.8 17.3 %collective-permute-start.18 = (bf16[128,2048]{1,0:T(8,128)(2,1)S(1)}, bf16[128,2048]{1,0:T(8,128)(2,1)S(1)}, u32[]{:S(2)}, u32[]{:S(2)}) collective-permute-start(bf16[128,2048]{1,0:T(8,128)(2,1)S(1)} %collective-permute-done.17.refs_3_), channel_id=1, source_target_pairs={{0,2},{1,3},{2,0},{3,1},{4,6},{5,7},{6,4},{7,5},{8,10},{9,11},{10,... | collective-permute-start | bytes 1572872 | tf_op jit(solution)/shard_map/ppermute | solution.py:1043
  381.6 20.4 %copy-start.12 = (bf16[32,6144]{1,0:T(8,128)(2,1)}, bf16[32,6144]{1,0:T(8,128)(2,1)S(1)}, u32[]{:S(2)}) copy-start(bf16[32,6144]{1,0:T(8,128)(2,1)S(1)} %collective-permute-done.11.refs_0_) | copy-start | bytes 1179652
  381.6 9.5 %collective-permute-start.26 = (bf16[128,2048]{1,0:T(8,128)(2,1)S(1)}, bf16[128,2048]{1,0:T(8,128)(2,1)S(1)}, u32[]{:S(2)}, u32[]{:S(2)}) collective-permute-start(bf16[128,2048]{1,0:T(8,128)(2,1)S(1)} %collective-permute-done.17.refs_3_), channel_id=1, source_target_pairs={{0,1},{1,0},{2,3},{3,2},{4,5},{5,4},{6,7},{7,6},{8,9},{9,8},{10,11... | collective-permute-start | bytes 1572872 | tf_op jit(solution)/shard_map/ppermute | solution.py:1043
  383.1 8.5 %collective-permute-start.24 = (bf16[128,2048]{1,0:T(8,128)(2,1)S(1)}, bf16[128,2048]{1,0:T(8,128)(2,1)S(1)}, u32[]{:S(2)}, u32[]{:S(2)}) collective-permute-start(bf16[128,2048]{1,0:T(8,128)(2,1)S(1)} %collective-permute-done.21.refs_1_), channel_id=1, source_target_pairs={{0,1},{1,0},{2,3},{3,2},{4,5},{5,4},{6,7},{7,6},{8,9},{9,8},{10,11... | collective-permute-start | bytes 1572872 | tf_op jit(solution)/shard_map/ppermute | solution.py:1043
  383.1 8.5 %copy-start.6 = (bf16[128,2048]{1,0:T(8,128)(2,1)}, bf16[128,2048]{1,0:T(8,128)(2,1)S(1)}, u32[]{:S(2)}) copy-start(bf16[128,2048]{1,0:T(8,128)(2,1)S(1)} %collective-permute-done.23.refs_4_) | copy-start | bytes 1572868
  383.1 38.6 %collective-permute-start.25 = (bf16[128,2048]{1,0:T(8,128)(2,1)S(1)}, bf16[128,2048]{1,0:T(8,128)(2,1)}, u32[]{:S(2)}, u32[]{:S(2)}) collective-permute-start(bf16[128,2048]{1,0:T(8,128)(2,1)S(1)} %collective-permute-done.22.refs_2_), channel_id=1, source_target_pairs={{0,1},{1,0},{2,3},{3,2},{4,5},{5,4},{6,7},{7,6},{8,9},{9,8},{10,11... | collective-permute-start | bytes 1572872 | tf_op jit(solution)/shard_map/ppermute | solution.py:1043
  389.8 2.6 copy-start.4
  389.8 40.6 %collective-permute-start.19 = (bf16[128,2048]{1,0:T(8,128)(2,1)S(1)}, bf16[128,2048]{1,0:T(8,128)(2,1)}, u32[]{:S(2)}, u32[]{:S(2)}) collective-permute-start(bf16[128,2048]{1,0:T(8,128)(2,1)S(1)} %collective-permute-done.16.refs_0_), channel_id=1, source_target_pairs={{0,1},{1,0},{2,3},{3,2},{4,5},{5,4},{6,7},{7,6},{8,9},{9,8},{10,11... | collective-permute-start | bytes 1572872 | tf_op jit(solution)/shard_map/ppermute | solution.py:1043
  391.1 1.4 copy-start.5
  391.1 39.4 %collective-permute-start.20 = (bf16[128,2048]{1,0:T(8,128)(2,1)S(1)}, bf16[128,2048]{1,0:T(8,128)(2,1)}, u32[]{:S(2)}, u32[]{:S(2)}) collective-permute-start(bf16[128,2048]{1,0:T(8,128)(2,1)S(1)} %collective-permute-done.18.refs_1_), channel_id=1, source_target_pairs={{0,1},{1,0},{2,3},{3,2},{4,5},{5,4},{6,7},{7,6},{8,9},{9,8},{10,11... | collective-permute-start | bytes 1572872 | tf_op jit(solution)/shard_map/ppermute | solution.py:1043
  391.1 0.9 copy-start.7
  391.1 36.3 %collective-permute-start.13 = (bf16[32,6144]{1,0:T(8,128)(2,1)S(1)}, bf16[32,6144]{1,0:T(8,128)(2,1)}, u32[]{:S(2)}, u32[]{:S(2)}) collective-permute-start(bf16[32,6144]{1,0:T(8,128)(2,1)S(1)} %collective-permute-done.11.refs_0_), channel_id=1, source_target_pairs={{0,1},{1,0},{2,3},{3,2},{4,5},{5,4},{6,7},{7,6},{8,9},{9,8},{10,11... | collective-permute-start | bytes 1179656 | tf_op jit(solution)/shard_map/ppermute | solution.py:1043
  391.6 0.8 copy-start.8
  391.6 35.8 %collective-permute-start.14 = (bf16[32,6144]{1,0:T(8,128)(2,1)}, bf16[32,6144]{1,0:T(8,128)(2,1)}, u32[]{:S(2)}, u32[]{:S(2)}) collective-permute-start(bf16[32,6144]{1,0:T(8,128)(2,1)} %collective-permute-done.12.refs_1_), channel_id=1, source_target_pairs={{0,1},{1,0},{2,3},{3,2},{4,5},{5,4},{6,7},{7,6},{8,9},{9,8},{10,11... | collective-permute-start | bytes 1179656 | tf_op jit(solution)/shard_map/ppermute | solution.py:1043
